TPU v7x, 16 devices: a whole 2x2x2 slice. The times are simulated.
16 devices in a mesh: dp: 4 (over z, y), pp: 4 (over x, core).
Axes of the slice: x: 2, y: 2, z: 2, core: 2. Of those that a mesh axis runs over, the one named last changes fastest.
Arguments:
- tokens: int32 [2, 32, 34], P(None, 'dp')
- emb_s: float32 [4, 32128, 1024], P('pp', 'dp')
- w_up: bfloat16 [4, 1, 1024, 4096], P('pp')
- w_down: bfloat16 [4, 1, 4096, 1024], P('pp')
- gain_f: bfloat16 [1024], replicated
- gain_h: bfloat16 [1024], replicated
- gain_e: bfloat16 [1024], replicated
- gain_m: bfloat16 [1024], replicated
- w_proj: bfloat16 [2048, 1024], replicated
- u_up: bfloat16 [1024, 4096], replicated
- u_down: bfloat16 [4096, 1024], replicated
Outputs:
- output 1: float32 [], replicated
- output 2: float32 [4, 32128, 1024], P('pp', 'dp')
- output 3: float32 [4, 1, 1024, 4096], P('pp')
- output 4: float32 [4, 1, 4096, 1024], P('pp')
All inputs are finite; a program needn't handle non-finite values.
Results may differ from a plain program's by a relative error of at most 0.0185332.
Values are sent between devices in bfloat16 or wider.
A program may use at most 1 GiB of HBM per device.

v0:
```python
import math
import jax
import jax.numpy as jnp
from jax import lax
from jax.sharding import PartitionSpec as P

MTP_WEIGHT = 0.3
EPS = 1e-6


def norm_only(acts):
    acts_f = acts.astype(jnp.float32)
    return acts_f * lax.rsqrt(jnp.mean(acts_f * acts_f, axis=-1, keepdims=True) + EPS)


def norm_bf16(acts):
    return norm_only(acts).astype(jnp.bfloat16)


def gain_norm(acts, gain):
    return (norm_only(acts) * gain.astype(jnp.float32)).astype(jnp.bfloat16)


def gelu_bf16(pre_act):
    return jax.nn.gelu(pre_act).astype(jnp.bfloat16)


def lookup_rows(emb_table, tok_ids, emb_scale):
    return (jnp.take(emb_table, tok_ids, axis=0).astype(jnp.float32) * emb_scale).astype(jnp.bfloat16)


def cross_sum(normed, emb_table, targets):
    logits = jnp.einsum('...h,vh->...v', normed, emb_table, preferred_element_type=jnp.float32)
    row_max = lax.stop_gradient(jnp.max(logits, axis=-1, keepdims=True))
    log_norm = jnp.log(jnp.sum(jnp.exp(logits - row_max), axis=-1)) + row_max[..., 0]
    picked = jnp.take_along_axis(logits, targets[..., None], axis=-1)[..., 0]
    return jnp.sum(log_norm - picked)


def head_terms(hid_rows, mtp_rows, emb_table, mid_tok, next_tok, weights, loss_scale):
    gain_f, gain_h, gain_e, gain_m, w_proj, u_up, u_down = weights
    main_sum = cross_sum(gain_norm(hid_rows, gain_f), emb_table, mid_tok)
    joined = jnp.concatenate([gain_norm(hid_rows, gain_h), gain_norm(mtp_rows, gain_e)], axis=-1)
    mtp_state = jnp.dot(joined, w_proj, preferred_element_type=jnp.float32).astype(jnp.bfloat16)
    mtp_inner = jax.nn.gelu(jnp.dot(gain_norm(mtp_state, gain_m), u_up, preferred_element_type=jnp.float32)).astype(jnp.bfloat16)
    mtp_state = (mtp_state.astype(jnp.float32) + jnp.dot(mtp_inner, u_down, preferred_element_type=jnp.float32)).astype(jnp.bfloat16)
    next_sum = cross_sum(gain_norm(mtp_state, gain_f), emb_table, next_tok)
    return (main_sum + MTP_WEIGHT * next_sum) * loss_scale


def layer_fwd(acts, w_in, w_out):
    normed, norm_back = jax.vjp(norm_bf16, acts)
    pre_act = jnp.dot(normed, w_in, preferred_element_type=jnp.float32)
    act_out, gelu_back = jax.vjp(gelu_bf16, pre_act)
    layer_out = (acts.astype(jnp.float32) + jnp.dot(act_out, w_out, preferred_element_type=jnp.float32)).astype(jnp.bfloat16)
    return layer_out, (normed, act_out, norm_back, gelu_back)


def layer_bwd(saved, w_in, w_out, d_out):
    normed, act_out, norm_back, gelu_back = saved
    g_out = jnp.einsum('tf,th->fh', act_out, d_out, preferred_element_type=jnp.float32)
    d_act = jnp.einsum('th,fh->tf', d_out, w_out, preferred_element_type=jnp.float32).astype(jnp.bfloat16)
    d_pre = gelu_back(d_act)[0].astype(jnp.bfloat16)
    g_in = jnp.einsum('th,tf->hf', normed, d_pre, preferred_element_type=jnp.float32)
    d_norm = jnp.einsum('tf,hf->th', d_pre, w_in, preferred_element_type=jnp.float32).astype(jnp.bfloat16)
    d_acts = (d_out.astype(jnp.float32) + norm_back(d_norm)[0].astype(jnp.float32)).astype(jnp.bfloat16)
    return d_acts, g_in, g_out


def stage_fwd(acts, w_in, w_out):
    for layer in range(w_in.shape[0]):
        acts = layer_fwd(acts, w_in[layer], w_out[layer])[0]
    return acts


def stage_bwd(acts, w_in, w_out, d_acts):
    saved_list = []
    for layer in range(w_in.shape[0]):
        acts, saved = layer_fwd(acts, w_in[layer], w_out[layer])
        saved_list.append(saved)
    in_grads = []
    out_grads = []
    for layer in reversed(range(w_in.shape[0])):
        d_acts, g_in, g_out = layer_bwd(saved_list[layer], w_in[layer], w_out[layer], d_acts)
        in_grads.append(g_in)
        out_grads.append(g_out)
    return d_acts, jnp.stack(in_grads[::-1]), jnp.stack(out_grads[::-1])


def solution(mesh):
    n_stages = mesh.shape['pp']
    n_data = mesh.shape['dp']
    fwd_perm = [(stage_idx, stage_idx + 1) for stage_idx in range(n_stages - 1)]
    bwd_perm = [(stage_idx + 1, stage_idx) for stage_idx in range(n_stages - 1)]
    to_first = [(n_stages - 1, 0)]
    to_last = [(0, n_stages - 1)]

    def device_step(tokens, emb_s, w_up, w_down, gain_f, gain_h, gain_e, gain_m, w_proj, u_up, u_down):
        weights = (gain_f, gain_h, gain_e, gain_m, w_proj, u_up, u_down)
        stage = lax.axis_index('pp')
        is_first = stage == 0
        is_last = stage == n_stages - 1
        n_micro, rows_dev, width = tokens.shape
        seq_len = width - 2
        n_tok = rows_dev * seq_len
        hidden = emb_s.shape[2]
        n_vocab = emb_s.shape[1] * n_data
        emb_scale = math.sqrt(hidden)
        loss_scale = 1.0 / (n_micro * rows_dev * n_data * seq_len)
        w_in = w_up[0]
        w_out = w_down[0]
        emb_table = lax.all_gather(emb_s[0].astype(jnp.bfloat16), 'dp', axis=0, tiled=True)
        in_ids = tokens[:, :, 0:seq_len].reshape(n_micro, n_tok)
        mid_ids = tokens[:, :, 1:seq_len + 1].reshape(n_micro, n_tok)
        out_ids = tokens[:, :, 2:seq_len + 2].reshape(n_micro, n_tok)
        n_ticks = n_micro + n_stages - 1
        act_zero = jnp.zeros((n_micro, n_tok, hidden), jnp.bfloat16)

        def fwd_tick(tick, carry):
            received, stage_in, stage_out = carry
            slot = tick - stage
            valid = (slot >= 0) & (slot < n_micro)
            slot_safe = jnp.clip(slot, 0, n_micro - 1)
            first_in = lookup_rows(emb_table, lax.dynamic_index_in_dim(in_ids, slot_safe, 0, keepdims=False), emb_scale)
            acts_in = jnp.where(is_first, first_in, received)
            acts_out = stage_fwd(acts_in, w_in, w_out)
            old_in = lax.dynamic_index_in_dim(stage_in, slot_safe, 0, keepdims=False)
            stage_in = lax.dynamic_update_index_in_dim(stage_in, jnp.where(valid, acts_in, old_in), slot_safe, 0)
            old_out = lax.dynamic_index_in_dim(stage_out, slot_safe, 0, keepdims=False)
            stage_out = lax.dynamic_update_index_in_dim(stage_out, jnp.where(valid, acts_out, old_out), slot_safe, 0)
            received = lax.ppermute(acts_out, 'pp', fwd_perm)
            return received, stage_in, stage_out

        fwd_start = (jnp.zeros((n_tok, hidden), jnp.bfloat16), act_zero, act_zero)
        _, stage_in, stage_out = lax.fori_loop(0, n_ticks, fwd_tick, fwd_start)
        head_in = lax.ppermute(stage_out, 'pp', to_first)

        def head_pass(hid_all):
            def head_step(g_table, scan_in):
                hid_rows, mid_tok, next_tok = scan_in
                mtp_rows = lookup_rows(emb_table, mid_tok, emb_scale)

                def local_loss(hid_in, rows_in, table_in):
                    return head_terms(hid_in, rows_in, table_in, mid_tok, next_tok, weights, loss_scale)

                value, head_back = jax.vjp(local_loss, hid_rows, mtp_rows, emb_table)
                d_hid, d_rows, d_table = head_back(jnp.ones((), jnp.float32))
                g_table = g_table + d_table.astype(jnp.float32) + jax.ops.segment_sum(d_rows.astype(jnp.float32) * emb_scale, mid_tok, num_segments=n_vocab)
                return g_table, (value, d_hid)

            g_table, (values, d_hid_all) = lax.scan(head_step, jnp.zeros((n_vocab, hidden), jnp.float32), (hid_all, mid_ids, out_ids))
            return g_table, jnp.sum(values), d_hid_all

        def head_skip(hid_all):
            return jnp.zeros((n_vocab, hidden), jnp.float32), jnp.zeros((), jnp.float32), jnp.zeros_like(hid_all)

        g_table, head_loss, d_hid_all = lax.cond(is_first, head_pass, head_skip, head_in)
        d_head = lax.ppermute(d_hid_all, 'pp', to_last)

        def bwd_tick(tick, carry):
            received, g_in, g_out, g_tab = carry
            slot = tick - (n_stages - 1 - stage)
            valid = (slot >= 0) & (slot < n_micro)
            slot_safe = jnp.clip(slot, 0, n_micro - 1)
            d_top = lax.dynamic_index_in_dim(d_head, slot_safe, 0, keepdims=False)
            d_out = jnp.where(is_last, d_top, received)
            acts_in = lax.dynamic_index_in_dim(stage_in, slot_safe, 0, keepdims=False)
            d_in, step_in, step_out = stage_bwd(acts_in, w_in, w_out, d_out)
            keep = valid.astype(jnp.float32)
            g_in = g_in + keep * step_in
            g_out = g_out + keep * step_out
            ids_now = lax.dynamic_index_in_dim(in_ids, slot_safe, 0, keepdims=False)

            def add_rows(g_acc):
                return g_acc + jax.ops.segment_sum(d_in.astype(jnp.float32) * emb_scale, ids_now, num_segments=n_vocab)

            g_tab = lax.cond(is_first & valid, add_rows, lambda g_acc: g_acc, g_tab)
            received = lax.ppermute(d_in, 'pp', bwd_perm)
            return received, g_in, g_out, g_tab

        bwd_start = (jnp.zeros((n_tok, hidden), jnp.bfloat16), jnp.zeros(w_in.shape, jnp.float32), jnp.zeros(w_out.shape, jnp.float32), g_table)
        _, g_in, g_out, g_table = lax.fori_loop(0, n_ticks, bwd_tick, bwd_start)
        g_shard = lax.psum_scatter(g_table, 'dp', scatter_dimension=0, tiled=True)
        g_in = lax.psum(g_in, 'dp')
        g_out = lax.psum(g_out, 'dp')
        loss = lax.psum(head_loss, ('dp', 'pp'))
        return loss, g_shard[None], g_in[None], g_out[None]

    return jax.shard_map(device_step, mesh=mesh, in_specs=(P(None, 'dp', None), P('pp', 'dp', None), P('pp'), P('pp'), P(), P(), P(), P(), P(), P(), P()), out_specs=(P(), P('pp', 'dp', None), P('pp'), P('pp')), check_vma=False)
```

profile of v0, /device:TPU:0, one launch (start us, length us, event | category | flops | bytes accessed | tf_op | source)
XLA Modules:
  0.0 3603.2 jit_solution(16970271017610928215)
XLA Ops:
  25.1 564.2 %all-gather.3.cloned.1.call-done = bf16[1,32128,1024]{2,1,0:T(8,128)(2,1)} async-done(((bf16[1,8032,1024]{2,1,0:T(8,128)(2,1)}), bf16[1,32128,1024]{2,1,0:T(8,128)(2,1)}) %all-gather.3.cloned.1.call-update) | async-done | bytes 65798160 | tf_op jit(solution)/shard_map/all_gather | solution.py:112
  590.6 130.3 %while.58 = (s32[]{:T(128)}, bf16[256,1024]{1,0:T(8,128)(2,1)S(1)}, bf16[2,256,1024]{2,1,0:T(8,128)(2,1)S(1)}, bf16[2,256,1024]{2,1,0:T(8,128)(2,1)}, pred[]{:T(...) while((s32[]{:T(128)}, bf16[256,1024]{1,0:T(8,128)(2,1)S(1)}, ...), condition=%wide.region_2.4_spmd, body=%wide.region_0.3_spmd.sunk | while | flops 4308602368 | bytes 27803632 | solution.py:135
  738.0 872.5 %conditional.2 = (f32[32128,1024]{1,0:T(8,128)}, f32[]{:T(128)}, bf16[2,256,1024]{2,1,0:T(8,128)(2,1)}) conditional(s32[]{:T(128)} %convert_element_type.470, () %tuple.83, (s32[2,8,34]{2,1,0:T(8,128)S(1)}, bf16[2,256,1024]{2,1,0:T(8,128)(2,1)}, bf16[1024]{0:T(1024)(128)(2,1)}, bf16[32128,1024]{1,0:T(8,128)(2,1)}, bf16[1024]{0:T(1024)(128)(2,1)}, ...), branch_computations={%region_3.5_spmd, %region_4.26_spmd} | conditional | flops 112216457216 | bytes 1225156992 | solution.py:157
  738.2 40.6 %broadcast.466 = f32[32128,1024]{1,0:T(8,128)} broadcast(f32[]{:T(128)} %constant.384.clone), dimensions={} | broadcast | bytes 131596288 | tf_op jit(solution)/shard_map/broadcast.53
  778.9 820.7 %while.57 = (s32[]{:T(128)}, f32[32128,1024]{1,0:T(8,128)}, f32[2]{0:T(128)}, bf16[2,256,1024]{2,1,0:T(8,128)(2,1)}, bf16[2,256,1024]{2,1,0:T(8,128)(2,1)S(1)}, ...) while((s32[]{:T(128)}, f32[32128,1024]{1,0:T(8,128)}, ...), condition=%wide.region_22.24_spmd, body=%wide.region_5.23_spmd.sunk | while | flops 112216457216 | bytes 1089316864 | solution.py:151
  795.4 35.7 fusion.359
  903.5 35.5 fusion.364
  956.8 36.1 %fusion.370 = (f32[256]{0:T(256)S(1)}, f32[256]{0:T(256)S(1)}, f32[256]{0:T(256)S(1)}, f32[256,1024]{1,0:T(8,128)S(1)}) fusion(f32[1024]{0:T(1024)S(1)} %copy-done.13, bf16[256,2048]{1,0:T(8,128)(2,1)} %convolution_convert_fusion.4, bf16[2,256,1024]{2,1,0:T(8,128)(2,1)S(1)} %get-tuple-element.1267, s32[]{:T(128)} %get-tuple-element.1245, ...), kind=kOutput, calls=%fused_computation.226.clone.1 | convolution fusion | flops 16890429440 | bytes 101861632 | tf_op jit(solution)/shard_map/cond/branch_1_fun/while/body/eval_jaxpr/transpose(jvp(...h,vh->...v))/dot_general | solution.py:33
  996.7 37.5 %fusion.363 = bf16[32128,1024]{1,0:T(8,128)(2,1)} fusion(f32[256,32128]{1,0:T(8,128)} %get-tuple-element.1205, f32[256]{0:T(256)S(1)} %get-tuple-element.1210, f32[256]{0:T(256)S(1)} %get-tuple-element.1209, s32[256]{0:T(256)S(1)} %bitcast.267, bf16[256,1024]{1,0:T(8,128)(2,1)S(1)} %get-tuple-element.1203, f32[1024]{0:T(1024)S(1)} %convert_element_type.940, ...), kind=kOutput, calls=%fused_computation.113.clone.3 | convolution fusion | flops 16886497280 | bytes 99229696 | tf_op jit(solution)/shard_map/cond/branch_1_fun/while/body/eval_jaxpr/transpose(jvp(...h,vh->...v))/dot_general | solution.py:33
  1034.3 117.3 %convert_add_fusion.4 = f32[32128,1024]{1,0:T(8,128)} fusion(f32[32128,1024]{1,0:T(8,128)} %get-tuple-element.1246, bf16[32128,1024]{1,0:T(8,128)(2,1)} %fusion.363, f32[256,32128]{1,0:T(8,128)} %get-tuple-element.1211, f32[256]{0:T(256)S(1)} %get-tuple-element.1214, f32[256]{0:T(256)S(1)} %get-tuple-element.1213, s32[256]{0:T(256)S(1)} %bitcast.261, ...), kind=kOutput, calls=%fused_computation.103.clone.3 | convolution fusion | flops 17018093568 | bytes 362422272 | tf_op jit(solution)/shard_map/cond/branch_1_fun/while/body/eval_jaxpr/transpose(jvp(...h,vh->...v))/dot_general | solution.py:33
  1151.6 35.3 scatter_fusion.1
  1205.1 35.8 fusion.359
  1313.4 35.5 fusion.364
  1366.6 36.3 %fusion.370 = (f32[256]{0:T(256)S(1)}, f32[256]{0:T(256)S(1)}, f32[256]{0:T(256)S(1)}, f32[256,1024]{1,0:T(8,128)S(1)}) fusion(f32[1024]{0:T(1024)S(1)} %copy-done.13, bf16[256,2048]{1,0:T(8,128)(2,1)} %convolution_convert_fusion.4, bf16[2,256,1024]{2,1,0:T(8,128)(2,1)S(1)} %get-tuple-element.1267, s32[]{:T(128)} %get-tuple-element.1245, ...), kind=kOutput, calls=%fused_computation.226.clone.1 | convolution fusion | flops 16890429440 | bytes 101861632 | tf_op jit(solution)/shard_map/cond/branch_1_fun/while/body/eval_jaxpr/transpose(jvp(...h,vh->...v))/dot_general | solution.py:33
  1406.7 37.5 %fusion.363 = bf16[32128,1024]{1,0:T(8,128)(2,1)} fusion(f32[256,32128]{1,0:T(8,128)} %get-tuple-element.1205, f32[256]{0:T(256)S(1)} %get-tuple-element.1210, f32[256]{0:T(256)S(1)} %get-tuple-element.1209, s32[256]{0:T(256)S(1)} %bitcast.267, bf16[256,1024]{1,0:T(8,128)(2,1)S(1)} %get-tuple-element.1203, f32[1024]{0:T(1024)S(1)} %convert_element_type.940, ...), kind=kOutput, calls=%fused_computation.113.clone.3 | convolution fusion | flops 16886497280 | bytes 99229696 | tf_op jit(solution)/shard_map/cond/branch_1_fun/while/body/eval_jaxpr/transpose(jvp(...h,vh->...v))/dot_general | solution.py:33
  1444.3 117.0 %convert_add_fusion.4 = f32[32128,1024]{1,0:T(8,128)} fusion(f32[32128,1024]{1,0:T(8,128)} %get-tuple-element.1246, bf16[32128,1024]{1,0:T(8,128)(2,1)} %fusion.363, f32[256,32128]{1,0:T(8,128)} %get-tuple-element.1211, f32[256]{0:T(256)S(1)} %get-tuple-element.1214, f32[256]{0:T(256)S(1)} %get-tuple-element.1213, s32[256]{0:T(256)S(1)} %bitcast.261, ...), kind=kOutput, calls=%fused_computation.103.clone.3 | convolution fusion | flops 17018093568 | bytes 362422272 | tf_op jit(solution)/shard_map/cond/branch_1_fun/while/body/eval_jaxpr/transpose(jvp(...h,vh->...v))/dot_general | solution.py:33
  1561.3 35.2 scatter_fusion.1
  1624.0 300.7 %while.59 = (s32[]{:T(128)}, bf16[256,1024]{1,0:T(8,128)(2,1)S(1)}, f32[1,1024,4096]{2,1,0:T(8,128)}, f32[1,4096,1024]{2,1,0:T(8,128)}, f32[32128,1024]{1,0:T(8,...) while((s32[]{:T(128)}, bf16[256,1024]{1,0:T(8,128)(2,1)S(1)}, ...), condition=%wide.region_31.34_spmd.clone, body=%wide.region_25.33_spmd.clone.sunk | while | flops 10802694144 | bytes 188242976 | solution.py:182
  1805.2 36.5 %conditional.5 = (f32[32128,1024]{1,0:T(8,128)}) conditional(s32[]{:T(128)} %convert_element_type.896, f32[32128,1024]{1,0:T(8,128)} %get-tuple-element.1346, (s32[2,256]{1,0:T(2,128)S(1)}, s32[]{:T(128)}, bf16[256,1024]{1,0:T(8,128)(2,1)}, f32[32128,1024]{1,0:T(8,128)}) %tuple.201), branch_computations={%region_28.30_spmd, %region_29.32_spmd} | conditional | flops 786432 | bytes 4721676 | solution.py:177
  1806.4 35.3 scatter_fusion
  1888.4 36.4 %conditional.5 = (f32[32128,1024]{1,0:T(8,128)}) conditional(s32[]{:T(128)} %convert_element_type.896, f32[32128,1024]{1,0:T(8,128)} %get-tuple-element.1346, (s32[2,256]{1,0:T(2,128)S(1)}, s32[]{:T(128)}, bf16[256,1024]{1,0:T(8,128)(2,1)}, f32[32128,1024]{1,0:T(8,128)}) %tuple.201), branch_computations={%region_28.30_spmd, %region_29.32_spmd} | conditional | flops 786432 | bytes 4721676 | solution.py:177
  1889.5 35.2 scatter_fusion
  1959.0 536.5 %all-reduce.4.cloned.1.call-done = (f32[1,1,1024,4096]{3,2,1,0:T(8,128)}, f32[1,1,4096,1024]{3,2,1,0:T(8,128)}) async-done(((f32[1,1,1024,4096]{3,2,1,0:T(8,128)}, f32[1,1,4096,1024]{3,2,1,0:T(8,128)}), (f32[1,1,1024,4096]{3,2,1,0:T(8,128)}, f32[1,1,4096,1024]{3,2,1,0:T(8,128)})) %all-reduce.4.cloned.1.call-update) | async-done | bytes 33554448 | tf_op jit(solution)/shard_map/psum | solution.py:184
  2495.5 1078.0 %reduce-scatter.4.cloned.1.call-done = f32[8032,1024]{1,0:T(8,128)} async-done(((f32[32128,1024]{1,0:T(8,128)}), f32[8032,1024]{1,0:T(8,128)}) %reduce-scatter.4.cloned.1.call-update) | async-done | bytes 32899088
  (467 shorter events, 688.3 us)
Async XLA Ops:
  7.2 582.1 %all-gather.3.cloned.1.call-start = ((), (), s32[]{:S(2)}) async-start(), calls=%async_computation.1 | async-start | bytes 82247680 | tf_op jit(solution)/shard_map/all_gather | solution.py:112
  24.3 2471.2 %all-reduce.4.cloned.1.call-start = ((), (), s32[]{:S(2)}) async-start(), calls=%async_computation.3 | async-start | bytes 67108864 | tf_op jit(solution)/shard_map/psum | solution.py:184
  607.8 3.0 collective-permute-start
  627.9 10.0 collective-permute-start
  655.0 10.5 collective-permute-start
  682.7 10.5 collective-permute-start
  710.3 10.5 collective-permute-start
  720.8 16.1 collective-permute-start.2
  738.2 40.7 %copy-start.6 = (bf16[2,256,1024]{2,1,0:T(8,128)(2,1)S(1)}, bf16[2,256,1024]{2,1,0:T(8,128)(2,1)}, u32[]{:S(2)}) copy-start(bf16[2,256,1024]{2,1,0:T(8,128)(2,1)} %get-tuple-element.1231) | copy-start | bytes 3145732 | tf_op jit(solution)/shard_map/cond
  738.2 40.7 %copy-start.27 = (bf16[1024]{0:T(1024)(128)(2,1)S(1)}, bf16[1024]{0:T(1024)(128)(2,1)}, u32[]{:S(2)}) copy-start(bf16[1024]{0:T(1024)(128)(2,1)} %get-tuple-element.1232) | copy-start | bytes 6148 | tf_op jit(solution)/shard_map/cond
  738.2 40.7 %copy-start.29 = (bf16[1024]{0:T(1024)(128)(2,1)S(1)}, bf16[1024]{0:T(1024)(128)(2,1)}, u32[]{:S(2)}) copy-start(bf16[1024]{0:T(1024)(128)(2,1)} %get-tuple-element.1235) | copy-start | bytes 6148 | tf_op jit(solution)/shard_map/cond
  738.2 40.7 %copy-start.31 = (bf16[1024]{0:T(1024)(128)(2,1)S(1)}, bf16[1024]{0:T(1024)(128)(2,1)}, u32[]{:S(2)}) copy-start(bf16[1024]{0:T(1024)(128)(2,1)} %get-tuple-element.1237) | copy-start | bytes 6148 | tf_op jit(solution)/shard_map/cond
  738.2 40.7 %copy-start.33 = (bf16[1024]{0:T(1024)(128)(2,1)S(1)}, bf16[1024]{0:T(1024)(128)(2,1)}, u32[]{:S(2)}) copy-start(bf16[1024]{0:T(1024)(128)(2,1)} %get-tuple-element.1240) | copy-start | bytes 6148 | tf_op jit(solution)/shard_map/cond
  1034.3 117.3 %copy-start.19 = (s32[1,256]{1,0:T(1,128)S(1)}, s32[1,256]{1,0:T(1,128)}, u32[]{:S(2)}) copy-start(s32[1,256]{1,0:T(1,128)} %copy-done.18) | copy-start | bytes 3076 | tf_op jit(solution)/shard_map/cond/branch_1_fun/while
  1366.6 38.7 %copy-start.17 = (f32[256]{0:T(256)S(1)}, f32[256]{0:T(256)}, u32[]{:S(2)}) copy-start(f32[256]{0:T(256)} %copy-done.16) | copy-start | bytes 3076 | tf_op jit(solution)/shard_map/cond/branch_1_fun/while
  1366.6 38.7 %copy-start.15 = (f32[256]{0:T(256)S(1)}, f32[256]{0:T(256)}, u32[]{:S(2)}) copy-start(f32[256]{0:T(256)} %copy-done.14) | copy-start | bytes 3076 | tf_op jit(solution)/shard_map/cond/branch_1_fun/while
  1444.3 117.0 %copy-start.19 = (s32[1,256]{1,0:T(1,128)S(1)}, s32[1,256]{1,0:T(1,128)}, u32[]{:S(2)}) copy-start(s32[1,256]{1,0:T(1,128)} %copy-done.18) | copy-start | bytes 3076 | tf_op jit(solution)/shard_map/cond/branch_1_fun/while
  1610.4 13.6 collective-permute-start.3
  1644.7 20.4 collective-permute-start.1
  1685.6 26.1 collective-permute-start.1
  1732.4 26.1 collective-permute-start.1
  1779.1 62.6 %collective-permute-start.1 = (bf16[256,1024]{1,0:T(8,128)(2,1)}, bf16[256,1024]{1,0:T(8,128)(2,1)S(1)}, u32[]{:S(2)}, u32[]{:S(2)}) collective-permute-start(bf16[256,1024]{1,0:T(8,128)(2,1)} %add_convert_fusion.2), channel_id=1, source_target_pairs={{1,0},{2,1},{3,2},{5,4},{6,5},{7,6},{9,8},{10,9},{11,10},{13,12},{... | collective-permute-start | bytes 1572872 | tf_op jit(solution)/shard_map/while/body/eval_jaxpr/ppermute | solution.py:178
  1862.3 62.5 %collective-permute-start.1 = (bf16[256,1024]{1,0:T(8,128)(2,1)}, bf16[256,1024]{1,0:T(8,128)(2,1)S(1)}, u32[]{:S(2)}, u32[]{:S(2)}) collective-permute-start(bf16[256,1024]{1,0:T(8,128)(2,1)} %add_convert_fusion.2), channel_id=1, source_target_pairs={{1,0},{2,1},{3,2},{5,4},{6,5},{7,6},{9,8},{10,9},{11,10},{13,12},{... | collective-permute-start | bytes 1572872 | tf_op jit(solution)/shard_map/while/body/eval_jaxpr/ppermute | solution.py:178
  1924.8 1648.8 %reduce-scatter.4.cloned.1.call-start = ((), (), s32[]{:S(2)}) async-start(), calls=%async_computation.2 | async-start | bytes 164495360
  (100 other events, 1373.6 us)
Sparse Core Ops, SparseCore 0:
  24.4 564.7 all-gather.2
  1924.9 570.6 all-reduce.3
  2499.3 1074.2 reduce-scatter.3
where the time goes:
time: 3620 us; the launch traced here: 3600 us
  waiting for transfers between devices  2210 us (61%)
  matrix products  918 us (25%)
  other arithmetic  253 us (7%)
  local copies, waits for them, and re-layouts  108 us (3%)
  starting transfers between devices  46.2 us (1%)
    unnamed x4, waiting for transfers between devices  1080 us
    dot_general x12, matrix products, cross_sum(): jnp.einsum('...h,vh->...v', normed, emb_table, preferred_element_type=jnp...  593 us
    all_gather x1, waiting for transfers between devices, device_step(): lax.all_gather(emb_s[0].astype(jnp.bfloat16), 'dp', axis=0, tiled=True)  564 us
    psum x1, waiting for transfers between devices, device_step(): g_in = lax.psum(g_in, 'dp')  537 us
  transfers between devices with their start and end apart: 15, of which 10 were waited for; matrix products, arithmetic and copies ran while one was open for 5% of the time, Pallas kernels for 0%

commit v1 on v0

v1 whole, which is shorter than its diff:
```python
import math
import jax
import jax.numpy as jnp
from jax import lax
from jax.experimental import pallas as pl
from jax.experimental.pallas import tpu as pltpu
from jax.sharding import PartitionSpec as P

MTP_WEIGHT = 0.3
EPS = 1e-6
BF = jnp.bfloat16
F32 = jnp.float32


def norm_only(acts):
    acts_f = acts.astype(F32)
    return acts_f * lax.rsqrt(jnp.mean(acts_f * acts_f, axis=-1, keepdims=True) + EPS)


def norm_bf16(acts):
    return norm_only(acts).astype(BF)


def gain_norm(acts, gain):
    return (norm_only(acts) * gain.astype(F32)).astype(BF)


def gelu_bf16(pre_act):
    return jax.nn.gelu(pre_act).astype(BF)


def dot(a, b, dims):
    return lax.dot_general(a, b, (dims, ((), ())), preferred_element_type=F32)


def normed_heads(hid, rows, gain_f, gain_h, gain_e, gain_m, w_proj, u_up, u_down):
    main = gain_norm(hid, gain_f)
    joined = jnp.concatenate([gain_norm(hid, gain_h), gain_norm(rows, gain_e)], axis=-1)
    state = jnp.dot(joined, w_proj, preferred_element_type=F32).astype(BF)
    inner = gelu_bf16(jnp.dot(gain_norm(state, gain_m), u_up, preferred_element_type=F32))
    state = (state.astype(F32) + jnp.dot(inner, u_down, preferred_element_type=F32)).astype(BF)
    return main, gain_norm(state, gain_f)


def stage_fwd(acts, w_in, w_out):
    act_out = gelu_bf16(jnp.dot(norm_bf16(acts), w_in, preferred_element_type=F32))
    return (acts.astype(F32) + jnp.dot(act_out, w_out, preferred_element_type=F32)).astype(BF)


def stage_dgrad(acts, w_in, w_out, d_out):
    normed, norm_back = jax.vjp(norm_bf16, acts)
    pre_act = jnp.dot(normed, w_in, preferred_element_type=F32)
    _, gelu_back = jax.vjp(gelu_bf16, pre_act)
    d_act = dot(d_out, w_out, ((1,), (1,))).astype(BF)
    d_pre = gelu_back(d_act)[0].astype(BF)
    d_norm = dot(d_pre, w_in, ((1,), (1,))).astype(BF)
    return (d_out.astype(F32) + norm_back(d_norm)[0].astype(F32)).astype(BF)


def stage_wgrad(acts, w_in, w_out, d_out):
    normed = norm_bf16(acts)
    pre_act = jnp.dot(normed, w_in, preferred_element_type=F32)
    act_out, gelu_back = jax.vjp(gelu_bf16, pre_act)
    g_out = dot(act_out, d_out, ((0,), (0,)))
    d_act = dot(d_out, w_out, ((1,), (1,))).astype(BF)
    d_pre = gelu_back(d_act)[0].astype(BF)
    g_in = dot(normed, d_pre, ((0,), (0,)))
    return g_in, g_out


TILE = 256


def scatter_kernel(starts_ref, rows_ref, perm_ref, base_ref, upd_ref, out_ref):
    tile = pl.program_id(0)
    out_ref[...] = base_ref[...]

    def add_row(k, carry):
        row = rows_ref[k] - tile * TILE
        out_ref[pl.ds(row, 1), :] += upd_ref[pl.ds(perm_ref[k], 1), :]
        return carry

    lax.fori_loop(starts_ref[tile], starts_ref[tile + 1], add_row, 0)


def scatter_rows(base, upd, ids):
    n_rows, hidden = base.shape
    n_tiles = pl.cdiv(n_rows, TILE)
    n_upd = ids.shape[0]
    sorted_ids, perm = lax.sort((ids, lax.iota(jnp.int32, n_upd)), num_keys=1)
    bounds = jnp.minimum(jnp.arange(n_tiles + 1, dtype=jnp.int32) * TILE, n_rows)
    starts = jnp.sum((ids[None, :] < bounds[:, None]).astype(jnp.int32), axis=1)
    return pl.pallas_call(
        scatter_kernel,
        grid_spec=pltpu.PrefetchScalarGridSpec(
            num_scalar_prefetch=3,
            grid=(n_tiles,),
            in_specs=[pl.BlockSpec((TILE, hidden), lambda i, *_: (i, 0)), pl.BlockSpec(memory_space=pltpu.VMEM)],
            out_specs=pl.BlockSpec((TILE, hidden), lambda i, *_: (i, 0)),
        ),
        out_shape=jax.ShapeDtypeStruct(base.shape, F32),
        name='scatter_rows',
    )(starts, sorted_ids, perm, base, upd)


def solution(mesh):
    n_stages = mesh.shape['pp']
    n_data = mesh.shape['dp']
    fwd_perm = [(i, i + 1) for i in range(n_stages - 1)]
    bwd_perm = [(i + 1, i) for i in range(n_stages - 1)]
    both = ('dp', 'pp')

    def from_first(pieces, stage):
        mine = jnp.where(stage == 0, pieces[0], jnp.zeros_like(pieces[0]))
        for q in range(1, n_stages):
            mine = mine + lax.ppermute(pieces[q], 'pp', [(0, q)])
        return mine

    def device_step(tokens, emb_s, w_up, w_down, gain_f, gain_h, gain_e, gain_m, w_proj, u_up, u_down):
        stage = lax.axis_index('pp')
        data = lax.axis_index('dp')
        is_first = stage == 0
        is_last = stage == n_stages - 1
        n_micro, rows_dev, width = tokens.shape
        seq_len = width - 2
        n_tok = rows_dev * seq_len
        n_own = n_micro * n_tok
        n_all = n_own * n_data
        table = emb_s[0]
        v_own, hidden = table.shape
        v_dev = v_own // n_stages
        n_vocab = v_own * n_data
        emb_scale = math.sqrt(hidden)
        loss_scale = 1.0 / n_all
        w_in = w_up[0, 0]
        w_out = w_down[0, 0]
        n_seq = n_micro * rows_dev
        q_seq = n_seq // n_stages
        n_q = q_seq * seq_len

        tok_all = lax.all_gather(tokens.reshape(n_seq, width), 'dp', axis=0, tiled=True)
        local_ids = tok_all.reshape(-1) - data * v_own
        owned = (local_ids >= 0) & (local_ids < v_own)
        got = jnp.take(table, jnp.clip(local_ids, 0, v_own - 1), axis=0)
        got = jnp.where(owned[:, None], got, 0.0).astype(BF)
        rows = lax.psum_scatter(got, 'dp', scatter_dimension=0, tiled=True)
        rows = rows.reshape(n_seq, width, hidden)

        table_q = from_first([table[q * v_dev:(q + 1) * v_dev].astype(BF) for q in range(n_stages)], stage)
        rows_q = from_first([rows[q * q_seq:(q + 1) * q_seq] for q in range(n_stages)], stage)

        first_in = (rows[:, 0:seq_len].astype(F32) * emb_scale).astype(BF).reshape(n_micro, n_tok, hidden)
        n_ticks = n_micro + n_stages - 1
        stage_in = jnp.zeros((n_micro, n_tok, hidden), BF)
        stage_out = jnp.zeros((n_micro, n_tok, hidden), BF)
        received = jnp.zeros((n_tok, hidden), BF)
        for tick in range(n_ticks):
            slot = tick - stage
            valid = (slot >= 0) & (slot < n_micro)
            slot_safe = jnp.clip(slot, 0, n_micro - 1)
            own_in = first_in[min(tick, n_micro - 1)]
            acts_in = jnp.where(is_first, own_in, received)
            acts_out = stage_fwd(acts_in, w_in, w_out)
            old_in = lax.dynamic_index_in_dim(stage_in, slot_safe, 0, keepdims=False)
            stage_in = lax.dynamic_update_index_in_dim(stage_in, jnp.where(valid, acts_in, old_in), slot_safe, 0)
            old_out = lax.dynamic_index_in_dim(stage_out, slot_safe, 0, keepdims=False)
            stage_out = lax.dynamic_update_index_in_dim(stage_out, jnp.where(valid, acts_out, old_out), slot_safe, 0)
            if tick < n_ticks - 1:
                received = lax.ppermute(acts_out, 'pp', fwd_perm)

        acts_all = lax.all_gather(stage_in.reshape(n_own, hidden), 'dp', axis=0, tiled=True)

        hid_flat = stage_out.reshape(n_own, hidden)
        hid_q = jnp.where(is_last, hid_flat[(n_stages - 1) * n_q:], jnp.zeros((n_q, hidden), BF))
        for q in range(n_stages - 1):
            hid_q = hid_q + lax.ppermute(hid_flat[q * n_q:(q + 1) * n_q], 'pp', [(n_stages - 1, q)])
        mtp_rows = (rows_q[:, 1:seq_len + 1].astype(F32) * emb_scale).astype(BF).reshape(n_q, hidden)

        def heads(hid, mtp):
            return normed_heads(hid, mtp, gain_f, gain_h, gain_e, gain_m, w_proj, u_up, u_down)

        (main_q, next_q), heads_back = jax.vjp(heads, hid_q, mtp_rows)

        dev_index = data * n_stages + stage
        shard_base = data * v_own + stage * v_dev
        columns = lax.broadcasted_iota(jnp.int32, (n_all, v_dev), 1)

        def head_fwd(norm_q):
            norm_all = lax.all_gather(norm_q, both, axis=0, tiled=True)
            logits = dot(norm_all, table_q, ((1,), (1,)))
            top = jnp.max(logits, axis=-1)
            total = jnp.sum(jnp.exp(logits - top[:, None]), axis=-1)
            stats = lax.all_gather(jnp.stack([top, total]), both, axis=0)
            top_all = jnp.max(stats[:, 0], axis=0)
            sum_all = jnp.sum(stats[:, 1] * jnp.exp(stats[:, 0] - top_all[None]), axis=0)
            return norm_all, logits, jnp.log(sum_all) + top_all

        def head_bwd(norm_all, logits, log_norm, targets, weight):
            hit = columns == (targets - shard_base)[:, None]
            d_logits = ((jnp.exp(logits - log_norm[:, None]) - hit.astype(F32)) * weight).astype(BF)
            d_norm = lax.psum_scatter(dot(d_logits, table_q, ((1,), (0,))), both, scatter_dimension=0, tiled=True)
            return d_norm.astype(BF), dot(d_logits, norm_all, ((0,), (0,)))

        mid_all = tok_all[:, 1:seq_len + 1].reshape(n_all)
        out_all = tok_all[:, 2:seq_len + 2].reshape(n_all)
        main_all, main_logits, main_lse = head_fwd(main_q)
        next_all, next_logits, next_lse = head_fwd(next_q)
        d_next, g_next = head_bwd(next_all, next_logits, next_lse, out_all, MTP_WEIGHT * loss_scale)
        d_main, g_main = head_bwd(main_all, main_logits, main_lse, mid_all, loss_scale)
        g_table = g_main + g_next

        def own(lse):
            return lax.dynamic_slice(lse, (dev_index * n_q,), (n_q,))

        mid_rows = rows_q[:, 1:seq_len + 1].reshape(n_q, hidden).astype(F32)
        out_rows = rows_q[:, 2:seq_len + 2].reshape(n_q, hidden).astype(F32)
        main_pick = jnp.sum(main_q.astype(F32) * mid_rows, axis=-1)
        next_pick = jnp.sum(next_q.astype(F32) * out_rows, axis=-1)
        local_loss = (jnp.sum(own(main_lse) - main_pick) + MTP_WEIGHT * jnp.sum(own(next_lse) - next_pick)) * loss_scale
        loss = lax.psum(local_loss, both)

        d_hid_q, d_rows_q = heads_back((d_main, d_next))
        d_rows_all = lax.all_gather(d_rows_q, both, axis=0, tiled=True)

        d_top = [lax.ppermute(d_hid_q, 'pp', [(q, n_stages - 1)]) for q in range(n_stages - 1)] + [d_hid_q]
        d_top = jnp.concatenate(d_top, axis=0).reshape(n_micro, n_tok, hidden)

        d_outs = jnp.zeros((n_micro, n_tok, hidden), BF)
        d_first = []
        received = jnp.zeros((n_tok, hidden), BF)
        for tick in range(n_ticks):
            slot = tick - (n_stages - 1 - stage)
            valid = (slot >= 0) & (slot < n_micro)
            slot_safe = jnp.clip(slot, 0, n_micro - 1)
            d_out = jnp.where(is_last, d_top[min(tick, n_micro - 1)], received)
            acts_in = lax.dynamic_index_in_dim(stage_in, slot_safe, 0, keepdims=False)
            old_d = lax.dynamic_index_in_dim(d_outs, slot_safe, 0, keepdims=False)
            d_outs = lax.dynamic_update_index_in_dim(d_outs, jnp.where(valid, d_out, old_d), slot_safe, 0)
            d_in = stage_dgrad(acts_in, w_in, w_out, d_out)
            if tick >= n_stages - 1:
                d_first.append(d_in)
            if tick < n_ticks - 1:
                received = lax.ppermute(d_in, 'pp', bwd_perm)
        d_out_all = lax.all_gather(d_outs.reshape(n_own, hidden), 'dp', axis=0, tiled=True)
        g_in, g_out = stage_wgrad(acts_all, w_in, w_out, d_out_all)

        d_first_all = lax.all_gather(jnp.concatenate(d_first, axis=0), 'dp', axis=0, tiled=True)
        seqs = n_seq * n_data
        upd = jnp.pad(d_first_all.reshape(seqs, seq_len, hidden), ((0, 0), (0, 1), (0, 0))).astype(F32)
        upd = upd + jnp.pad(d_rows_all.reshape(seqs, seq_len, hidden), ((0, 0), (1, 0), (0, 0))).astype(F32)
        upd = (upd * emb_scale).reshape(seqs * (seq_len + 1), hidden)
        pieces = [jnp.where(is_first, g_table, 0.0)]
        for q in range(1, n_stages):
            pieces.append(lax.ppermute(g_table, 'pp', [(q, 0)]))
        base = jnp.concatenate(pieces, axis=0)
        look_ids = jnp.where(is_first, tok_all[:, 0:seq_len + 1].reshape(-1) - data * v_own, -1)
        look_ids = jnp.where((look_ids >= 0) & (look_ids < v_own), look_ids, n_vocab)
        g_shard = scatter_rows(base, upd, look_ids)
        return loss, g_shard[None], g_in[None, None], g_out[None, None]

    return jax.shard_map(device_step, mesh=mesh, in_specs=(P(None, 'dp', None), P('pp', 'dp', None), P('pp'), P('pp'), P(), P(), P(), P(), P(), P(), P()), out_specs=(P(), P('pp', 'dp', None), P('pp'), P('pp')), check_vma=False)
```

time: 3620 us -> 1190 us (0.33)
  waiting for transfers between devices: 2210 us -> 294 us
  matrix products: 918 us -> 397 us
  blocking collectives: 33.5 us -> 209 us
  other arithmetic: 253 us -> 115 us
  local copies, waits for them, and re-layouts: 108 us -> 50.6 us
  Pallas kernels: 0 us -> 40.3 us
    unnamed x4 -> x9, waiting for transfers between devices: 1080 us -> 0.15 us
    all_gather x1 -> x6, waiting for transfers between devices: 564 us -> 0.03 us  [the longest x1 0.02 us: device_step(): lax.all_gather(stage_in.reshape(n_own, hidden), 'dp', axis=0, tiled=True)]
    psum x1 -> x0, waiting for transfers between devices: 537 us -> none  [device_step(): g_in = lax.psum(g_in, 'dp')]
    dot_general x52 -> x30, matrix products: 918 us -> 397 us  [the longest x14 255 us: dot(): return lax.dot_general(a, b, (dims, ((), ())), preferred_element_type=F32)]
    reduce_scatter x0 -> x3, waiting for transfers between devices: none -> 185 us  [the longest x2 134 us: head_bwd(): lax.psum_scatter(dot(d_logits, table_q, ((1,), (0,))), both, scatter_dime...]
    scatter-add x4 -> x0, other arithmetic: 141 us -> none  [the longest x2 70.5 us: head_step(): jax.ops.segment_sum(d_rows.astype(jnp.float32) * emb_scale, mid_tok, num_...]
    psum x1, blocking collectives: 33.5 us -> 171 us  [device_step(): loss = lax.psum(local_loss, both)]
    ppermute x12 -> x23, waiting for transfers between devices: 34.5 us -> 109 us  [the longest x6 98.9 us: from_first(): mine = mine + lax.ppermute(pieces[q], 'pp', [(0, q)])]
  transfers between devices with their start and end apart: 15 -> 32, of which waited for: 10 -> 9; matrix products, arithmetic and copies ran while one was open for 5% -> 28% of each run, Pallas kernels for 0% -> 3%
where the time goes in v1:
time: 1190 us
  matrix products  397 us (33%)
  waiting for transfers between devices  294 us (25%)
  blocking collectives  209 us (18%)
  other arithmetic  115 us (10%)
  starting transfers between devices  63.6 us (5%)
  local copies, waits for them, and re-layouts  50.6 us (4%)
  Pallas kernels  40.3 us (3%)
  between operations  17.1 us (1%)
    dot_general x14, matrix products, dot(): return lax.dot_general(a, b, (dims, ((), ())), preferred_element_type=F32)  255 us
    psum x1, blocking collectives, device_step(): loss = lax.psum(local_loss, both)  171 us
    reduce_scatter x2, waiting for transfers between devices, head_bwd(): lax.psum_scatter(dot(d_logits, table_q, ((1,), (0,))), both, scatter_dime...  134 us
    ppermute x6, waiting for transfers between devices, from_first(): mine = mine + lax.ppermute(pieces[q], 'pp', [(0, q)])  98.9 us
    dot_general x5, matrix products, stage_fwd(): jnp.dot(act_out, w_out, preferred_element_type=F32)  56.7 us
    reduce_scatter x1, waiting for transfers between devices, device_step(): rows = lax.psum_scatter(got, 'dp', scatter_dimension=0, tiled=True)  51 us
    pallas_call x1, Pallas kernels, scatter_rows(): pl.pallas_call(scatter_kernel, grid_spec=pltpu.PrefetchScalarGridSpec(num...  40.3 us
    dot_general x5, matrix products, stage_dgrad(): pre_act = jnp.dot(normed, w_in, preferred_element_type=F32)  36.1 us
  transfers between devices with their start and end apart: 32, of which 9 were waited for; matrix products, arithmetic and copies ran while one was open for 28% of the time, Pallas kernels for 3%

profile of v1, /device:TPU:0, one launch (start us, length us, event | category | flops | bytes accessed | tf_op | source)
XLA Modules:
  0.0 1186.5 jit_solution(16531258344180737158)
XLA Ops:
  17.9 21.3 %gather_fusion = bf16[2176,1024]{1,0:T(8,128)(2,1)} fusion(f32[8032,1024]{1,0:T(8,128)} %bitcast.509, s32[3072]{0:T(1024)S(1)} %pad_clamp_fusion), kind=kCustom, calls=%fused_computation | custom fusion | bytes 8921600 | tf_op jit(solution)/shard_map/jit(_take)/gather | solution.py:144
  44.2 51.0 %reduce-scatter.4.cloned.1.call-done = bf16[544,1024]{1,0:T(8,128)(2,1)} async-done(((bf16[2176,1024]{1,0:T(8,128)(2,1)}), bf16[544,1024]{1,0:T(8,128)(2,1)}) %reduce-scatter.4.cloned.1.call-update) | async-done | bytes 1114128 | tf_op jit(solution)/shard_map/reduce_scatter | solution.py:146
  253.4 54.8 %collective-permute-done.9 = bf16[2008,1024]{1,0:T(8,128)(2,1)} collective-permute-done((bf16[2008,1024]{1,0:T(8,128)(2,1)}, bf16[2008,1024]{1,0:T(8,128)(2,1)}, u32[]{:S(2)}, u32[]{:S(2)}) %collective-permute-start.9) | collective-permute-done | bytes 4112416 | tf_op jit(solution)/shard_map/ppermute | solution.py:116
  308.2 44.1 %collective-permute-done.8 = bf16[2008,1024]{1,0:T(8,128)(2,1)} collective-permute-done((bf16[2008,1024]{1,0:T(8,128)(2,1)}, bf16[2008,1024]{1,0:T(8,128)(2,1)}, u32[]{:S(2)}, u32[]{:S(2)}) %collective-permute-start.8) | collective-permute-done | bytes 4112416 | tf_op jit(solution)/shard_map/ppermute | solution.py:116
  360.5 15.1 %fusion.575 = (f32[2048]{0:T(1024)S(1)}, f32[2048,2008]{0,1:T(8,128)}) fusion(bf16[2048,1024]{1,0:T(8,128)(2,1)} %all-gather.13.cloned.1.call-done, bf16[2008,1024]{1,0:T(8,128)(2,1)} %fusion.202), kind=kOutput, calls=%fused_computation.645 | convolution fusion | flops 8426272768 | bytes 24764416 | tf_op jit(solution)/shard_map/dot_general | solution.py:33
  383.7 15.0 %all-gather.3 = f32[16,2,2048]{2,1,0:T(2,128)S(1)} all-gather(f32[1,2,2048]{2,1,0:T(2,128)S(1)} %maximum_bitcast_fusion.1), channel_id=3, replica_groups=mesh['dp'=4,'pp'=4] {'dp','pp'}, dimensions={0}, use_global_device_ids=true | all-gather | bytes 278528 | tf_op jit(solution)/shard_map/all_gather | solution.py:193
  398.7 15.1 %fusion.574 = (f32[2048]{0:T(1024)S(1)}, f32[2048,2008]{0,1:T(8,128)}) fusion(bf16[2048,1024]{1,0:T(8,128)(2,1)} %all-gather.11.cloned.1.call-done, bf16[2008,1024]{1,0:T(8,128)(2,1)} %fusion.202), kind=kOutput, calls=%fused_computation.644 | convolution fusion | flops 8426272768 | bytes 24764416 | tf_op jit(solution)/shard_map/dot_general | solution.py:33
  421.8 12.6 %all-gather.2 = f32[16,2,2048]{2,1,0:T(2,128)S(1)} all-gather(f32[1,2,2048]{2,1,0:T(2,128)S(1)} %maximum_bitcast_fusion), channel_id=2, replica_groups=mesh['dp'=4,'pp'=4] {'dp','pp'}, dimensions={0}, use_global_device_ids=true | all-gather | bytes 278528 | tf_op jit(solution)/shard_map/all_gather | solution.py:193
  435.0 16.1 %fusion.552 = f32[2048,1024]{1,0:T(8,128)} fusion(bf16[2008,1024]{1,0:T(8,128)(2,1)} %fusion.202, f32[2048,2008]{0,1:T(8,128)} %get-tuple-element.79, s32[2048]{0:T(1024)S(1)} %sub.197, f32[2048]{0:T(1024)S(1)} %log_add_fusion), kind=kOutput, calls=%fused_computation.638 | convolution fusion | flops 8446836736 | bytes 28966912 | tf_op jit(solution)/shard_map/dot_general | solution.py:33
  451.4 16.1 %fusion.550 = f32[2048,1024]{1,0:T(8,128)} fusion(bf16[2008,1024]{1,0:T(8,128)(2,1)} %fusion.202, f32[2048,2008]{0,1:T(8,128)} %get-tuple-element.73, s32[2048]{0:T(1024)S(1)} %sub.192, f32[2048]{0:T(1024)S(1)} %log_add_fusion.1), kind=kOutput, calls=%fused_computation.636 | convolution fusion | flops 8446836736 | bytes 28966912 | tf_op jit(solution)/shard_map/dot_general | solution.py:33
  483.2 60.9 %reduce-scatter.6.cloned.1.call-done = f32[128,1024]{1,0:T(8,128)} async-done(((f32[2048,1024]{1,0:T(8,128)}), f32[128,1024]{1,0:T(8,128)}) %reduce-scatter.6.cloned.1.call-update) | async-done | bytes 524304 | tf_op jit(solution)/shard_map/reduce_scatter | solution.py:201
  546.5 13.3 %multiply_reduce_fusion.1 = (f32[128]{0:T(128)S(1)}, f32[128,1024]{1,0:T(8,128)}) fusion(f32[128,1024]{1,0:T(8,128)S(1)} %get-tuple-element.75, f32[1024]{0:T(1024)S(1)} %convert_element_type.529, bf16[1024,4096]{1,0:T(8,128)(2,1)} %param.20, f32[128,4096]{1,0:T(8,128)} %copy-done.11, bf16[128,1024]{1,0:T(8,128)(2,1)S(1)} %fusion.391, ...), kind=kOutput, calls=%fused_computation.442 | convolution fusion | flops 2159149056 | bytes 20189696 | tf_op jit(solution)/shard_map/transpose(jvp())/dot_general | solution.py:40
  563.9 73.3 %reduce-scatter.8.cloned.1.call-done = f32[128,1024]{1,0:T(8,128)} async-done(((f32[2048,1024]{1,0:T(8,128)}), f32[128,1024]{1,0:T(8,128)}) %reduce-scatter.8.cloned.1.call-update) | async-done | bytes 524304 | tf_op jit(solution)/shard_map/reduce_scatter | solution.py:201
  697.5 12.0 %fusion.349 = (f32[256]{0:T(256)S(1)}, bf16[256,1024]{1,0:T(8,128)(2,1)}) fusion(bf16[2,256,1024]{2,1,0:T(8,128)(2,1)S(1)} %copy-done.1, s32[]{:T(128)S(6)} %min.69, bf16[1,1,1024,4096]{3,2,1,0:T(8,128)(2,1)} %param.13, f32[256,4096]{1,0:T(8,128)} %fusion.53, bf16[256,1024]{1,0:T(8,128)(2,1)} %get-tuple-element.21, bf16[1,1,4096,1024]{3,2,1,0:T(8,128)(2,1)} %param.14), kind=kOutput, calls=%fused_computation.325 | convolution fusion | flops 4319346688 | bytes 22545412 | tf_op jit(solution)/shard_map/dot_general | solution.py:33
  734.1 15.8 %fusion.551 = f32[2008,1024]{1,0:T(8,128)} fusion(bf16[2048,1024]{1,0:T(8,128)(2,1)} %all-gather.11.cloned.1.call-done, f32[2048,2008]{0,1:T(8,128)} %get-tuple-element.73, s32[2048]{0:T(1024)S(1)} %sub.192, f32[2048]{0:T(1024)S(1)} %log_add_fusion.1), kind=kOutput, calls=%fused_computation.637 | convolution fusion | flops 8446836736 | bytes 28884992 | tf_op jit(solution)/shard_map/dot_general | solution.py:33
  751.1 12.3 %fusion.355 = (f32[256]{0:T(256)S(1)}, bf16[256,1024]{1,0:T(8,128)(2,1)}) fusion(bf16[2,256,1024]{2,1,0:T(8,128)(2,1)S(1)} %copy-done.1, s32[]{:T(128)S(6)} %min.71, bf16[1,1,1024,4096]{3,2,1,0:T(8,128)(2,1)} %param.13, f32[256,4096]{1,0:T(8,128)} %fusion.45, bf16[256,1024]{1,0:T(8,128)(2,1)} %get-tuple-element.17, bf16[1,1,4096,1024]{3,2,1,0:T(8,128)(2,1)} %param.14), kind=kOutput, calls=%fused_computation.331 | convolution fusion | flops 4319346688 | bytes 22545412 | tf_op jit(solution)/shard_map/dot_general | solution.py:33
  766.0 18.8 %broadcast_select_fusion = (f32[2008,1024]{1,0:T(8,128)}, f32[2008,1024]{1,0:T(8,128)}) fusion(pred[]{:T(512)S(6)} %eq.25, f32[2008,1024]{1,0:T(8,128)} %fusion.551, bf16[2048,1024]{1,0:T(8,128)(2,1)} %all-gather.13.cloned.1.call-done, f32[2048,2008]{0,1:T(8,128)} %get-tuple-element.79, s32[2048]{0:T(1024)S(1)} %copy-done.34, f32[2048]{0:T(1024)S(1)} %copy-done.32), kind=kOutput, calls=%fused_computation.217 | convolution fusion | flops 8450949120 | bytes 45334528 | tf_op jit(solution)/shard_map/dot_general | solution.py:33
  801.6 24.3 %fusion.41 = f32[2048,4096]{1,0:T(8,128)} fusion(bf16[1,1,1024,4096]{3,2,1,0:T(8,128)(2,1)} %param.13, bf16[2048,1024]{1,0:T(8,128)(2,1)} %all-gather.19.cloned.1.call-done, f32[2048]{0:T(1024)S(1)} %add_rsqrt_fusion), kind=kOutput, calls=%fused_computation.55 | convolution fusion | flops 17186160640 | bytes 46145536 | tf_op jit(solution)/shard_map/dot_general | solution.py:62
  826.0 171.0 %psum.7 = f32[]{:T(128)} all-reduce(f32[]{:T(128)S(6)} %mul.974), channel_id=1, replica_groups=mesh['dp'=4,'pp'=4] {'dp','pp'}, use_global_device_ids=true, to_apply=%region_22.23 | all-reduce | flops 1 | bytes 8 | tf_op jit(solution)/shard_map/psum | solution.py:220
  997.0 22.6 %pad_maximum_fusion.base_ref = f32[8032,1024]{1,0:T(8,128)} fusion(f32[2008,1024]{1,0:T(8,128)} %collective-permute-done.15, f32[2008,1024]{1,0:T(8,128)} %collective-permute-done.14, f32[2008,1024]{1,0:T(8,128)} %collective-permute-done.13, f32[2008,1024]{1,0:T(8,128)} %get-tuple-element.80), kind=kLoop, calls=%fused_computation.16 | loop fusion | flops 24674304 | bytes 65798144 | tf_op jit(solution)/shard_map/concatenate | solution.py:255
  1039.8 40.3 %scatter_rows.1 = f32[8032,1024]{1,0:T(8,128)} custom-call(s32[33]{0:T(128)} %convert_reduce_fusion.starts_ref, s32[2112]{0:T(1024)} %get-tuple-element.6.rows_ref, s32[2112]{0:T(1024)} %get-tuple-element.7.perm_ref, f32[8032,1024]{1,0:T(8,128)} %pad_maximum_fusion.base_ref, f32[2112,1024]{1,0:T(8,128)} %reshape.496.upd_ref), custom_call_target="tpu_custom_call" | custom-call | tf_op jit(solution)/shard_map/scatter_rows/pallas_call | solution.py:93
  1080.1 31.6 %fusion.16 = f32[1,1,4096,1024]{3,2,1,0:T(8,128)} fusion(bf16[2048,1024]{1,0:T(8,128)(2,1)} %all-gather.21.cloned.1.call-done, f32[2048,4096]{1,0:T(8,128)} %fusion.41), kind=kOutput, calls=%fused_computation.30 | convolution fusion | flops 17255366656 | bytes 54525952 | tf_op jit(solution)/shard_map/dot_general | solution.py:33
  1111.6 43.9 %fusion.622 = bf16[2048,4096]{1,0:T(8,128)(2,1)} fusion(f32[2048,4096]{1,0:T(8,128)} %fusion.41, bf16[2048,1024]{1,0:T(8,128)(2,1)S(1)} %copy-done.55, bf16[1,1,4096,1024]{3,2,1,0:T(8,128)(2,1)} %param.14), kind=kOutput, calls=%fused_computation.7.clone.clone.clone.clone.2 | convolution fusion | flops 17364418560 | bytes 62914560 | tf_op jit(solution)/shard_map/dot_general | solution.py:33
  1155.6 23.9 %fusion.13 = f32[1,1,1024,4096]{3,2,1,0:T(8,128)} fusion(bf16[2048,1024]{1,0:T(8,128)(2,1)S(1)} %copy-done.8, f32[2048]{0:T(1024)S(1)} %copy-done.36, bf16[2048,4096]{1,0:T(8,128)(2,1)} %fusion.622), kind=kOutput, calls=%fused_computation.29 | convolution fusion | flops 17186160640 | bytes 37756928 | tf_op jit(solution)/shard_map/dot_general | solution.py:33
  (334 shorter events, 344.1 us)
Async XLA Ops:
  7.2 88.0 %reduce-scatter.4.cloned.1.call-start = ((), (), s32[]{:S(2)}) async-start(), calls=%async_computation.3 | async-start | bytes 5570560 | tf_op jit(solution)/shard_map/reduce_scatter | solution.py:146
  44.2 316.4 %all-gather.13.cloned.1.call-start = ((), (), s32[]{:S(2)}) async-start(), calls=%async_computation.5 | async-start | bytes 4456448 | tf_op jit(solution)/shard_map/all_gather | solution.py:189
  123.9 10.0 collective-permute-start.1
  146.1 23.7 %collective-permute-start.2 = (bf16[256,1024]{1,0:T(8,128)(2,1)}, bf16[256,1024]{1,0:T(8,128)(2,1)}, u32[]{:S(2)}, u32[]{:S(2)}) collective-permute-start(bf16[256,1024]{1,0:T(8,128)(2,1)} %get-tuple-element.69), channel_id=1, source_target_pairs={{0,1},{1,2},{2,3},{4,5},{5,6},{6,7},{8,9},{9,10},{10,11},{12,13},{... | collective-permute-start | bytes 1572872 | tf_op jit(solution)/shard_map/ppermute | solution.py:169
  161.3 21.9 %collective-permute-start.11 = (bf16[4,34,1024]{2,1,0:T(8,128)(2,1)}, bf16[4,34,1024]{2,1,0:T(8,128)(2,1)}, u32[]{:S(2)}, u32[]{:S(2)}) collective-permute-start(bf16[4,34,1024]{2,1,0:T(8,128)(2,1)} %slice.124), channel_id=1, source_target_pairs={{0,2},{4,6},{8,10},{12,14}} | collective-permute-start | bytes 835592 | tf_op jit(solution)/shard_map/ppermute | solution.py:116
  165.6 17.6 %collective-permute-start.12 = (bf16[4,34,1024]{2,1,0:T(8,128)(2,1)}, bf16[4,34,1024]{2,1,0:T(8,128)(2,1)}, u32[]{:S(2)}, u32[]{:S(2)}) collective-permute-start(bf16[4,34,1024]{2,1,0:T(8,128)(2,1)} %slice.126), channel_id=1, source_target_pairs={{0,3},{4,7},{8,11},{12,15}} | collective-permute-start | bytes 835592 | tf_op jit(solution)/shard_map/ppermute | solution.py:116
  167.6 15.6 %collective-permute-start.10 = (bf16[4,34,1024]{2,1,0:T(8,128)(2,1)}, bf16[4,34,1024]{2,1,0:T(8,128)(2,1)}, u32[]{:S(2)}, u32[]{:S(2)}) collective-permute-start(bf16[4,34,1024]{2,1,0:T(8,128)(2,1)} %slice.122), channel_id=1, source_target_pairs={{0,1},{4,5},{8,9},{12,13}} | collective-permute-start | bytes 835592 | tf_op jit(solution)/shard_map/ppermute | solution.py:116
  215.7 183.0 %all-gather.11.cloned.1.call-start = ((), (), s32[]{:S(2)}) async-start(), calls=%async_computation.4 | async-start | bytes 4456448 | tf_op jit(solution)/shard_map/all_gather | solution.py:189
  237.3 16.1 %collective-permute-start.7 = (bf16[2008,1024]{1,0:T(8,128)(2,1)}, bf16[2008,1024]{1,0:T(8,128)(2,1)}, u32[]{:S(2)}, u32[]{:S(2)}) collective-permute-start(bf16[2008,1024]{1,0:T(8,128)(2,1)} %get-tuple-element.40), channel_id=1, source_target_pairs={{0,1},{4,5},{8,9},{12,13}} | collective-permute-start | bytes 12337160 | tf_op jit(solution)/shard_map/ppermute | solution.py:116
  246.5 61.8 %collective-permute-start.9 = (bf16[2008,1024]{1,0:T(8,128)(2,1)}, bf16[2008,1024]{1,0:T(8,128)(2,1)}, u32[]{:S(2)}, u32[]{:S(2)}) collective-permute-start(bf16[2008,1024]{1,0:T(8,128)(2,1)} %get-tuple-element.41), channel_id=1, source_target_pairs={{0,3},{4,7},{8,11},{12,15}} | collective-permute-start | bytes 12337160 | tf_op jit(solution)/shard_map/ppermute | solution.py:116
  249.7 102.6 %collective-permute-start.8 = (bf16[2008,1024]{1,0:T(8,128)(2,1)}, bf16[2008,1024]{1,0:T(8,128)(2,1)}, u32[]{:S(2)}, u32[]{:S(2)}) collective-permute-start(bf16[2008,1024]{1,0:T(8,128)(2,1)} %get-tuple-element.42), channel_id=1, source_target_pairs={{0,2},{4,6},{8,10},{12,14}} | collective-permute-start | bytes 12337160 | tf_op jit(solution)/shard_map/ppermute | solution.py:116
  252.9 291.1 %reduce-scatter.6.cloned.1.call-start = ((), (), s32[]{:S(2)}) async-start(), calls=%async_computation.6 | async-start | bytes 8912896 | tf_op jit(solution)/shard_map/reduce_scatter | solution.py:201
  451.2 186.0 %reduce-scatter.8.cloned.1.call-start = ((), (), s32[]{:S(2)}) async-start(), calls=%async_computation.7 | async-start | bytes 8912896 | tf_op jit(solution)/shard_map/reduce_scatter | solution.py:201
  467.5 328.4 %all-gather.19.cloned.1.call-start = ((), (), s32[]{:S(2)}) async-start(), calls=%async_computation.10 | async-start | bytes 5242880 | tf_op jit(solution)/shard_map/all_gather | solution.py:171
  483.1 536.4 %all-gather.17.cloned.1.call-start = ((), (), s32[]{:S(2)}) async-start(), calls=%async_computation.9 | async-start | bytes 4456448 | tf_op jit(solution)/shard_map/all_gather | solution.py:223
  640.0 10.9 collective-permute-start.18
  640.7 10.2 collective-permute-start.17
  662.1 10.3 collective-permute-start.19
  714.1 305.4 %all-gather.15.cloned.1.call-start = ((), (), s32[]{:S(2)}) async-start(), calls=%async_computation.8 | async-start | bytes 5242880 | tf_op jit(solution)/shard_map/all_gather | solution.py:247
  732.4 17.6 %collective-permute-start.22 = (bf16[256,1024]{1,0:T(8,128)(2,1)S(1)}, bf16[256,1024]{1,0:T(8,128)(2,1)S(1)}, u32[]{:S(2)}, u32[]{:S(2)}) collective-permute-start(bf16[256,1024]{1,0:T(8,128)(2,1)S(1)} %add_convert_fusion.1), channel_id=1, source_target_pairs={{1,0},{2,1},{3,2},{5,4},{6,5},{7,6},{9,8},{10,9},{11,10},{13,12},{... | collective-permute-start | bytes 1572872 | tf_op jit(solution)/shard_map/ppermute | solution.py:243
  765.9 314.1 %all-gather.21.cloned.1.call-start = ((), (), s32[]{:S(2)}) async-start(), calls=%async_computation.11 | async-start | bytes 5242880 | tf_op jit(solution)/shard_map/all_gather | solution.py:244
  784.8 212.1 %collective-permute-start.14 = (f32[2008,1024]{1,0:T(8,128)}, f32[2008,1024]{1,0:T(8,128)}, u32[]{:S(2)}, u32[]{:S(2)}) collective-permute-start(f32[2008,1024]{1,0:T(8,128)} %get-tuple-element.81), channel_id=1, source_target_pairs={{2,0},{6,4},{10,8},{14,12}} | collective-permute-start | bytes 24674312 | tf_op jit(solution)/shard_map/ppermute | solution.py:254
  786.3 210.7 %collective-permute-start.13 = (f32[2008,1024]{1,0:T(8,128)}, f32[2008,1024]{1,0:T(8,128)}, u32[]{:S(2)}, u32[]{:S(2)}) collective-permute-start(f32[2008,1024]{1,0:T(8,128)} %get-tuple-element.81), channel_id=1, source_target_pairs={{1,0},{5,4},{9,8},{13,12}} | collective-permute-start | bytes 24674312 | tf_op jit(solution)/shard_map/ppermute | solution.py:254
  787.6 209.4 %collective-permute-start.15 = (f32[2008,1024]{1,0:T(8,128)}, f32[2008,1024]{1,0:T(8,128)}, u32[]{:S(2)}, u32[]{:S(2)}) collective-permute-start(f32[2008,1024]{1,0:T(8,128)} %get-tuple-element.81), channel_id=1, source_target_pairs={{3,0},{7,4},{11,8},{15,12}} | collective-permute-start | bytes 24674312 | tf_op jit(solution)/shard_map/ppermute | solution.py:254
  (68 other events, 1720.8 us)
Sparse Core Ops, SparseCore 0:
  44.3 50.8 reduce-scatter.3
  215.8 39.1 all-gather.12
  257.2 40.0 all-gather.10
  451.3 92.7 reduce-scatter.5
  546.2 90.9 reduce-scatter.7
  638.8 46.6 all-gather.18
  714.3 42.2 all-gather.16
  766.1 56.4 all-gather.14
  824.4 48.4 all-gather.20

commit v2 on v1

v2 whole, which is shorter than its diff:
```python
import math
import jax
import jax.numpy as jnp
from jax import lax
from jax.experimental import pallas as pl
from jax.experimental.pallas import tpu as pltpu
from jax.sharding import PartitionSpec as P

MTP_WEIGHT = 0.3
EPS = 1e-6
BF = jnp.bfloat16
F32 = jnp.float32


def norm_only(acts):
    acts_f = acts.astype(F32)
    return acts_f * lax.rsqrt(jnp.mean(acts_f * acts_f, axis=-1, keepdims=True) + EPS)


def norm_bf16(acts):
    return norm_only(acts).astype(BF)


def gain_norm(acts, gain):
    return (norm_only(acts) * gain.astype(F32)).astype(BF)


def gelu_bf16(pre_act):
    return jax.nn.gelu(pre_act).astype(BF)


def dot(a, b, dims):
    return lax.dot_general(a, b, (dims, ((), ())), preferred_element_type=F32)


def normed_heads(hid, rows, gain_f, gain_h, gain_e, gain_m, w_proj, u_up, u_down):
    main = gain_norm(hid, gain_f)
    joined = jnp.concatenate([gain_norm(hid, gain_h), gain_norm(rows, gain_e)], axis=-1)
    state = jnp.dot(joined, w_proj, preferred_element_type=F32).astype(BF)
    inner = gelu_bf16(jnp.dot(gain_norm(state, gain_m), u_up, preferred_element_type=F32))
    state = (state.astype(F32) + jnp.dot(inner, u_down, preferred_element_type=F32)).astype(BF)
    return main, gain_norm(state, gain_f)


MESH = pl.DeviceIdType.MESH
VMEM_LIMIT = 64 * 1024 * 1024 - 65536
FF_STEP = 512
WG_STEP = 512
WG_ROWS = 512
TILE = 256
GELU_K = math.sqrt(2.0 / math.pi)


def gelu_slope(x):
    t = jnp.tanh(GELU_K * (x + 0.044715 * x * x * x))
    return 0.5 * (1.0 + t) + 0.5 * x * (1.0 - t * t) * (GELU_K * (1.0 + 3.0 * 0.044715 * x * x))


def greet(peers):
    barrier = pltpu.get_barrier_semaphore()
    for peer in peers:
        pl.semaphore_signal(barrier, inc=1, device_id=peer, device_id_type=MESH)
    pl.semaphore_wait(barrier, len(peers))


def pipe_fwd_kernel(n_stages, x_ref, wi_hbm, wo_hbm, in_ref, hid_ref, wi, wo, recv, send, hid_buf, acc, w_sem, send_sem, recv_sem, hsend_sem, hrecv_sem):
    stage = lax.axis_index('pp')
    data = lax.axis_index('dp')
    last = n_stages - 1
    chunk = send.shape[1]
    ffn = wi.shape[1]
    load_in = pltpu.make_async_copy(wi_hbm, wi, w_sem.at[0])
    load_out = pltpu.make_async_copy(wo_hbm, wo, w_sem.at[1])
    load_in.start()
    load_out.start()
    greet([(data, lax.rem(stage + k, n_stages)) for k in range(1, n_stages)])

    def onward(c):
        return pltpu.make_async_remote_copy(
            src_ref=send.at[c], dst_ref=recv.at[c], send_sem=send_sem.at[c], recv_sem=recv_sem.at[c],
            device_id=(data, lax.rem(stage + 1, n_stages)), device_id_type=MESH)

    def deliver(c):
        return pltpu.make_async_remote_copy(
            src_ref=send.at[c], dst_ref=hid_buf, send_sem=hsend_sem.at[c], recv_sem=hrecv_sem,
            device_id=(data, c), device_id_type=MESH)

    load_in.wait()
    load_out.wait()

    def step(c, carry):
        rows = pl.ds(pl.multiple_of(c * chunk, chunk), chunk)

        @pl.when(stage == 0)
        def _():
            in_ref[rows, :] = x_ref[rows, :]

        @pl.when(stage > 0)
        def _():
            onward(c).wait_recv()
            in_ref[rows, :] = recv[c]

        acts = in_ref[rows, :].astype(F32)
        normed = norm_only(acts).astype(BF)
        acc[...] = acts

        def ffn_step(t, inner):
            cols = pl.ds(pl.multiple_of(t * FF_STEP, FF_STEP), FF_STEP)
            pre = jnp.dot(normed, wi[:, cols], preferred_element_type=F32)
            acc[...] += jnp.dot(gelu_bf16(pre), wo[cols, :], preferred_element_type=F32)
            return inner

        lax.fori_loop(0, ffn // FF_STEP, ffn_step, 0)
        send[c] = acc[...].astype(BF)

        @pl.when(stage < last)
        def _():
            onward(c).start()

        @pl.when((stage == last) & (c < last))
        def _():
            deliver(c).start()

        return carry

    lax.fori_loop(0, n_stages, step, 0)

    @pl.when(stage < last)
    def _():
        for c in range(n_stages):
            onward(c).wait_send()
        deliver(0).wait_recv()
        hid_ref[...] = hid_buf[...]

    @pl.when(stage == last)
    def _():
        hid_ref[...] = send[last]
        for c in range(last):
            deliver(c).wait_send()


def pipe_fwd(x, w_in, w_out, n_stages):
    n_tok, hidden = x.shape
    ffn = w_in.shape[1]
    chunk = n_tok // n_stages
    vmem = pl.BlockSpec(memory_space=pltpu.VMEM)
    hbm = pl.BlockSpec(memory_space=pl.ANY)
    return pl.pallas_call(
        lambda *refs: pipe_fwd_kernel(n_stages, *refs),
        in_specs=[vmem, hbm, hbm],
        out_specs=[vmem, vmem],
        out_shape=[jax.ShapeDtypeStruct((n_tok, hidden), BF), jax.ShapeDtypeStruct((chunk, hidden), BF)],
        scratch_shapes=[
            pltpu.VMEM((hidden, ffn), BF),
            pltpu.VMEM((ffn, hidden), BF),
            pltpu.VMEM((n_stages, chunk, hidden), BF),
            pltpu.VMEM((n_stages, chunk, hidden), BF),
            pltpu.VMEM((chunk, hidden), BF),
            pltpu.VMEM((chunk, hidden), F32),
            pltpu.SemaphoreType.DMA((2,)),
            pltpu.SemaphoreType.DMA((n_stages,)),
            pltpu.SemaphoreType.DMA((n_stages,)),
            pltpu.SemaphoreType.DMA((n_stages,)),
            pltpu.SemaphoreType.DMA,
        ],
        compiler_params=pltpu.CompilerParams(collective_id=0, has_side_effects=True, vmem_limit_bytes=VMEM_LIMIT),
        cost_estimate=pl.CostEstimate(flops=4 * n_tok * hidden * ffn * 4, bytes_accessed=4 * hidden * ffn, transcendentals=0),
        name='pipe_fwd',
    )(x, w_in, w_out)


def pipe_bwd_kernel(n_stages, n_data, top_ref, acts_ref, wi_hbm, wo_hbm, dall_hbm, fall_hbm, wi, wo, slope, top, dall, fall, acc,
                    w_sem, csend, crecv, tsend, trecv, gsend, grecv, fsend, frecv, o_sem):
    stage = lax.axis_index('pp')
    data = lax.axis_index('dp')
    last = n_stages - 1
    chunk = top.shape[1]
    ffn = wi.shape[1]
    load_in = pltpu.make_async_copy(wi_hbm, wi, w_sem.at[0])
    load_out = pltpu.make_async_copy(wo_hbm, wo, w_sem.at[1])
    load_in.start()
    load_out.start()
    greet([(data, lax.rem(stage + k, n_stages)) for k in range(1, n_stages)]
          + [(lax.rem(data + k, n_data), stage) for k in range(1, n_data)])

    def hand_in(slot):
        return pltpu.make_async_remote_copy(
            src_ref=top_ref, dst_ref=top.at[slot], send_sem=tsend, recv_sem=trecv.at[slot],
            device_id=(data, last), device_id_type=MESH)

    def back(c):
        return pltpu.make_async_remote_copy(
            src_ref=fall.at[data, c], dst_ref=dall.at[data, c], send_sem=csend.at[c], recv_sem=crecv.at[c],
            device_id=(data, lax.rem(stage + last, n_stages)), device_id_type=MESH)

    def share(buf, owner, k, c, send_sem, recv_sem):
        return pltpu.make_async_remote_copy(
            src_ref=buf.at[owner, c], dst_ref=buf.at[owner, c], send_sem=send_sem.at[k - 1, c], recv_sem=recv_sem.at[k - 1, c],
            device_id=(lax.rem(data + k, n_data), stage), device_id_type=MESH)

    @pl.when(stage < last)
    def _():
        hand_in(stage).start()

    @pl.when(stage == last)
    def _():
        top[last] = top_ref[...]

    load_in.wait()
    normed_all = norm_only(acts_ref[...].astype(F32)).astype(BF)

    def slope_step(t, carry):
        cols = pl.ds(pl.multiple_of(t * FF_STEP, FF_STEP), FF_STEP)
        slope[:, cols] = gelu_slope(jnp.dot(normed_all, wi[:, cols], preferred_element_type=F32))
        return carry

    lax.fori_loop(0, ffn // FF_STEP, slope_step, 0)
    load_out.wait()

    def step(c, carry):
        rows = pl.ds(pl.multiple_of(c * chunk, chunk), chunk)

        @pl.when((stage == last) & (c < last))
        def _():
            hand_in(c).wait_recv()

        @pl.when(stage == last)
        def _():
            dall[data, c] = top[c]

        @pl.when(stage < last)
        def _():
            back(c).wait_recv()

        d_out = dall[data, c]
        acc[...] = jnp.zeros_like(acc)

        def ffn_step(t, inner):
            cols = pl.ds(pl.multiple_of(t * FF_STEP, FF_STEP), FF_STEP)
            d_act = dot(d_out, wo[cols, :], ((1,), (1,))).astype(BF).astype(F32)
            d_pre = (d_act * slope[rows, cols]).astype(BF)
            acc[...] += dot(d_pre, wi[:, cols], ((1,), (1,)))
            return inner

        lax.fori_loop(0, ffn // FF_STEP, ffn_step, 0)
        d_norm = acc[...].astype(BF).astype(F32)
        acts = acts_ref[rows, :].astype(F32)
        scale = lax.rsqrt(jnp.mean(acts * acts, axis=-1, keepdims=True) + EPS)
        inner_mean = jnp.mean(d_norm * acts, axis=-1, keepdims=True)
        d_acts = (d_norm * scale - acts * (scale * scale * scale * inner_mean)).astype(BF)
        fall[data, c] = (d_out.astype(F32) + d_acts.astype(F32)).astype(BF)

        @pl.when(stage > 0)
        def _():
            back(c).start()

        for k in range(1, n_data):
            share(dall, data, k, c, gsend, grecv).start()

        @pl.when(stage == 0)
        def _():
            for k in range(1, n_data):
                share(fall, data, k, c, fsend, frecv).start()

        return carry

    lax.fori_loop(0, n_stages, step, 0)

    @pl.when(stage < last)
    def _():
        hand_in(stage).wait_send()

    @pl.when(stage > 0)
    def _():
        for c in range(n_stages):
            back(c).wait_send()

    for k in range(1, n_data):
        for c in range(n_stages):
            share(dall, data, k, c, gsend, grecv).wait_send()
            share(dall, lax.rem(data + n_data - k, n_data), k, c, gsend, grecv).wait_recv()
    save = pltpu.make_async_copy(dall, dall_hbm, o_sem.at[0])
    save.start()

    @pl.when(stage == 0)
    def _():
        for k in range(1, n_data):
            for c in range(n_stages):
                share(fall, data, k, c, fsend, frecv).wait_send()
                share(fall, lax.rem(data + n_data - k, n_data), k, c, fsend, frecv).wait_recv()
        save_first = pltpu.make_async_copy(fall, fall_hbm, o_sem.at[1])
        save_first.start()
        save_first.wait()

    save.wait()


def pipe_bwd(d_top, acts, w_in, w_out, n_stages, n_data):
    n_tok, hidden = acts.shape
    ffn = w_in.shape[1]
    chunk = n_tok // n_stages
    vmem = pl.BlockSpec(memory_space=pltpu.VMEM)
    hbm = pl.BlockSpec(memory_space=pl.ANY)
    full = (n_data, n_stages, chunk, hidden)
    dma = pltpu.SemaphoreType.DMA
    return pl.pallas_call(
        lambda *refs: pipe_bwd_kernel(n_stages, n_data, *refs),
        in_specs=[vmem, vmem, hbm, hbm],
        out_specs=[hbm, hbm],
        out_shape=[jax.ShapeDtypeStruct(full, BF), jax.ShapeDtypeStruct(full, BF)],
        scratch_shapes=[
            pltpu.VMEM((hidden, ffn), BF),
            pltpu.VMEM((ffn, hidden), BF),
            pltpu.VMEM((n_tok, ffn), F32),
            pltpu.VMEM((n_stages, chunk, hidden), BF),
            pltpu.VMEM(full, BF),
            pltpu.VMEM(full, BF),
            pltpu.VMEM((chunk, hidden), F32),
            dma((2,)), dma((n_stages,)), dma((n_stages,)), dma, dma((n_stages,)),
            dma((n_data - 1, n_stages)), dma((n_data - 1, n_stages)),
            dma((n_data - 1, n_stages)), dma((n_data - 1, n_stages)), dma((2,)),
        ],
        compiler_params=pltpu.CompilerParams(collective_id=1, has_side_effects=True, vmem_limit_bytes=VMEM_LIMIT),
        cost_estimate=pl.CostEstimate(flops=6 * n_tok * hidden * ffn * 4, bytes_accessed=4 * hidden * ffn, transcendentals=0),
        name='pipe_bwd',
    )(d_top, acts, w_in, w_out)


def wgrad_kernel(n_ref, nt_ref, d_ref, wi_ref, wo_ref, gi_ref, go_ref):
    gi_ref[...] = jnp.zeros_like(gi_ref)
    go_ref[...] = jnp.zeros_like(go_ref)
    for b in range(n_ref.shape[0] // WG_ROWS):
        rows = slice(b * WG_ROWS, (b + 1) * WG_ROWS)
        pre = jnp.dot(n_ref[rows, :], wi_ref[...], preferred_element_type=F32)
        d_act = dot(d_ref[rows, :], wo_ref[...], ((1,), (1,))).astype(BF).astype(F32)
        t = jnp.tanh(GELU_K * (pre + 0.044715 * pre * pre * pre))
        half = 0.5 * (1.0 + t)
        act = (pre * half).astype(BF)
        slope = half + 0.5 * pre * (1.0 - t * t) * (GELU_K * (1.0 + 3.0 * 0.044715 * pre * pre))
        gi_ref[...] += jnp.dot(nt_ref[:, rows], (d_act * slope).astype(BF), preferred_element_type=F32)
        go_ref[...] += dot(act, d_ref[rows, :], ((0,), (0,)))


def stage_wgrad(normed, normed_t, w_in, w_out, d_out):
    n_all, hidden = normed.shape
    ffn = w_in.shape[1]
    vmem = pl.BlockSpec(memory_space=pltpu.VMEM)
    cols = pl.BlockSpec((hidden, WG_STEP), lambda i: (0, i))
    rows = pl.BlockSpec((WG_STEP, hidden), lambda i: (i, 0))
    return pl.pallas_call(
        wgrad_kernel,
        grid=(ffn // WG_STEP,),
        in_specs=[vmem, vmem, vmem, cols, rows],
        out_specs=[cols, rows],
        out_shape=[jax.ShapeDtypeStruct((hidden, ffn), F32), jax.ShapeDtypeStruct((ffn, hidden), F32)],
        compiler_params=pltpu.CompilerParams(vmem_limit_bytes=VMEM_LIMIT),
        cost_estimate=pl.CostEstimate(flops=8 * n_all * hidden * ffn, bytes_accessed=12 * hidden * ffn, transcendentals=n_all * ffn),
        name='stage_wgrad',
    )(normed, normed_t, d_out, w_in, w_out)


def scatter_kernel(scale, firsts, starts_ref, rows_ref, perm_ref, *refs):
    pieces = refs[:-4]
    first_ref, next_ref, out_ref, upd = refs[-4:]
    tile = pl.program_id(0)
    n_tiles = pl.num_programs(0)
    owner = starts_ref[n_tiles + 1] == 1
    n_first = first_ref.shape[0]

    @pl.when(owner & (tile == 0))
    def _():
        upd[0:n_first] = first_ref[...].astype(F32) * scale
        upd[n_first:] = next_ref[...].astype(F32) * scale

    @pl.when(jnp.logical_not(owner))
    def _():
        out_ref[...] = jnp.zeros_like(out_ref)

    for q, piece in enumerate(pieces):
        @pl.when(owner & (tile >= firsts[q]) & (tile < firsts[q + 1]))
        def _():
            out_ref[...] = piece[...]

    def add_row(k, carry):
        row = rows_ref[k] - tile * TILE
        out_ref[pl.ds(row, 1), :] += upd[pl.ds(perm_ref[k], 1), :]
        return carry

    lax.fori_loop(starts_ref[tile], starts_ref[tile + 1], add_row, 0)


def scatter_plan(ids, owner, n_rows):
    n_tiles = pl.cdiv(n_rows, TILE)
    sorted_ids, perm = lax.sort((ids, lax.iota(jnp.int32, ids.shape[0])), num_keys=1)
    bounds = jnp.minimum(jnp.arange(n_tiles + 1, dtype=jnp.int32) * TILE, n_rows)
    starts = jnp.sum((ids[None, :] < bounds[:, None]).astype(jnp.int32), axis=1)
    return jnp.concatenate([starts, owner.astype(jnp.int32)[None]]), sorted_ids, perm


def scatter_rows(pieces, n_rows, first, following, plan, scale):
    hidden = first.shape[1]
    n_tiles = pl.cdiv(n_rows, TILE)
    n_upd = plan[1].shape[0]
    firsts = [0]
    for piece in pieces:
        firsts.append(firsts[-1] + piece.shape[0] // TILE)

    def piece_map(q):
        return lambda i, starts_ref, *_: (jnp.clip(i - firsts[q], 0, firsts[q + 1] - firsts[q] - 1) * starts_ref[n_tiles + 1], 0)

    vmem = pl.BlockSpec(memory_space=pltpu.VMEM)
    return pl.pallas_call(
        lambda *refs: scatter_kernel(scale, firsts, *refs),
        grid_spec=pltpu.PrefetchScalarGridSpec(
            num_scalar_prefetch=3,
            grid=(n_tiles,),
            in_specs=[pl.BlockSpec((TILE, hidden), piece_map(q)) for q in range(len(pieces))] + [vmem, vmem],
            out_specs=pl.BlockSpec((TILE, hidden), lambda i, *_: (i, 0)),
            scratch_shapes=[pltpu.VMEM((n_upd, hidden), F32)],
        ),
        out_shape=jax.ShapeDtypeStruct((n_rows, hidden), F32),
        compiler_params=pltpu.CompilerParams(vmem_limit_bytes=VMEM_LIMIT),
        name='scatter_rows',
    )(*plan, *pieces, first, following)


VTILE = 512
SHARES = (6, 6, 2, 2)
ROWS = 512
LOWEST = float(jnp.finfo(jnp.float32).min)


def head_fwd_kernel(meta, n_ref, e_ref, z_ref, top_ref, sum_ref):
    tile = pl.program_id(0)

    @pl.when(tile == 0)
    def _():
        top_ref[...] = jnp.full_like(top_ref, LOWEST)
        sum_ref[...] = jnp.zeros_like(sum_ref)

    @pl.when(tile < meta[0])
    def _():
        keep = tile * VTILE + lax.broadcasted_iota(jnp.int32, (ROWS, VTILE), 1) < meta[1]

        def block(b, carry):
            rows = pl.ds(pl.multiple_of(b * ROWS, ROWS), ROWS)
            z = dot(n_ref[rows, :], e_ref[...], ((1,), (1,)))
            z = jnp.where(keep, z, LOWEST)
            z_ref[rows, :] = z
            lanes = [z[:, k * 128:(k + 1) * 128] for k in range(VTILE // 128)]
            old = top_ref[rows, :]
            new = old
            for part in lanes:
                new = jnp.maximum(new, part)
            total = sum_ref[rows, :] * jnp.exp(old - new)
            for part in lanes:
                total = total + jnp.exp(part - new)
            top_ref[rows, :] = new
            sum_ref[rows, :] = total
            return carry

        lax.fori_loop(0, n_ref.shape[0] // ROWS, block, 0, unroll=True)


def head_fwd(meta, norm_all, table_q):
    n_all, hidden = norm_all.shape
    tiles = table_q.shape[0] // VTILE
    vmem = pl.BlockSpec(memory_space=pltpu.VMEM)
    return pl.pallas_call(
        head_fwd_kernel,
        grid_spec=pltpu.PrefetchScalarGridSpec(
            num_scalar_prefetch=1,
            grid=(tiles,),
            in_specs=[vmem, pl.BlockSpec((VTILE, hidden), lambda i, meta: (jnp.minimum(i, meta[0] - 1), 0))],
            out_specs=[pl.BlockSpec((n_all, VTILE), lambda i, meta: (0, jnp.minimum(i, meta[0] - 1))), vmem, vmem],
        ),
        out_shape=[jax.ShapeDtypeStruct((n_all, tiles * VTILE), F32)] + [jax.ShapeDtypeStruct((n_all, 128), F32)] * 2,
        compiler_params=pltpu.CompilerParams(vmem_limit_bytes=VMEM_LIMIT),
        cost_estimate=pl.CostEstimate(flops=2 * n_all * hidden * tiles * VTILE, bytes_accessed=4 * n_all * tiles * VTILE, transcendentals=n_all * tiles * VTILE),
        name='head_fwd',
    )(meta, norm_all, table_q)


def head_bwd_kernel(weight, meta, n_ref, e_ref, z_ref, lse_ref, tgt_ref, *refs):
    prev_ref = refs[0] if len(refs) == 4 else None
    dn_ref, de_ref, grad = refs[-3:]
    tile = pl.program_id(0)

    @pl.when(tile == 0)
    def _():
        dn_ref[...] = jnp.zeros_like(dn_ref)

    @pl.when(tile < meta[0])
    def _():
        column = tile * VTILE + lax.broadcasted_iota(jnp.int32, (ROWS, VTILE), 1)

        def block(b, carry):
            rows = pl.ds(pl.multiple_of(b * ROWS, ROWS), ROWS)
            prob = jnp.exp(z_ref[rows, :] - lse_ref[rows, :])
            hit = column == tgt_ref[rows, :]
            g = (jnp.where(hit, prob - 1.0, prob) * weight).astype(BF)
            grad[rows, :] = g
            dn_ref[rows, :] += jnp.dot(g, e_ref[...], preferred_element_type=F32)
            return carry

        lax.fori_loop(0, n_ref.shape[0] // ROWS, block, 0, unroll=True)
        de = dot(grad[...], n_ref[...], ((0,), (0,)))
        de_ref[...] = de if prev_ref is None else de + prev_ref[...]


def head_bwd(meta, norm_all, table_q, z, lse, targets, weight, prev):
    n_all, hidden = norm_all.shape
    tiles = table_q.shape[0] // VTILE
    vmem = pl.BlockSpec(memory_space=pltpu.VMEM)
    vrows = pl.BlockSpec((VTILE, hidden), lambda i, meta: (jnp.minimum(i, meta[0] - 1), 0))
    vcols = pl.BlockSpec((n_all, VTILE), lambda i, meta: (0, jnp.minimum(i, meta[0] - 1)))
    extra = [] if prev is None else [prev]
    return pl.pallas_call(
        lambda *refs: head_bwd_kernel(weight, *refs),
        grid_spec=pltpu.PrefetchScalarGridSpec(
            num_scalar_prefetch=1,
            grid=(tiles,),
            in_specs=[vmem, vrows, vcols, vmem, vmem] + [vrows] * len(extra),
            out_specs=[vmem, vrows],
            scratch_shapes=[pltpu.VMEM((n_all, VTILE), BF)],
        ),
        out_shape=[jax.ShapeDtypeStruct((n_all, hidden), F32), jax.ShapeDtypeStruct(table_q.shape, F32)],
        compiler_params=pltpu.CompilerParams(vmem_limit_bytes=VMEM_LIMIT),
        cost_estimate=pl.CostEstimate(flops=4 * n_all * hidden * tiles * VTILE, bytes_accessed=4 * n_all * tiles * VTILE, transcendentals=n_all * tiles * VTILE),
        name='head_bwd',
    )(meta, norm_all, table_q, z, lse[:, None], targets[:, None], *extra)


def solution(mesh):
    n_stages = mesh.shape['pp']
    n_data = mesh.shape['dp']
    both = ('dp', 'pp')

    firsts = [VTILE * sum(SHARES[:q]) for q in range(n_stages + 1)]

    def from_first(pieces, stage):
        mine = jnp.where(stage == 0, pieces[0], jnp.zeros_like(pieces[0]))
        for q in range(1, n_stages):
            mine = mine + lax.ppermute(pieces[q], 'pp', [(0, q)])
        return mine

    def device_body(tokens, emb_s, w_up, w_down, gain_f, gain_h, gain_e, gain_m, w_proj, u_up, u_down):
        stage = lax.axis_index('pp')
        data = lax.axis_index('dp')
        is_first = stage == 0
        n_micro, rows_dev, width = tokens.shape
        seq_len = width - 2
        table = emb_s[0]
        v_own, hidden = table.shape
        v_dev = VTILE * max(SHARES)
        emb_scale = math.sqrt(hidden)
        w_in = w_up[0, 0]
        w_out = w_down[0, 0]
        n_seq = n_micro * rows_dev
        n_own = n_seq * seq_len
        n_all = n_own * n_data
        loss_scale = 1.0 / n_all
        q_seq = n_seq // n_stages
        n_q = q_seq * seq_len
        n_pos = n_seq * width

        tok_all = lax.all_gather(tokens.reshape(n_seq, width), 'dp', axis=0, tiled=True)
        local_ids = tok_all.reshape(-1) - data * v_own
        owned = (local_ids >= 0) & (local_ids < v_own)
        got = jnp.take(table, jnp.clip(local_ids, 0, v_own - 1), axis=0)
        got = jnp.where(owned[:, None], got, 0.0).astype(BF).reshape(n_data, n_pos, hidden)
        rows = lax.dynamic_index_in_dim(got, data, 0, keepdims=False)
        for k in range(1, n_data):
            outgoing = lax.dynamic_index_in_dim(got, lax.rem(data + k, n_data), 0, keepdims=False)
            pairs = [(d * n_stages, ((d + k) % n_data) * n_stages) for d in range(n_data)]
            rows = rows + lax.ppermute(outgoing, both, pairs)
        rows = rows.reshape(n_seq, width, hidden)

        def piece(q):
            part = table[firsts[q]:min(firsts[q + 1], v_own)].astype(BF)
            return jnp.pad(part, ((0, VTILE * SHARES[q] - part.shape[0]), (0, 0)))

        table_q = jnp.where(is_first, piece(0), 0)
        for q in range(1, n_stages):
            sent = lax.ppermute(piece(q), 'pp', [(0, q)])
            table_q = table_q + jnp.pad(sent, ((0, v_dev - sent.shape[0]), (0, 0)))
        rows_q = from_first([rows[q * q_seq:(q + 1) * q_seq] for q in range(n_stages)], stage)

        first_in = (rows[:, 0:seq_len].astype(F32) * emb_scale).astype(BF).reshape(n_own, hidden)
        stage_in, hid_q = pipe_fwd(first_in, w_in, w_out, n_stages)
        mtp_rows = (rows_q[:, 1:seq_len + 1].astype(F32) * emb_scale).astype(BF).reshape(n_q, hidden)

        def heads(hid, mtp):
            return normed_heads(hid, mtp, gain_f, gain_h, gain_e, gain_m, w_proj, u_up, u_down)

        (main_q, next_q), heads_back = jax.vjp(heads, hid_q, mtp_rows)

        dev_index = data * n_stages + stage
        shard_first = jnp.asarray(firsts[:-1], jnp.int32)[stage]
        shard_last = jnp.minimum(jnp.asarray(firsts[1:], jnp.int32)[stage], v_own)
        valid = shard_last - shard_first
        meta = jnp.stack([jnp.asarray(SHARES, jnp.int32)[stage], valid])

        def targets_of(ids):
            local = ids - data_base
            return jnp.where((local >= 0) & (local < valid), local, -1)

        data_base = data * v_own + shard_first

        def collect(partial):
            return lax.psum_scatter(partial, both, scatter_dimension=0, tiled=True).astype(BF)

        mid_all = tok_all[:, 1:seq_len + 1].reshape(n_all)
        out_all = tok_all[:, 2:seq_len + 2].reshape(n_all)
        main_all = lax.all_gather(main_q, both, axis=0, tiled=True)
        next_all = lax.all_gather(next_q, both, axis=0, tiled=True)
        stage_in_late, main_all, next_all = lax.optimization_barrier((stage_in, main_all, next_all))
        acts_all = lax.all_gather(stage_in_late, 'dp', axis=0, tiled=True)
        main_z, main_top, main_sum = head_fwd(meta, main_all, table_q)
        next_z, next_top, next_sum = head_fwd(meta, next_all, table_q)
        lane_top = jnp.stack([main_top, next_top])
        top = jnp.max(lane_top, axis=-1)
        total = jnp.sum(jnp.stack([main_sum, next_sum]) * jnp.exp(lane_top - top[..., None]), axis=-1)
        stats = lax.all_gather(jnp.stack([top, total]), both, axis=0)
        top_all = jnp.max(stats[:, 0], axis=0)
        sum_all = jnp.sum(stats[:, 1] * jnp.exp(stats[:, 0] - top_all[None]), axis=0)
        main_lse, next_lse = jnp.log(sum_all) + top_all
        next_part, next_g = head_bwd(meta, next_all, table_q, next_z, next_lse, targets_of(out_all), MTP_WEIGHT * loss_scale, None)
        d_next = collect(next_part)
        main_part, g_table = head_bwd(meta, main_all, table_q, main_z, main_lse, targets_of(mid_all), loss_scale, next_g)
        d_main = collect(main_part)

        def own(lse):
            return lax.dynamic_slice(lse, (dev_index * n_q,), (n_q,))

        mid_rows = rows_q[:, 1:seq_len + 1].reshape(n_q, hidden).astype(F32)
        out_rows = rows_q[:, 2:seq_len + 2].reshape(n_q, hidden).astype(F32)
        main_pick = jnp.sum(main_q.astype(F32) * mid_rows, axis=-1)
        next_pick = jnp.sum(next_q.astype(F32) * out_rows, axis=-1)
        local_loss = (jnp.sum(own(main_lse) - main_pick) + MTP_WEIGHT * jnp.sum(own(next_lse) - next_pick)) * loss_scale

        d_hid_q, d_rows_q = heads_back((d_main, d_next))
        d_rows_all = lax.all_gather(d_rows_q, both, axis=0, tiled=True)

        look_ids = jnp.concatenate([tok_all[:, 0:seq_len].reshape(-1), mid_all]) - data * v_own
        look_ids = jnp.where(is_first & (look_ids >= 0) & (look_ids < v_own), look_ids, v_own)
        plan = scatter_plan(look_ids, is_first, v_own)
        normed = norm_bf16(acts_all)
        prepared = lax.optimization_barrier((d_hid_q, normed, normed.T, plan))
        d_hid_q, normed, normed_t, plan = prepared
        d_out_all, d_first_all = pipe_bwd(d_hid_q, stage_in, w_in, w_out, n_stages, n_data)
        g_late, d_out_all, d_first_all = lax.optimization_barrier((g_table, d_out_all, d_first_all))
        pieces = [g_table] + [lax.ppermute(g_late[0:VTILE * SHARES[q]], 'pp', [(q, 0)]) for q in range(1, n_stages)]
        d_out_all = d_out_all.reshape(n_all, hidden)
        d_first_all = d_first_all.reshape(n_all, hidden)
        g_in, g_out = stage_wgrad(normed, normed_t, w_in, w_out, d_out_all)

        d_first_all, g_in = lax.optimization_barrier((d_first_all, g_in))
        g_shard = scatter_rows(pieces, v_own, d_first_all, d_rows_all, plan, emb_scale)
        local_loss, _ = lax.optimization_barrier((local_loss, g_shard))
        loss = lax.psum(local_loss, both)
        return loss, g_shard[None], g_in[None, None], g_out[None, None]

    return jax.shard_map(device_body, mesh=mesh, in_specs=(P(None, 'dp', None), P('pp', 'dp', None), P('pp'), P('pp'), P(), P(), P(), P(), P(), P(), P()), out_specs=(P(), P('pp', 'dp', None), P('pp'), P('pp')), check_vma=False)
```

time: 1190 us -> 892 us (0.75)
  Pallas kernels: 40.3 us -> 422 us
  matrix products: 397 us -> 24.8 us
  blocking collectives: 209 us -> 61 us
  waiting for transfers between devices: 294 us -> 169 us
  other arithmetic: 115 us -> 78.5 us
  starting transfers between devices: 63.6 us -> 40.6 us
  local copies, waits for them, and re-layouts: 50.6 us -> 66.3 us
    pallas_call x1 -> x8, Pallas kernels: 40.3 us -> 422 us  [the longest x1 116 us: pipe_bwd(): pl.pallas_call(lambda *refs: pipe_bwd_kernel(n_stages, n_data, *refs), in...]
    dot_general x25 -> x0, matrix products: 372 us -> none  [the longest x14 255 us: dot(): return lax.dot_general(a, b, (dims, ((), ())), preferred_element_type=F32)]
    psum x1, blocking collectives: 171 us -> 32.4 us  [device_body(): loss = lax.psum(local_loss, both)]
    ppermute x6 -> x3, waiting for transfers between devices: 98.9 us -> 0.01 us  [from_first(): mine = mine + lax.ppermute(pieces[q], 'pp', [(0, q)])]
    reduce_scatter x3 -> x2, waiting for transfers between devices: 185 us -> 103 us  [collect(): lax.psum_scatter(partial, both, scatter_dimension=0, tiled=True).astype(BF)]
    ppermute x17 -> x9, waiting for transfers between devices: 9.83 us -> 65.4 us  [the longest x3 39.5 us: device_body(): sent = lax.ppermute(piece(q), 'pp', [(0, q)])]
    concatenate x2 -> x1, other arithmetic: 23.6 us -> 0.56 us  [scatter_plan(): jnp.concatenate([starts, owner.astype(jnp.int32)[None]])]
    ppermute x6 -> x3, starting transfers between devices: 24 us -> 6.03 us  [from_first(): mine = mine + lax.ppermute(pieces[q], 'pp', [(0, q)])]
  transfers between devices with their start and end apart: 32 -> 18, of which waited for: 9 -> 9; matrix products, arithmetic and copies ran while one was open for 28% -> 14% of each run, Pallas kernels for 3% -> 30%
where the time goes in v2:
time: 892 us; the launch traced here: 881 us
  Pallas kernels  422 us (47%)
  waiting for transfers between devices  169 us (19%)
  other arithmetic  78.5 us (9%)
  local copies, waits for them, and re-layouts  66.3 us (7%)
  blocking collectives  61 us (7%)
  starting transfers between devices  40.6 us (5%)
  matrix products  24.8 us (3%)
  between operations  18.3 us (2%)
    pallas_call x1, Pallas kernels, pipe_bwd(): pl.pallas_call(lambda *refs: pipe_bwd_kernel(n_stages, n_data, *refs), in...  116 us
    reduce_scatter x2, waiting for transfers between devices, collect(): lax.psum_scatter(partial, both, scatter_dimension=0, tiled=True).astype(BF)  103 us
    pallas_call x1, Pallas kernels, stage_wgrad(): pl.pallas_call(wgrad_kernel, grid=(ffn // WG_STEP,), in_specs=[vmem, vmem...  91.4 us
    pallas_call x2, Pallas kernels, head_bwd(): pl.pallas_call(lambda *refs: head_bwd_kernel(weight, *refs), grid_spec=pl...  83.5 us
    pallas_call x2, Pallas kernels, head_fwd(): pl.pallas_call(head_fwd_kernel, grid_spec=pltpu.PrefetchScalarGridSpec(nu...  47.6 us
    pallas_call x1, Pallas kernels, scatter_rows(): pl.pallas_call(lambda *refs: scatter_kernel(scale, firsts, *refs), grid_s...  43.3 us
    pallas_call x1, Pallas kernels, pipe_fwd(): pl.pallas_call(lambda *refs: pipe_fwd_kernel(n_stages, *refs), in_specs=[...  40.6 us
    ppermute x3, waiting for transfers between devices, device_body(): sent = lax.ppermute(piece(q), 'pp', [(0, q)])  39.5 us
  transfers between devices with their start and end apart: 18, of which 9 were waited for; matrix products, arithmetic and copies ran while one was open for 14% of the time, Pallas kernels for 30%

profile of v2, /device:TPU:0, one launch (start us, length us, event | category | flops | bytes accessed | tf_op | source)
XLA Modules:
  0.0 881.0 jit_solution(523647854465198311)
XLA Ops:
  7.2 10.1 %all_gather.21 = s32[64,34]{1,0:T(8,128)S(1)} all-gather(s32[16,34]{1,0:T(8,128)} %bitcast.121), channel_id=1, replica_groups=mesh['dp'=4,'pp'=4] {'dp'}, dimensions={0}, use_global_device_ids=true | all-gather | bytes 10880 | tf_op jit(solution)/shard_map/all_gather | solution.py:567
  18.4 21.3 %gather_fusion = bf16[2176,1024]{1,0:T(8,128)(2,1)} fusion(f32[8032,1024]{1,0:T(8,128)} %bitcast.106, s32[3072]{0:T(1024)S(1)} %pad_clamp_fusion), kind=kCustom, calls=%fused_computation | custom fusion | bytes 8921600 | tf_op jit(solution)/shard_map/jit(_take)/gather | solution.py:570
  57.9 6.8 collective-permute-done
  64.7 11.9 %collective-permute-done.2 = bf16[544,1024]{1,0:T(8,128)(2,1)} collective-permute-done((bf16[544,1024]{1,0:T(8,128)(2,1)S(1)}, bf16[544,1024]{1,0:T(8,128)(2,1)}, u32[]{:S(2)}, u32[]{:S(2)}) %collective-permute-start.2) | collective-permute-done | bytes 1114144 | tf_op jit(solution)/shard_map/ppermute | solution.py:576
  89.5 40.6 %pipe_fwd.1 = (bf16[512,1024]{1,0:T(8,128)(2,1)}, bf16[128,1024]{1,0:T(8,128)(2,1)}) custom-call(bf16[512,1024]{1,0:T(8,128)(2,1)} %bitcast.116, bf16[1024,4096]{1,0:T(8,128)(2,1)} %bitcast.124, bf16[4096,1024]{1,0:T(8,128)(2,1)} %bitcast.127), custom_call_target="tpu_custom_call" | custom-call | flops 34359738368 | bytes 16777216 | tf_op jit(solution)/shard_map/pipe_fwd/pallas_call | solution.py:148
  136.8 17.4 %convert.10 = bf16[1,8032,1024]{2,1,0:T(8,128)(2,1)} convert(f32[1,8032,1024]{2,1,0:T(8,128)} %param.15) | non-fusion elementwise | flops 8224768 | bytes 49348608 | tf_op jit(solution)/shard_map/convert.7
  171.3 9.1 %collective-permute-start.6 = (bf16[3072,1024]{1,0:T(8,128)(2,1)}, bf16[3072,1024]{1,0:T(8,128)(2,1)}, u32[]{:S(2)}, u32[]{:S(2)}) collective-permute-start(bf16[3072,1024]{1,0:T(8,128)(2,1)} %slice_bitcast_fusion), channel_id=1, source_target_pairs={{0,1},{4,5},{8,9},{12,13}} | collective-permute-start | bytes 18874376 | tf_op jit(solution)/shard_map/ppermute | solution.py:585
  207.0 10.9 %collective-permute-done.7 = bf16[1024,1024]{1,0:T(8,128)(2,1)} collective-permute-done((bf16[1024,1024]{1,0:T(8,128)(2,1)}, bf16[1024,1024]{1,0:T(8,128)(2,1)}, u32[]{:S(2)}, u32[]{:S(2)}) %collective-permute-start.7) | collective-permute-done | bytes 2097184 | tf_op jit(solution)/shard_map/ppermute | solution.py:585
  218.0 28.6 %collective-permute-done.8 = bf16[1024,1024]{1,0:T(8,128)(2,1)} collective-permute-done((bf16[1024,1024]{1,0:T(8,128)(2,1)}, bf16[1024,1024]{1,0:T(8,128)(2,1)}, u32[]{:S(2)}, u32[]{:S(2)}) %collective-permute-start.8) | collective-permute-done | bytes 2097184 | tf_op jit(solution)/shard_map/ppermute | solution.py:585
  246.5 9.3 %fusion.5.e_ref.refs_2_ = bf16[3072,1024]{1,0:T(8,128)(2,1)} fusion(bf16[3072,1024]{1,0:T(8,128)(2,1)} %collective-permute-done.6, bf16[1,8032,1024]{2,1,0:T(8,128)(2,1)} %convert.10, bf16[1024,1024]{1,0:T(8,128)(2,1)} %collective-permute-done.8, bf16[1024,1024]{1,0:T(8,128)(2,1)} %collective-permute-done.7, pred[]{:T(512)S(6)} %eq.4), kind=kLoop, calls=%fused_computation.11 | loop fusion | flops 28311552 | bytes 23068672 | tf_op jit(solution)/shard_map/add | solution.py:586
  257.2 23.8 %head_fwd.3 = (f32[2048,3072]{1,0:T(8,128)}, f32[2048,128]{1,0:T(8,128)}, f32[2048,128]{1,0:T(8,128)}) custom-call(s32[2]{0:T(128)} %pad_add_fusion.meta.refs_0_, bf16[2048,1024]{1,0:T(8,128)(2,1)} %all-gather.8.cloned.1.call-done.n_ref.refs_1_, bf16[3072,1024]{1,0:T(8,128)(2,1)} %fusion.5.e_ref.refs_2_), custom_call_target="tpu_custom_call" | custom-call | flops 12884901888 | bytes 25165824 | tf_op jit(solution)/shard_map/head_fwd/pallas_call | solution.py:469
  281.1 23.8 %head_fwd.2 = (f32[2048,3072]{1,0:T(8,128)}, f32[2048,128]{1,0:T(8,128)}, f32[2048,128]{1,0:T(8,128)}) custom-call(s32[2]{0:T(128)} %pad_add_fusion.meta.refs_0_, bf16[2048,1024]{1,0:T(8,128)(2,1)} %all-gather.6.cloned.1.call-done.n_ref.refs_1_, bf16[3072,1024]{1,0:T(8,128)(2,1)} %fusion.5.e_ref.refs_2_), custom_call_target="tpu_custom_call" | custom-call | flops 12884901888 | bytes 25165824 | tf_op jit(solution)/shard_map/head_fwd/pallas_call | solution.py:469
  309.9 18.5 %all-gather = f32[32,2,2048]{2,1,0:T(2,128)S(1)} all-gather(f32[2,2,2048]{2,1,0:T(2,128)S(1)} %pad_maximum_fusion.1), channel_id=2, replica_groups=mesh['dp'=4,'pp'=4] {'dp','pp'}, dimensions={0}, use_global_device_ids=true | all-gather | bytes 557056 | tf_op jit(solution)/shard_map/all_gather | solution.py:624
  330.7 40.8 %head_bwd.2 = (f32[2048,1024]{1,0:T(8,128)}, f32[3072,1024]{1,0:T(8,128)}) custom-call(s32[2]{0:T(128)} %pad_add_fusion.meta.refs_0_, bf16[2048,1024]{1,0:T(8,128)(2,1)} %all-gather.8.cloned.1.call-done.n_ref.refs_1_, bf16[3072,1024]{1,0:T(8,128)(2,1)} %fusion.5.e_ref.refs_2_, f32[2048,3072]{1,0:T(8,128)} %get-tuple-element.45.refs_3_, ...), custom_call_target="tpu_custom_call" | custom-call | flops 25769803776 | bytes 25165824 | tf_op jit(solution)/shard_map/head_bwd/pallas_call | solution.py:518
  373.6 42.7 %head_bwd.3 = (f32[2048,1024]{1,0:T(8,128)}, f32[3072,1024]{1,0:T(8,128)}) custom-call(s32[2]{0:T(128)} %pad_add_fusion.meta.refs_0_, bf16[2048,1024]{1,0:T(8,128)(2,1)} %all-gather.6.cloned.1.call-done.n_ref.refs_1_, bf16[3072,1024]{1,0:T(8,128)(2,1)} %fusion.5.e_ref.refs_2_, f32[2048,3072]{1,0:T(8,128)} %get-tuple-element.47.refs_3_, ...), custom_call_target="tpu_custom_call" | custom-call | flops 25769803776 | bytes 25165824 | tf_op jit(solution)/shard_map/head_bwd/pallas_call | solution.py:518
  433.8 30.0 %reduce-scatter.3.cloned.1.call-done = f32[128,1024]{1,0:T(8,128)} async-done(((f32[2048,1024]{1,0:T(8,128)}), f32[128,1024]{1,0:T(8,128)}) %reduce-scatter.3.cloned.1.call-update) | async-done | bytes 524304 | tf_op jit(solution)/shard_map/reduce_scatter | solution.py:611
  466.9 13.0 %multiply_reduce_fusion = (f32[128]{0:T(128)S(1)}, f32[128,1024]{1,0:T(8,128)}) fusion(f32[128,1024]{1,0:T(8,128)S(1)} %copy-done.6, f32[1024]{0:T(1024)S(1)} %copy-done.23, bf16[1024,4096]{1,0:T(8,128)(2,1)} %param.23, f32[128,4096]{1,0:T(8,128)S(1)} %copy-done.13, bf16[128,1024]{1,0:T(8,128)(2,1)S(1)} %fusion.57, bf16[4096,1024]{1,0:T(8,128)(2,1)} %param.24), kind=kOutput, calls=%fused_computation.111 | convolution fusion | flops 2159149056 | bytes 20189696 | tf_op jit(solution)/shard_map/transpose(jvp())/dot_general | solution.py:40
  484.1 73.5 %reduce-scatter.5.cloned.1.call-done = f32[128,1024]{1,0:T(8,128)} async-done(((f32[2048,1024]{1,0:T(8,128)}), f32[128,1024]{1,0:T(8,128)}) %reduce-scatter.5.cloned.1.call-update) | async-done | bytes 524304 | tf_op jit(solution)/shard_map/reduce_scatter | solution.py:611
  561.7 116.0 %pipe_bwd.1 = (bf16[4,4,128,1024]{3,2,1,0:T(8,128)(2,1)}, bf16[4,4,128,1024]{3,2,1,0:T(8,128)(2,1)}) custom-call(bf16[128,1024]{1,0:T(8,128)(2,1)} %fusion.75.refs_0_, bf16[512,1024]{1,0:T(8,128)(2,1)} %get-tuple-element.50.refs_1_, bf16[1024,4096]{1,0:T(8,128)(2,1)} %bitcast.125, bf16[4096,1024]{1,0:T(8,128)(2,1)} %bitcast.128), custom_call_target="tpu_custom_call" | custom-call | flops 51539607552 | bytes 16777216 | tf_op jit(solution)/shard_map/pipe_bwd/pallas_call | solution.py:306
  693.0 6.4 copy.53.n_ref
  699.4 91.4 %stage_wgrad.1 = (f32[1024,4096]{1,0:T(8,128)}, f32[4096,1024]{1,0:T(8,128)}) custom-call(bf16[2048,1024]{1,0:T(8,128)(2,1)} %copy.53.n_ref, bf16[1024,2048]{1,0:T(8,128)(2,1)} %fusion.117.nt_ref, bf16[2048,1024]{1,0:T(8,128)(2,1)} %bitcast.132, bf16[1024,4096]{1,0:T(8,128)(2,1)} %bitcast.126, bf16[4096,1024]{1,0:T(8,128)(2,1)} %bitcast.129), custom_call_target="tpu_custom_call" | custom-call | flops 68719476736 | bytes 50331648 | tf_op jit(solution)/shard_map/stage_wgrad/pallas_call | solution.py:350
  790.8 6.5 collective-permute-done.11.refs_6_
  798.0 43.3 %scatter_rows.1 = f32[8032,1024]{1,0:T(8,128)} custom-call(s32[34]{0:T(128)} %pad_add_fusion.1.refs_0_, s32[4096]{0:T(1024)} %get-tuple-element.54.refs_1_, s32[4096]{0:T(1024)} %get-tuple-element.55.refs_2_, f32[3072,1024]{1,0:T(8,128)} %get-tuple-element.60.refs_3_, f32[3072,1024]{1,0:T(8,128)} %collective-permute-done.9.refs_4_, ...), custom_call_target="tpu_custom_call" | custom-call | tf_op jit(solution)/shard_map/scatter_rows/pallas_call | solution.py:412
  841.4 32.4 %psum.7 = f32[]{:T(128)} all-reduce(f32[]{:T(128)S(6)} %mul.380), channel_id=1, replica_groups=mesh['dp'=4,'pp'=4] {'dp','pp'}, use_global_device_ids=true, to_apply=%region_22.23 | all-reduce | flops 1 | bytes 8 | tf_op jit(solution)/shard_map/psum | solution.py:661
  (220 shorter events, 134.5 us)
Async XLA Ops:
  7.2 248.7 %all-gather.6.cloned.1.call-start = ((), (), s32[]{:S(2)}) async-start(), calls=%async_computation.2 | async-start | bytes 4456448 | tf_op jit(solution)/shard_map/all_gather | solution.py:615
  46.1 18.6 %collective-permute-start = (bf16[544,1024]{1,0:T(8,128)(2,1)}, bf16[544,1024]{1,0:T(8,128)(2,1)S(1)}, u32[]{:S(2)}, u32[]{:S(2)}) collective-permute-start(bf16[544,1024]{1,0:T(8,128)(2,1)} %get-tuple-element.79), channel_id=1, source_target_pairs={{0,4},{4,8},{8,12},{12,0}} | collective-permute-start | bytes 3342344 | tf_op jit(solution)/shard_map/ppermute | solution.py:576
  49.3 27.2 %collective-permute-start.2 = (bf16[544,1024]{1,0:T(8,128)(2,1)S(1)}, bf16[544,1024]{1,0:T(8,128)(2,1)}, u32[]{:S(2)}, u32[]{:S(2)}) collective-permute-start(bf16[544,1024]{1,0:T(8,128)(2,1)S(1)} %get-tuple-element.80), channel_id=1, source_target_pairs={{0,12},{4,0},{8,4},{12,8}} | collective-permute-start | bytes 3342344 | tf_op jit(solution)/shard_map/ppermute | solution.py:576
  52.8 23.8 %collective-permute-start.1 = (bf16[544,1024]{1,0:T(8,128)(2,1)S(1)}, bf16[544,1024]{1,0:T(8,128)(2,1)}, u32[]{:S(2)}, u32[]{:S(2)}) collective-permute-start(bf16[544,1024]{1,0:T(8,128)(2,1)S(1)} %get-tuple-element.81), channel_id=1, source_target_pairs={{0,8},{4,12},{8,0},{12,4}} | collective-permute-start | bytes 3342344 | tf_op jit(solution)/shard_map/ppermute | solution.py:576
  83.5 48.9 %collective-permute-start.4 = (bf16[4,34,1024]{2,1,0:T(8,128)(2,1)}, bf16[4,34,1024]{2,1,0:T(8,128)(2,1)}, u32[]{:S(2)}, u32[]{:S(2)}) collective-permute-start(bf16[4,34,1024]{2,1,0:T(8,128)(2,1)} %slice.77), channel_id=1, source_target_pairs={{0,2},{4,6},{8,10},{12,14}} | collective-permute-start | bytes 835592 | tf_op jit(solution)/shard_map/ppermute | solution.py:544
  85.5 46.9 %collective-permute-start.5 = (bf16[4,34,1024]{2,1,0:T(8,128)(2,1)}, bf16[4,34,1024]{2,1,0:T(8,128)(2,1)}, u32[]{:S(2)}, u32[]{:S(2)}) collective-permute-start(bf16[4,34,1024]{2,1,0:T(8,128)(2,1)} %slice.79), channel_id=1, source_target_pairs={{0,3},{4,7},{8,11},{12,15}} | collective-permute-start | bytes 835592 | tf_op jit(solution)/shard_map/ppermute | solution.py:544
  87.5 44.9 %collective-permute-start.3 = (bf16[4,34,1024]{2,1,0:T(8,128)(2,1)}, bf16[4,34,1024]{2,1,0:T(8,128)(2,1)}, u32[]{:S(2)}, u32[]{:S(2)}) collective-permute-start(bf16[4,34,1024]{2,1,0:T(8,128)(2,1)} %slice.75), channel_id=1, source_target_pairs={{0,1},{4,5},{8,9},{12,13}} | collective-permute-start | bytes 835592 | tf_op jit(solution)/shard_map/ppermute | solution.py:544
  136.8 119.1 %all-gather.8.cloned.1.call-start = ((), (), s32[]{:S(2)}) async-start(), calls=%async_computation.3 | async-start | bytes 4456448 | tf_op jit(solution)/shard_map/all_gather | solution.py:616
  164.9 259.0 %all-gather.10.cloned.1.call-start = ((), (), s32[]{:S(2)}) async-start(), calls=%async_computation.6 | async-start | bytes 5242880 | tf_op jit(solution)/shard_map/all_gather | solution.py:618
  171.3 75.2 %collective-permute-start.6 = (bf16[3072,1024]{1,0:T(8,128)(2,1)}, bf16[3072,1024]{1,0:T(8,128)(2,1)}, u32[]{:S(2)}, u32[]{:S(2)}) collective-permute-start(bf16[3072,1024]{1,0:T(8,128)(2,1)} %slice_bitcast_fusion), channel_id=1, source_target_pairs={{0,1},{4,5},{8,9},{12,13}} | collective-permute-start | bytes 18874376 | tf_op jit(solution)/shard_map/ppermute | solution.py:585
  183.5 34.5 %collective-permute-start.7 = (bf16[1024,1024]{1,0:T(8,128)(2,1)}, bf16[1024,1024]{1,0:T(8,128)(2,1)}, u32[]{:S(2)}, u32[]{:S(2)}) collective-permute-start(bf16[1024,1024]{1,0:T(8,128)(2,1)} %slice_bitcast_fusion.1), channel_id=1, source_target_pairs={{0,2},{4,6},{8,10},{12,14}} | collective-permute-start | bytes 6291464 | tf_op jit(solution)/shard_map/ppermute | solution.py:585
  191.6 55.0 %collective-permute-start.8 = (bf16[1024,1024]{1,0:T(8,128)(2,1)}, bf16[1024,1024]{1,0:T(8,128)(2,1)}, u32[]{:S(2)}, u32[]{:S(2)}) collective-permute-start(bf16[1024,1024]{1,0:T(8,128)(2,1)} %pad.12), channel_id=1, source_target_pairs={{0,3},{4,7},{8,11},{12,15}} | collective-permute-start | bytes 6291464 | tf_op jit(solution)/shard_map/ppermute | solution.py:585
  257.2 206.6 %reduce-scatter.3.cloned.1.call-start = ((), (), s32[]{:S(2)}) async-start(), calls=%async_computation.4 | async-start | bytes 8912896 | tf_op jit(solution)/shard_map/reduce_scatter | solution.py:611
  371.6 186.1 %reduce-scatter.5.cloned.1.call-start = ((), (), s32[]{:S(2)}) async-start(), calls=%async_computation.5 | async-start | bytes 8912896 | tf_op jit(solution)/shard_map/reduce_scatter | solution.py:611
  416.3 381.7 %all-gather.12.cloned.1.call-start = ((), (), s32[]{:S(2)}) async-start(), calls=%async_computation.7 | async-start | bytes 4456448 | tf_op jit(solution)/shard_map/all_gather | solution.py:643
  479.9 77.7 %copy-start.4 = (bf16[4,34,1024]{2,1,0:T(8,128)(2,1)S(1)}, bf16[4,34,1024]{2,1,0:T(8,128)(2,1)}, u32[]{:S(2)}) copy-start(bf16[4,34,1024]{2,1,0:T(8,128)(2,1)} %copy-done.3) | copy-start | bytes 835588
  479.9 77.7 %copy-start.11 = (bf16[128,1024]{1,0:T(8,128)(2,1)S(1)}, bf16[128,1024]{1,0:T(8,128)(2,1)}, u32[]{:S(2)}) copy-start(bf16[128,1024]{1,0:T(8,128)(2,1)} %get-tuple-element.38) | copy-start | bytes 786436
  479.9 77.7 %copy-start.24 = (f32[1024]{0:T(1024)S(1)}, f32[1024]{0:T(1024)}, u32[]{:S(2)}) copy-start(f32[1024]{0:T(1024)} %convert_element_type.186) | copy-start | bytes 12292
  479.9 77.7 %copy-start.25 = (f32[1024]{0:T(1024)S(1)}, f32[1024]{0:T(1024)}, u32[]{:S(2)}) copy-start(f32[1024]{0:T(1024)} %convert_element_type.179) | copy-start | bytes 12292
  479.9 79.7 %copy-start.32 = (f32[128]{0:T(128)S(1)}, f32[128]{0:T(128)}, u32[]{:S(2)}) copy-start(f32[128]{0:T(128)} %copy-done.31) | copy-start | bytes 1540
  480.0 79.7 %copy-start.38 = (f32[128]{0:T(128)S(1)}, f32[128]{0:T(128)}, u32[]{:S(2)}) copy-start(f32[128]{0:T(128)} %copy-done.37) | copy-start | bytes 1540
  677.7 120.3 %collective-permute-start.9 = (f32[3072,1024]{1,0:T(8,128)}, f32[3072,1024]{1,0:T(8,128)}, u32[]{:S(2)}, u32[]{:S(2)}) collective-permute-start(f32[3072,1024]{1,0:T(8,128)} %get-tuple-element.60.refs_3_), channel_id=1, source_target_pairs={{1,0},{5,4},{9,8},{13,12}} | collective-permute-start | bytes 37748744 | tf_op jit(solution)/shard_map/ppermute | solution.py:653
  690.4 106.9 %collective-permute-start.11 = (f32[1024,1024]{1,0:T(8,128)}, f32[1024,1024]{1,0:T(8,128)}, u32[]{:S(2)}, u32[]{:S(2)}) collective-permute-start(f32[1024,1024]{1,0:T(8,128)} %slice.91), channel_id=1, source_target_pairs={{3,0},{7,4},{11,8},{15,12}} | collective-permute-start | bytes 12582920 | tf_op jit(solution)/shard_map/ppermute | solution.py:653
  691.7 106.4 %collective-permute-start.10 = (f32[1024,1024]{1,0:T(8,128)}, f32[1024,1024]{1,0:T(8,128)}, u32[]{:S(2)}, u32[]{:S(2)}) collective-permute-start(f32[1024,1024]{1,0:T(8,128)} %slice.91), channel_id=1, source_target_pairs={{2,0},{6,4},{10,8},{14,12}} | collective-permute-start | bytes 12582920 | tf_op jit(solution)/shard_map/ppermute | solution.py:653
  (44 other events, 617.1 us)
Sparse Core Ops, SparseCore 0:
  136.9 50.0 all-gather.5
  189.2 37.9 all-gather.7
  257.3 54.3 all-gather.9
  371.7 92.0 reduce-scatter.2
  466.4 91.1 reduce-scatter.4
  681.8 52.3 all-gather.11

commit v3 on v2

--- a/solution.py
+++ b/solution.py
@@ -44,7 +44,7 @@
 
 MESH = pl.DeviceIdType.MESH
 VMEM_LIMIT = 64 * 1024 * 1024 - 65536
-FF_STEP = 512
+FF_STEP = 2048
 WG_STEP = 512
 WG_ROWS = 512
 TILE = 256
@@ -170,7 +170,7 @@
 
 
 def pipe_bwd_kernel(n_stages, n_data, top_ref, acts_ref, wi_hbm, wo_hbm, dall_hbm, fall_hbm, wi, wo, slope, top, dall, fall, acc,
-                    w_sem, csend, crecv, tsend, trecv, gsend, grecv, fsend, frecv, o_sem):
+                    w_sem, csend, crecv, tsend, trecv, gsend, grecv, o_sem):
     stage = lax.axis_index('pp')
     data = lax.axis_index('dp')
     last = n_stages - 1
@@ -190,7 +190,7 @@
 
     def back(c):
         return pltpu.make_async_remote_copy(
-            src_ref=fall.at[data, c], dst_ref=dall.at[data, c], send_sem=csend.at[c], recv_sem=crecv.at[c],
+            src_ref=fall.at[c], dst_ref=dall.at[data, c], send_sem=csend.at[c], recv_sem=crecv.at[c],
             device_id=(data, lax.rem(stage + last, n_stages)), device_id_type=MESH)
 
     def share(buf, owner, k, c, send_sem, recv_sem):
@@ -248,7 +248,7 @@
         scale = lax.rsqrt(jnp.mean(acts * acts, axis=-1, keepdims=True) + EPS)
         inner_mean = jnp.mean(d_norm * acts, axis=-1, keepdims=True)
         d_acts = (d_norm * scale - acts * (scale * scale * scale * inner_mean)).astype(BF)
-        fall[data, c] = (d_out.astype(F32) + d_acts.astype(F32)).astype(BF)
+        fall[c] = (d_out.astype(F32) + d_acts.astype(F32)).astype(BF)
 
         @pl.when(stage > 0)
         def _():
@@ -256,11 +256,6 @@
 
         for k in range(1, n_data):
             share(dall, data, k, c, gsend, grecv).start()
-
-        @pl.when(stage == 0)
-        def _():
-            for k in range(1, n_data):
-                share(fall, data, k, c, fsend, frecv).start()
 
         return carry
 
@@ -282,16 +277,9 @@
     save = pltpu.make_async_copy(dall, dall_hbm, o_sem.at[0])
     save.start()
 
-    @pl.when(stage == 0)
-    def _():
-        for k in range(1, n_data):
-            for c in range(n_stages):
-                share(fall, data, k, c, fsend, frecv).wait_send()
-                share(fall, lax.rem(data + n_data - k, n_data), k, c, fsend, frecv).wait_recv()
-        save_first = pltpu.make_async_copy(fall, fall_hbm, o_sem.at[1])
-        save_first.start()
-        save_first.wait()
-
+    save_first = pltpu.make_async_copy(fall, fall_hbm, o_sem.at[1])
+    save_first.start()
+    save_first.wait()
     save.wait()
 
 
@@ -307,17 +295,16 @@
         lambda *refs: pipe_bwd_kernel(n_stages, n_data, *refs),
         in_specs=[vmem, vmem, hbm, hbm],
         out_specs=[hbm, hbm],
-        out_shape=[jax.ShapeDtypeStruct(full, BF), jax.ShapeDtypeStruct(full, BF)],
+        out_shape=[jax.ShapeDtypeStruct(full, BF), jax.ShapeDtypeStruct(full[1:], BF)],
         scratch_shapes=[
             pltpu.VMEM((hidden, ffn), BF),
             pltpu.VMEM((ffn, hidden), BF),
             pltpu.VMEM((n_tok, ffn), F32),
             pltpu.VMEM((n_stages, chunk, hidden), BF),
             pltpu.VMEM(full, BF),
-            pltpu.VMEM(full, BF),
+            pltpu.VMEM(full[1:], BF),
             pltpu.VMEM((chunk, hidden), F32),
             dma((2,)), dma((n_stages,)), dma((n_stages,)), dma, dma((n_stages,)),
-            dma((n_data - 1, n_stages)), dma((n_data - 1, n_stages)),
             dma((n_data - 1, n_stages)), dma((n_data - 1, n_stages)), dma((2,)),
         ],
         compiler_params=pltpu.CompilerParams(collective_id=1, has_side_effects=True, vmem_limit_bytes=VMEM_LIMIT),
@@ -481,9 +468,16 @@
     )(meta, norm_all, table_q)
 
 
-def head_bwd_kernel(weight, meta, n_ref, e_ref, z_ref, lse_ref, tgt_ref, *refs):
-    prev_ref = refs[0] if len(refs) == 4 else None
-    dn_ref, de_ref, grad = refs[-3:]
+def softmax_grad(z, lse, column, target, weight):
+    prob = jnp.exp(z - lse)
+    return (jnp.where(column == target, prob - 1.0, prob) * weight).astype(BF)
+
+
+def tile_columns(tile):
+    return tile * VTILE + lax.broadcasted_iota(jnp.int32, (ROWS, VTILE), 1)
+
+
+def head_bwd_kernel(weight, meta, e_ref, z_ref, lse_ref, tgt_ref, dn_ref):
     tile = pl.program_id(0)
 
     @pl.when(tile == 0)
@@ -492,43 +486,185 @@
 
     @pl.when(tile < meta[0])
     def _():
-        column = tile * VTILE + lax.broadcasted_iota(jnp.int32, (ROWS, VTILE), 1)
-
-        def block(b, carry):
-            rows = pl.ds(pl.multiple_of(b * ROWS, ROWS), ROWS)
-            prob = jnp.exp(z_ref[rows, :] - lse_ref[rows, :])
-            hit = column == tgt_ref[rows, :]
-            g = (jnp.where(hit, prob - 1.0, prob) * weight).astype(BF)
-            grad[rows, :] = g
+        column = tile_columns(tile)
+        for b in range(dn_ref.shape[0] // ROWS):
+            rows = slice(b * ROWS, (b + 1) * ROWS)
+            g = softmax_grad(z_ref[rows, :], lse_ref[rows, 1:2], column, tgt_ref[rows, 1:2], weight)
             dn_ref[rows, :] += jnp.dot(g, e_ref[...], preferred_element_type=F32)
-            return carry
-
-        lax.fori_loop(0, n_ref.shape[0] // ROWS, block, 0, unroll=True)
-        de = dot(grad[...], n_ref[...], ((0,), (0,)))
-        de_ref[...] = de if prev_ref is None else de + prev_ref[...]
-
-
-def head_bwd(meta, norm_all, table_q, z, lse, targets, weight, prev):
-    n_all, hidden = norm_all.shape
+
+
+def head_bwd(meta, table_q, z, lse, targets, weight):
+    n_all = z.shape[0]
+    hidden = table_q.shape[1]
     tiles = table_q.shape[0] // VTILE
     vmem = pl.BlockSpec(memory_space=pltpu.VMEM)
     vrows = pl.BlockSpec((VTILE, hidden), lambda i, meta: (jnp.minimum(i, meta[0] - 1), 0))
     vcols = pl.BlockSpec((n_all, VTILE), lambda i, meta: (0, jnp.minimum(i, meta[0] - 1)))
-    extra = [] if prev is None else [prev]
     return pl.pallas_call(
         lambda *refs: head_bwd_kernel(weight, *refs),
         grid_spec=pltpu.PrefetchScalarGridSpec(
             num_scalar_prefetch=1,
             grid=(tiles,),
-            in_specs=[vmem, vrows, vcols, vmem, vmem] + [vrows] * len(extra),
-            out_specs=[vmem, vrows],
-            scratch_shapes=[pltpu.VMEM((n_all, VTILE), BF)],
+            in_specs=[vrows, vcols, vmem, vmem],
+            out_specs=vmem,
         ),
-        out_shape=[jax.ShapeDtypeStruct((n_all, hidden), F32), jax.ShapeDtypeStruct(table_q.shape, F32)],
+        out_shape=jax.ShapeDtypeStruct((n_all, hidden), F32),
         compiler_params=pltpu.CompilerParams(vmem_limit_bytes=VMEM_LIMIT),
-        cost_estimate=pl.CostEstimate(flops=4 * n_all * hidden * tiles * VTILE, bytes_accessed=4 * n_all * tiles * VTILE, transcendentals=n_all * tiles * VTILE),
+        cost_estimate=pl.CostEstimate(flops=2 * n_all * hidden * tiles * VTILE, bytes_accessed=4 * n_all * tiles * VTILE, transcendentals=n_all * tiles * VTILE),
         name='head_bwd',
-    )(meta, norm_all, table_q, z, lse[:, None], targets[:, None], *extra)
+    )(meta, table_q, z, lse, targets)
+
+
+def head_reduce_kernel(weights, n_stages, n_data, nm_ref, nn_ref, e_ref, zm_ref, zn_ref, lse_ref, tgt_ref, other_hbm,
+                       de_ref, d_other_ref, d_mine_ref, dn, grad, pair, half_a, slot_a, slot_b,
+                       l_sem, psend, precv, asend, arecv, credit):
+    step_id = pl.program_id(0)
+    tiles = max(SHARES)
+    tile = lax.rem(step_id, tiles)
+    stage = lax.axis_index('pp')
+    data = lax.axis_index('dp')
+    core = lax.rem(stage, 2)
+    half_stage = lax.div(stage, 2)
+    per = n_stages // 2
+    count = n_data * per
+    me = data * per + half_stage
+    n_q = pair.shape[1]
+    mate = (data, half_stage * 2 + 1 - core)
+
+    def device(j):
+        return (lax.div(j, per), lax.rem(j, per) * 2 + core)
+
+    def block_of(j, side):
+        return lax.div(j, per) * n_stages + lax.rem(j, per) * 2 + side
+
+    def to_mate(src, phase, j):
+        return pltpu.make_async_remote_copy(
+            src_ref=src.at[block_of(j, 1 - core)], dst_ref=pair.at[j], send_sem=psend.at[phase, j], recv_sem=precv.at[phase, j],
+            device_id=mate, device_id_type=MESH)
+
+    def load_own(j):
+        return pltpu.make_async_copy(other_hbm.at[block_of(j, core)], half_a.at[j], l_sem.at[j])
+
+    def to_owner(src, dst, phase, step):
+        return pltpu.make_async_remote_copy(
+            src_ref=src, dst_ref=dst.at[step - 1], send_sem=asend.at[phase, step - 1], recv_sem=arecv.at[phase, step - 1],
+            device_id=device(lax.rem(me + step, count)), device_id_type=MESH)
+
+    def send_a(step):
+        return to_owner(half_a.at[lax.rem(me + step, count)], slot_a, 0, step)
+
+    def send_b(step):
+        return to_owner(dn.at[block_of(lax.rem(me + step, count), core)], slot_b, 1, step)
+
+    @pl.when(step_id == 0)
+    def _():
+        greet([mate] + [device(lax.rem(me + step, count)) for step in range(1, count)])
+        for j in range(count):
+            to_mate(other_hbm, 0, j).start()
+            load_own(j).start()
+        dn[...] = jnp.zeros_like(dn)
+
+    @pl.when(step_id == 1)
+    def _():
+        for j in range(count):
+            load_own(j).wait()
+            to_mate(other_hbm, 0, j).wait()
+        half_a[...] += pair[...]
+        pl.semaphore_signal(credit, inc=1, device_id=mate, device_id_type=MESH)
+        for step in range(1, count):
+            send_a(step).start()
+
+    @pl.when(step_id == tiles)
+    def _():
+        for j in range(count):
+            to_mate(dn, 1, j).wait()
+        for j in range(count):
+            dn[block_of(j, core)] += pair[j]
+        for step in range(1, count):
+            send_b(step).start()
+
+    active = tile < SHARES[0] - (SHARES[0] - SHARES[2]) * half_stage
+    n_blocks = nm_ref.shape[0] // ROWS
+
+    @pl.when(active & (step_id < tiles))
+    def _():
+        column = tile_columns(tile)
+        per_block = ROWS // n_q
+        for b in range(n_blocks):
+            rows = slice(b * ROWS, (b + 1) * ROWS)
+            g = softmax_grad(zm_ref[rows, :], lse_ref[rows, 0:1], column, tgt_ref[rows, 0:1], weights[0])
+            part = jnp.dot(g, e_ref[...], preferred_element_type=F32)
+            dn[b * per_block:(b + 1) * per_block] += part.reshape(per_block, n_q, part.shape[1])
+
+    @pl.when(active & (step_id >= tiles))
+    def _():
+        column = tile_columns(tile)
+        for head, (n_ref, z_ref) in enumerate(((nm_ref, zm_ref), (nn_ref, zn_ref))):
+            cols = slice(head, head + 1)
+            for b in range(n_blocks):
+                rows = slice(b * ROWS, (b + 1) * ROWS)
+                grad[rows, :] = softmax_grad(z_ref[rows, :], lse_ref[rows, cols], column, tgt_ref[rows, cols], weights[head])
+            de = dot(grad[...], n_ref[...], ((0,), (0,)))
+            if head == 0:
+                de_ref[...] = de
+            else:
+                de_ref[...] += de
+
+    @pl.when(step_id == tiles - 1)
+    def _():
+        pl.semaphore_wait(credit, 1)
+        for j in range(count):
+            to_mate(dn, 1, j).start()
+
+    @pl.when(step_id == 2 * tiles - 1)
+    def _():
+        total = half_a[me]
+        for step in range(1, count):
+            send_a(step).wait()
+            total = total + slot_a[step - 1]
+        d_other_ref[...] = total
+        total = dn[block_of(me, core)]
+        for step in range(1, count):
+            send_b(step).wait()
+            total = total + slot_b[step - 1]
+        d_mine_ref[...] = total
+
+
+def head_reduce(norms, table_q, zs, lse, targets, weights, other, n_stages, n_data):
+    n_all, hidden = norms[0].shape
+    tiles = table_q.shape[0] // VTILE
+    n_dev = n_stages * n_data
+    n_q = n_all // n_dev
+    half = n_dev // 2
+    vmem = pl.BlockSpec(memory_space=pltpu.VMEM)
+    single = pl.Buffered(1)
+    dma = pltpu.SemaphoreType.DMA
+    return pl.pallas_call(
+        lambda *refs: head_reduce_kernel(weights, n_stages, n_data, *refs),
+        grid=(2 * tiles,),
+        in_specs=[
+            vmem, vmem,
+            pl.BlockSpec((VTILE, hidden), lambda i: (jnp.minimum(i, tiles - 1), 0), pipeline_mode=single),
+            pl.BlockSpec((n_all, VTILE), lambda i: (0, lax.rem(i, tiles))),
+            pl.BlockSpec((n_all, VTILE), lambda i: (0, jnp.maximum(i - tiles, 0)), pipeline_mode=single),
+            vmem, vmem, pl.BlockSpec(memory_space=pl.ANY),
+        ],
+        out_specs=[pl.BlockSpec((VTILE, hidden), lambda i: (jnp.maximum(i - tiles, 0), 0)), vmem, vmem],
+        out_shape=[jax.ShapeDtypeStruct(table_q.shape, F32)] + [jax.ShapeDtypeStruct((n_q, hidden), F32)] * 2,
+        scratch_shapes=[
+            pltpu.VMEM((n_dev, n_q, hidden), F32),
+            pltpu.VMEM((n_all, VTILE), BF),
+            pltpu.VMEM((half, n_q, hidden), F32),
+            pltpu.VMEM((half, n_q, hidden), F32),
+            pltpu.VMEM((half - 1, n_q, hidden), F32),
+            pltpu.VMEM((half - 1, n_q, hidden), F32),
+            dma((half,)), dma((2, half)), dma((2, half)), dma((2, half - 1)), dma((2, half - 1)),
+            pltpu.SemaphoreType.REGULAR,
+        ],
+        compiler_params=pltpu.CompilerParams(collective_id=2, has_side_effects=True, vmem_limit_bytes=VMEM_LIMIT),
+        cost_estimate=pl.CostEstimate(flops=6 * n_all * hidden * tiles * VTILE, bytes_accessed=12 * n_all * tiles * VTILE, transcendentals=3 * n_all * tiles * VTILE),
+        name='head_reduce',
+    )(*norms, table_q, *zs, lse, targets, other.reshape(n_dev, n_q, hidden))
 
 
 def solution(mesh):
@@ -576,18 +712,19 @@
             rows = rows + lax.ppermute(outgoing, both, pairs)
         rows = rows.reshape(n_seq, width, hidden)
 
-        def piece(q):
-            part = table[firsts[q]:min(firsts[q + 1], v_own)].astype(BF)
+        def piece(q, source):
+            part = source[firsts[q]:min(firsts[q + 1], v_own)].astype(BF)
             return jnp.pad(part, ((0, VTILE * SHARES[q] - part.shape[0]), (0, 0)))
 
-        table_q = jnp.where(is_first, piece(0), 0)
-        for q in range(1, n_stages):
-            sent = lax.ppermute(piece(q), 'pp', [(0, q)])
-            table_q = table_q + jnp.pad(sent, ((0, v_dev - sent.shape[0]), (0, 0)))
+        far = [lax.ppermute(piece(q, table), 'pp', [(0, q)]) for q in range(2, n_stages)]
         rows_q = from_first([rows[q * q_seq:(q + 1) * q_seq] for q in range(n_stages)], stage)
 
         first_in = (rows[:, 0:seq_len].astype(F32) * emb_scale).astype(BF).reshape(n_own, hidden)
         stage_in, hid_q = pipe_fwd(first_in, w_in, w_out, n_stages)
+        table_late, stage_in = lax.optimization_barrier((table, stage_in))
+        table_q = jnp.where(is_first, piece(0, table_late), 0)
+        for sent in [lax.ppermute(piece(1, table_late), 'pp', [(0, 1)])] + far:
+            table_q = table_q + jnp.pad(sent, ((0, v_dev - sent.shape[0]), (0, 0)))
         mtp_rows = (rows_q[:, 1:seq_len + 1].astype(F32) * emb_scale).astype(BF).reshape(n_q, hidden)
 
         def heads(hid, mtp):
@@ -595,7 +732,6 @@
 
         (main_q, next_q), heads_back = jax.vjp(heads, hid_q, mtp_rows)
 
-        dev_index = data * n_stages + stage
         shard_first = jnp.asarray(firsts[:-1], jnp.int32)[stage]
         shard_last = jnp.minimum(jnp.asarray(firsts[1:], jnp.int32)[stage], v_own)
         valid = shard_last - shard_first
@@ -607,37 +743,38 @@
 
         data_base = data * v_own + shard_first
 
-        def collect(partial):
-            return lax.psum_scatter(partial, both, scatter_dimension=0, tiled=True).astype(BF)
-
         mid_all = tok_all[:, 1:seq_len + 1].reshape(n_all)
         out_all = tok_all[:, 2:seq_len + 2].reshape(n_all)
         main_all = lax.all_gather(main_q, both, axis=0, tiled=True)
         next_all = lax.all_gather(next_q, both, axis=0, tiled=True)
-        stage_in_late, main_all, next_all = lax.optimization_barrier((stage_in, main_all, next_all))
+        stage_in_late, next_all = lax.optimization_barrier((stage_in, next_all))
         acts_all = lax.all_gather(stage_in_late, 'dp', axis=0, tiled=True)
         main_z, main_top, main_sum = head_fwd(meta, main_all, table_q)
         next_z, next_top, next_sum = head_fwd(meta, next_all, table_q)
         lane_top = jnp.stack([main_top, next_top])
         top = jnp.max(lane_top, axis=-1)
         total = jnp.sum(jnp.stack([main_sum, next_sum]) * jnp.exp(lane_top - top[..., None]), axis=-1)
-        stats = lax.all_gather(jnp.stack([top, total]), both, axis=0)
-        top_all = jnp.max(stats[:, 0], axis=0)
-        sum_all = jnp.sum(stats[:, 1] * jnp.exp(stats[:, 0] - top_all[None]), axis=0)
-        main_lse, next_lse = jnp.log(sum_all) + top_all
-        next_part, next_g = head_bwd(meta, next_all, table_q, next_z, next_lse, targets_of(out_all), MTP_WEIGHT * loss_scale, None)
-        d_next = collect(next_part)
-        main_part, g_table = head_bwd(meta, main_all, table_q, main_z, main_lse, targets_of(mid_all), loss_scale, next_g)
-        d_main = collect(main_part)
-
-        def own(lse):
-            return lax.dynamic_slice(lse, (dev_index * n_q,), (n_q,))
-
         mid_rows = rows_q[:, 1:seq_len + 1].reshape(n_q, hidden).astype(F32)
         out_rows = rows_q[:, 2:seq_len + 2].reshape(n_q, hidden).astype(F32)
         main_pick = jnp.sum(main_q.astype(F32) * mid_rows, axis=-1)
         next_pick = jnp.sum(next_q.astype(F32) * out_rows, axis=-1)
-        local_loss = (jnp.sum(own(main_lse) - main_pick) + MTP_WEIGHT * jnp.sum(own(next_lse) - next_pick)) * loss_scale
+        packed = jnp.concatenate([top.reshape(-1), total.reshape(-1), main_pick, next_pick])
+        packed = lax.all_gather(packed, both, axis=0)
+        n_dev = n_stages * n_data
+        stats = packed[:, :4 * n_all].reshape(n_dev, 2, 2, n_all)
+        picks = packed[:, 4 * n_all:].reshape(n_dev, 2, n_q)
+        top_all = jnp.max(stats[:, 0], axis=0)
+        sum_all = jnp.sum(stats[:, 1] * jnp.exp(stats[:, 0] - top_all[None]), axis=0)
+        main_lse, next_lse = jnp.log(sum_all) + top_all
+        terms = jnp.sum(jnp.stack([main_lse, next_lse]), axis=-1) - jnp.sum(picks, axis=(0, 2))
+        loss = (terms[0] + MTP_WEIGHT * terms[1]) * loss_scale
+        lse_cols = jnp.stack([main_lse, next_lse], axis=-1)
+        target_cols = jnp.stack([targets_of(mid_all), targets_of(out_all)], axis=-1)
+        weights = (loss_scale, MTP_WEIGHT * loss_scale)
+        next_part = head_bwd(meta, table_q, next_z, lse_cols, target_cols, weights[1])
+        g_table, d_next, d_main = head_reduce((main_all, next_all), table_q, (main_z, next_z), lse_cols, target_cols, weights, next_part, n_stages, n_data)
+        d_next = d_next.astype(BF)
+        d_main = d_main.astype(BF)
 
         d_hid_q, d_rows_q = heads_back((d_main, d_next))
         d_rows_all = lax.all_gather(d_rows_q, both, axis=0, tiled=True)
@@ -652,13 +789,11 @@
         g_late, d_out_all, d_first_all = lax.optimization_barrier((g_table, d_out_all, d_first_all))
         pieces = [g_table] + [lax.ppermute(g_late[0:VTILE * SHARES[q]], 'pp', [(q, 0)]) for q in range(1, n_stages)]
         d_out_all = d_out_all.reshape(n_all, hidden)
-        d_first_all = d_first_all.reshape(n_all, hidden)
+        d_first_all = lax.all_gather(d_first_all.reshape(n_own, hidden), 'dp', axis=0, tiled=True)
         g_in, g_out = stage_wgrad(normed, normed_t, w_in, w_out, d_out_all)
 
         d_first_all, g_in = lax.optimization_barrier((d_first_all, g_in))
         g_shard = scatter_rows(pieces, v_own, d_first_all, d_rows_all, plan, emb_scale)
-        local_loss, _ = lax.optimization_barrier((local_loss, g_shard))
-        loss = lax.psum(local_loss, both)
         return loss, g_shard[None], g_in[None, None], g_out[None, None]
 
     return jax.shard_map(device_body, mesh=mesh, in_specs=(P(None, 'dp', None), P('pp', 'dp', None), P('pp'), P('pp'), P(), P(), P(), P(), P(), P(), P()), out_specs=(P(), P('pp', 'dp', None), P('pp'), P('pp')), check_vma=False)

time: 892 us -> 788 us (0.88)
  waiting for transfers between devices: 169 us -> 67.4 us
  Pallas kernels: 422 us -> 463 us
  blocking collectives: 61 us -> 27.9 us
  local copies, waits for them, and re-layouts: 66.3 us -> 57.1 us
    pallas_call x0 -> x1, Pallas kernels: none -> 127 us  [head_reduce(): pl.pallas_call(lambda *refs: head_reduce_kernel(weights, n_stages, n_data...]
    reduce_scatter x2 -> x0, waiting for transfers between devices: 103 us -> none  [collect(): lax.psum_scatter(partial, both, scatter_dimension=0, tiled=True).astype(BF)]
    pallas_call x2 -> x1, Pallas kernels: 83.5 us -> 24.6 us  [head_bwd(): pl.pallas_call(lambda *refs: head_bwd_kernel(weight, *refs), grid_spec=pl...]
    psum x1 -> x0, blocking collectives: 32.4 us -> none  [device_body(): loss = lax.psum(local_loss, both)]
    pallas_call x1, Pallas kernels: 116 us -> 95.1 us  [pipe_bwd(): pl.pallas_call(lambda *refs: pipe_bwd_kernel(n_stages, n_data, *refs), in...]
    convert_element_type x3 -> x2, local copies, waits for them, and re-layouts: 11.1 us -> 1.64 us  [piece(): part = source[firsts[q]:min(firsts[q + 1], v_own)].astype(BF)]
    another operation x2 -> x4, other arithmetic: 17.4 us -> 23.9 us
  transfers between devices with their start and end apart: 18 -> 17, of which waited for: 9 -> 7; matrix products, arithmetic and copies ran while one was open for 14% -> 13% of each run, Pallas kernels for 30% -> 42%
where the time goes in v3:
time: 788 us; the launch traced here: 777 us
  Pallas kernels  463 us (59%)
  other arithmetic  80.7 us (10%)
  waiting for transfers between devices  67.4 us (9%)
  local copies, waits for them, and re-layouts  57.1 us (7%)
  starting transfers between devices  36 us (5%)
  blocking collectives  27.9 us (4%)
  matrix products  26.1 us (3%)
  between operations  19.4 us (2%)
    pallas_call x1, Pallas kernels, head_reduce(): pl.pallas_call(lambda *refs: head_reduce_kernel(weights, n_stages, n_data...  127 us
    pallas_call x1, Pallas kernels, pipe_bwd(): pl.pallas_call(lambda *refs: pipe_bwd_kernel(n_stages, n_data, *refs), in...  95.1 us
    pallas_call x1, Pallas kernels, stage_wgrad(): pl.pallas_call(wgrad_kernel, grid=(ffn // WG_STEP,), in_specs=[vmem, vmem...  91.9 us
    pallas_call x2, Pallas kernels, head_fwd(): pl.pallas_call(head_fwd_kernel, grid_spec=pltpu.PrefetchScalarGridSpec(nu...  47.6 us
    pallas_call x1, Pallas kernels, scatter_rows(): pl.pallas_call(lambda *refs: scatter_kernel(scale, firsts, *refs), grid_s...  43.3 us
    ppermute x2, waiting for transfers between devices, device_body(): lax.ppermute(piece(q, table), 'pp', [(0, q)])  41.4 us
    pallas_call x1, Pallas kernels, pipe_fwd(): pl.pallas_call(lambda *refs: pipe_fwd_kernel(n_stages, *refs), in_specs=[...  32.8 us
    pallas_call x1, Pallas kernels, head_bwd(): pl.pallas_call(lambda *refs: head_bwd_kernel(weight, *refs), grid_spec=pl...  24.6 us
  transfers between devices with their start and end apart: 17, of which 7 were waited for; matrix products, arithmetic and copies ran while one was open for 13% of the time, Pallas kernels for 42%

profile of v3, /device:TPU:0, one launch (start us, length us, event | category | flops | bytes accessed | tf_op | source)
XLA Modules:
  0.0 777.3 jit_solution(1448403142356476682)
XLA Ops:
  7.2 10.1 %all_gather.24 = s32[64,34]{1,0:T(8,128)S(1)} all-gather(s32[16,34]{1,0:T(8,128)} %bitcast.110), channel_id=1, replica_groups=mesh['dp'=4,'pp'=4] {'dp'}, dimensions={0}, use_global_device_ids=true | all-gather | bytes 10880 | tf_op jit(solution)/shard_map/all_gather | solution.py:703
  18.4 21.3 %gather_fusion = bf16[2176,1024]{1,0:T(8,128)(2,1)} fusion(f32[8032,1024]{1,0:T(8,128)} %bitcast.92, s32[3072]{0:T(1024)S(1)} %pad_clamp_fusion), kind=kCustom, calls=%fused_computation | custom fusion | bytes 8921600 | tf_op jit(solution)/shard_map/jit(_take)/gather | solution.py:706
  57.5 6.2 collective-permute-done
  63.7 11.9 %collective-permute-done.2 = bf16[544,1024]{1,0:T(8,128)(2,1)} collective-permute-done((bf16[544,1024]{1,0:T(8,128)(2,1)S(1)}, bf16[544,1024]{1,0:T(8,128)(2,1)}, u32[]{:S(2)}, u32[]{:S(2)}) %collective-permute-start.2) | collective-permute-done | bytes 1114144 | tf_op jit(solution)/shard_map/ppermute | solution.py:712
  88.6 32.8 %pipe_fwd.1 = (bf16[512,1024]{1,0:T(8,128)(2,1)}, bf16[128,1024]{1,0:T(8,128)(2,1)}) custom-call(bf16[512,1024]{1,0:T(8,128)(2,1)} %bitcast.103, bf16[1024,4096]{1,0:T(8,128)(2,1)} %bitcast.113, bf16[4096,1024]{1,0:T(8,128)(2,1)} %bitcast.116), custom_call_target="tpu_custom_call" | custom-call | flops 34359738368 | bytes 16777216 | tf_op jit(solution)/shard_map/pipe_fwd/pallas_call | solution.py:148
  140.2 11.8 %convert.12 = bf16[8032,1024]{1,0:T(8,128)(2,1)S(1)} convert(f32[8032,1024]{1,0:T(8,128)} %bitcast.93) | non-fusion elementwise | flops 8224768 | bytes 49348608 | tf_op jit(solution)/shard_map/convert.7
  155.9 8.0 %collective-permute-start.3 = (bf16[3072,1024]{1,0:T(8,128)(2,1)}, bf16[3072,1024]{1,0:T(8,128)(2,1)}, u32[]{:S(2)}, u32[]{:S(2)}) collective-permute-start(bf16[3072,1024]{1,0:T(8,128)(2,1)} %slice.111), channel_id=1, source_target_pairs={{0,1},{4,5},{8,9},{12,13}} | collective-permute-start | bytes 18874376 | tf_op jit(solution)/shard_map/ppermute | solution.py:726
  163.9 12.1 %convert.13 = bf16[1,8032,1024]{2,1,0:T(8,128)(2,1)S(1)} convert(f32[1,8032,1024]{2,1,0:T(8,128)} %param.15) | non-fusion elementwise | flops 8224768 | bytes 49348608 | tf_op jit(solution)/shard_map/convert.5
  177.7 5.3 collective-permute-start.5
  192.9 5.8 sort.15
  200.9 11.5 %collective-permute-done.5 = bf16[1024,1024]{1,0:T(8,128)(2,1)S(1)} collective-permute-done((bf16[1024,1024]{1,0:T(8,128)(2,1)}, bf16[1024,1024]{1,0:T(8,128)(2,1)S(1)}, u32[]{:S(2)}, u32[]{:S(2)}) %collective-permute-start.5) | collective-permute-done | bytes 2097184 | tf_op jit(solution)/shard_map/ppermute | solution.py:719
  212.3 29.9 %collective-permute-done.4 = bf16[1024,1024]{1,0:T(8,128)(2,1)} collective-permute-done((bf16[1024,1024]{1,0:T(8,128)(2,1)}, bf16[1024,1024]{1,0:T(8,128)(2,1)}, u32[]{:S(2)}, u32[]{:S(2)}) %collective-permute-start.4) | collective-permute-done | bytes 2097184 | tf_op jit(solution)/shard_map/ppermute | solution.py:719
  242.3 8.8 %fusion.4.e_ref.refs_1_.refs_2_ = bf16[3072,1024]{1,0:T(8,128)(2,1)} fusion(bf16[3072,1024]{1,0:T(8,128)(2,1)} %collective-permute-done.3, bf16[8032,1024]{1,0:T(8,128)(2,1)} %copy-done, bf16[1024,1024]{1,0:T(8,128)(2,1)S(1)} %collective-permute-done.5, bf16[1024,1024]{1,0:T(8,128)(2,1)} %collective-permute-done.4, pred[]{:T(512)S(6)} %eq.4), kind=kLoop, calls=%fused_computation.9 | loop fusion | flops 28311552 | bytes 23068672 | tf_op jit(solution)/shard_map/add | solution.py:727
  252.5 23.8 %head_fwd.3 = (f32[2048,3072]{1,0:T(8,128)}, f32[2048,128]{1,0:T(8,128)}, f32[2048,128]{1,0:T(8,128)}) custom-call(s32[2]{0:T(128)} %pad_add_fusion.1.meta.refs_0_, bf16[2048,1024]{1,0:T(8,128)(2,1)} %all-gather.10.cloned.1.call-done.n_ref.refs_1_, bf16[3072,1024]{1,0:T(8,128)(2,1)} %fusion.4.e_ref.refs_1_.refs_2_), custom_call_target="tpu_custom_call" | custom-call | flops 12884901888 | bytes 25165824 | tf_op jit(solution)/shard_map/head_fwd/pallas_call | solution.py:456
  276.3 23.8 %head_fwd.2 = (f32[2048,3072]{1,0:T(8,128)}, f32[2048,128]{1,0:T(8,128)}, f32[2048,128]{1,0:T(8,128)}) custom-call(s32[2]{0:T(128)} %pad_add_fusion.1.meta.refs_0_, bf16[2048,1024]{1,0:T(8,128)(2,1)} %all-gather.8.cloned.1.call-done.n_ref.refs_0_, bf16[3072,1024]{1,0:T(8,128)(2,1)} %fusion.4.e_ref.refs_1_.refs_2_), custom_call_target="tpu_custom_call" | custom-call | flops 12884901888 | bytes 25165824 | tf_op jit(solution)/shard_map/head_fwd/pallas_call | solution.py:456
  305.1 17.8 %all-gather.1 = f32[16,1,8448]{2,1,0:T(1,128)S(1)} all-gather(f32[1,1,8448]{2,1,0:T(1,128)S(1)} %reshape.318), channel_id=2, replica_groups=mesh['dp'=4,'pp'=4] {'dp','pp'}, dimensions={0}, use_global_device_ids=true | all-gather | bytes 574464 | tf_op jit(solution)/shard_map/all_gather | solution.py:762
  326.5 24.6 %head_bwd.1 = f32[2048,1024]{1,0:T(8,128)} custom-call(s32[2]{0:T(128)} %pad_add_fusion.1.meta.refs_0_, bf16[3072,1024]{1,0:T(8,128)(2,1)} %fusion.4.e_ref.refs_1_.refs_2_, f32[2048,3072]{1,0:T(8,128)} %get-tuple-element.46.refs_2_.refs_4_, f32[2048,2]{1,0:T(8,128)} %copy.42.refs_3_.refs_5_, s32[2048,2]{1,0:T(8,128)} %copy.43.refs_4_.refs_6_), custom_call_target="tpu_custom_call" | custom-call | flops 12884901888 | bytes 25165824 | tf_op jit(solution)/shard_map/head_bwd/pallas_call | solution.py:503
  351.1 127.3 %head_reduce.1 = (f32[3072,1024]{1,0:T(8,128)}, f32[128,1024]{1,0:T(8,128)}, f32[128,1024]{1,0:T(8,128)}) custom-call(bf16[2048,1024]{1,0:T(8,128)(2,1)} %all-gather.8.cloned.1.call-done.n_ref.refs_0_, bf16[2048,1024]{1,0:T(8,128)(2,1)} %all-gather.10.cloned.1.call-done.n_ref.refs_1_, bf16[3072,1024]{1,0:T(8,128)(2,1)} %fusion.4.e_ref.refs_1_.refs_2_, ...), custom_call_target="tpu_custom_call" | custom-call | flops 38654705664 | bytes 75497472 | tf_op jit(solution)/shard_map/head_reduce/pallas_call | solution.py:642
  481.9 12.5 %multiply_reduce_fusion = (f32[128]{0:T(128)S(1)}, f32[128,1024]{1,0:T(8,128)S(1)}) fusion(f32[128,1024]{1,0:T(8,128)S(1)} %copy-done.6, f32[1024]{0:T(1024)S(1)} %copy-done.22, bf16[1024,4096]{1,0:T(8,128)(2,1)} %param.23, f32[128,4096]{1,0:T(8,128)} %copy-done.14, bf16[128,1024]{1,0:T(8,128)(2,1)S(1)} %fusion.56, bf16[4096,1024]{1,0:T(8,128)(2,1)} %param.24), kind=kOutput, calls=%fused_computation.108 | convolution fusion | flops 2159149056 | bytes 20189696 | tf_op jit(solution)/shard_map/transpose(jvp())/dot_general | solution.py:40
  510.2 95.1 %pipe_bwd.1 = (bf16[4,4,128,1024]{3,2,1,0:T(8,128)(2,1)}, bf16[4,128,1024]{2,1,0:T(8,128)(2,1)}) custom-call(bf16[128,1024]{1,0:T(8,128)(2,1)} %fusion.74.refs_0_, bf16[512,1024]{1,0:T(8,128)(2,1)} %get-tuple-element.49.refs_1_, bf16[1024,4096]{1,0:T(8,128)(2,1)} %bitcast.114, bf16[4096,1024]{1,0:T(8,128)(2,1)} %bitcast.117), custom_call_target="tpu_custom_call" | custom-call | flops 51539607552 | bytes 16777216 | tf_op jit(solution)/shard_map/pipe_bwd/pallas_call | solution.py:294
  620.6 6.6 copy.45.n_ref
  627.1 91.9 %stage_wgrad.1 = (f32[1024,4096]{1,0:T(8,128)}, f32[4096,1024]{1,0:T(8,128)}) custom-call(bf16[2048,1024]{1,0:T(8,128)(2,1)} %copy.45.n_ref, bf16[1024,2048]{1,0:T(8,128)(2,1)} %fusion.111.nt_ref, bf16[2048,1024]{1,0:T(8,128)(2,1)} %bitcast.122, bf16[1024,4096]{1,0:T(8,128)(2,1)} %bitcast.115, bf16[4096,1024]{1,0:T(8,128)(2,1)} %bitcast.118), custom_call_target="tpu_custom_call" | custom-call | flops 68719476736 | bytes 50331648 | tf_op jit(solution)/shard_map/stage_wgrad/pallas_call | solution.py:337
  719.1 5.1 collective-permute-done.11.refs_6_
  726.1 43.3 %scatter_rows.1 = f32[8032,1024]{1,0:T(8,128)} custom-call(s32[34]{0:T(128)} %pad_add_fusion.2.refs_0_, s32[4096]{0:T(1024)} %get-tuple-element.53.refs_1_, s32[4096]{0:T(1024)} %get-tuple-element.54.refs_2_, f32[3072,1024]{1,0:T(8,128)} %get-tuple-element.59.refs_3_, f32[3072,1024]{1,0:T(8,128)} %collective-permute-done.9.refs_4_, ...), custom_call_target="tpu_custom_call" | custom-call | tf_op jit(solution)/shard_map/scatter_rows/pallas_call | solution.py:399
  (227 shorter events, 110.5 us)
Async XLA Ops:
  7.2 243.9 %all-gather.10.cloned.1.call-start = ((), (), s32[]{:S(2)}) async-start(), calls=%async_computation.1 | async-start | bytes 4456448 | tf_op jit(solution)/shard_map/all_gather | solution.py:749
  42.7 13.0 %copy-start.34 = (bf16[1024]{0:T(1024)(128)(2,1)S(1)}, bf16[1024]{0:T(1024)(128)(2,1)}, u32[]{:S(2)}) copy-start(bf16[1024]{0:T(1024)(128)(2,1)} %param.19) | copy-start | bytes 6148
  42.7 13.6 %copy-start.35 = (bf16[1024]{0:T(1024)(128)(2,1)S(1)}, bf16[1024]{0:T(1024)(128)(2,1)}, u32[]{:S(2)}) copy-start(bf16[1024]{0:T(1024)(128)(2,1)} %param.20) | copy-start | bytes 6148
  42.7 14.2 %copy-start.36 = (bf16[1024]{0:T(1024)(128)(2,1)S(1)}, bf16[1024]{0:T(1024)(128)(2,1)}, u32[]{:S(2)}) copy-start(bf16[1024]{0:T(1024)(128)(2,1)} %param.21) | copy-start | bytes 6148
  45.1 18.6 %collective-permute-start = (bf16[544,1024]{1,0:T(8,128)(2,1)}, bf16[544,1024]{1,0:T(8,128)(2,1)S(1)}, u32[]{:S(2)}, u32[]{:S(2)}) collective-permute-start(bf16[544,1024]{1,0:T(8,128)(2,1)} %get-tuple-element.79), channel_id=1, source_target_pairs={{0,4},{4,8},{8,12},{12,0}} | collective-permute-start | bytes 3342344 | tf_op jit(solution)/shard_map/ppermute | solution.py:712
  48.4 27.2 %collective-permute-start.2 = (bf16[544,1024]{1,0:T(8,128)(2,1)S(1)}, bf16[544,1024]{1,0:T(8,128)(2,1)}, u32[]{:S(2)}, u32[]{:S(2)}) collective-permute-start(bf16[544,1024]{1,0:T(8,128)(2,1)S(1)} %get-tuple-element.80), channel_id=1, source_target_pairs={{0,12},{4,0},{8,4},{12,8}} | collective-permute-start | bytes 3342344 | tf_op jit(solution)/shard_map/ppermute | solution.py:712
  51.8 23.8 %collective-permute-start.1 = (bf16[544,1024]{1,0:T(8,128)(2,1)S(1)}, bf16[544,1024]{1,0:T(8,128)(2,1)}, u32[]{:S(2)}, u32[]{:S(2)}) collective-permute-start(bf16[544,1024]{1,0:T(8,128)(2,1)S(1)} %get-tuple-element.81), channel_id=1, source_target_pairs={{0,8},{4,12},{8,0},{12,4}} | collective-permute-start | bytes 3342344 | tf_op jit(solution)/shard_map/ppermute | solution.py:712
  82.5 41.1 %collective-permute-start.7 = (bf16[4,34,1024]{2,1,0:T(8,128)(2,1)}, bf16[4,34,1024]{2,1,0:T(8,128)(2,1)}, u32[]{:S(2)}, u32[]{:S(2)}) collective-permute-start(bf16[4,34,1024]{2,1,0:T(8,128)(2,1)} %slice.92), channel_id=1, source_target_pairs={{0,2},{4,6},{8,10},{12,14}} | collective-permute-start | bytes 835592 | tf_op jit(solution)/shard_map/ppermute | solution.py:680
  84.5 39.1 %collective-permute-start.8 = (bf16[4,34,1024]{2,1,0:T(8,128)(2,1)}, bf16[4,34,1024]{2,1,0:T(8,128)(2,1)}, u32[]{:S(2)}, u32[]{:S(2)}) collective-permute-start(bf16[4,34,1024]{2,1,0:T(8,128)(2,1)} %slice.94), channel_id=1, source_target_pairs={{0,3},{4,7},{8,11},{12,15}} | collective-permute-start | bytes 835592 | tf_op jit(solution)/shard_map/ppermute | solution.py:680
  86.5 37.1 %collective-permute-start.6 = (bf16[4,34,1024]{2,1,0:T(8,128)(2,1)}, bf16[4,34,1024]{2,1,0:T(8,128)(2,1)}, u32[]{:S(2)}, u32[]{:S(2)}) collective-permute-start(bf16[4,34,1024]{2,1,0:T(8,128)(2,1)} %slice.90), channel_id=1, source_target_pairs={{0,1},{4,5},{8,9},{12,13}} | collective-permute-start | bytes 835592 | tf_op jit(solution)/shard_map/ppermute | solution.py:680
  139.4 136.9 %all-gather.8.cloned.1.call-start = ((), (), s32[]{:S(2)}) async-start(), calls=%async_computation | async-start | bytes 4456448 | tf_op jit(solution)/shard_map/all_gather | solution.py:748
  140.2 360.2 %all-gather.12.cloned.1.call-start = ((), (), s32[]{:S(2)}) async-start(), calls=%async_computation.2 | async-start | bytes 5242880 | tf_op jit(solution)/shard_map/all_gather | solution.py:751
  152.0 23.9 %copy-start = (bf16[8032,1024]{1,0:T(8,128)(2,1)}, bf16[8032,1024]{1,0:T(8,128)(2,1)S(1)}, u32[]{:S(2)}) copy-start(bf16[8032,1024]{1,0:T(8,128)(2,1)S(1)} %convert.12) | copy-start | bytes 49348612
  155.9 86.4 %collective-permute-start.3 = (bf16[3072,1024]{1,0:T(8,128)(2,1)}, bf16[3072,1024]{1,0:T(8,128)(2,1)}, u32[]{:S(2)}, u32[]{:S(2)}) collective-permute-start(bf16[3072,1024]{1,0:T(8,128)(2,1)} %slice.111), channel_id=1, source_target_pairs={{0,1},{4,5},{8,9},{12,13}} | collective-permute-start | bytes 18874376 | tf_op jit(solution)/shard_map/ppermute | solution.py:726
  177.7 13.4 %copy-start.17 = (s32[64,34]{1,0:T(8,128)S(1)}, s32[64,34]{1,0:T(8,128)}, u32[]{:S(2)}) copy-start(s32[64,34]{1,0:T(8,128)} %copy-done.16) | copy-start | bytes 26116
  177.7 34.7 %collective-permute-start.5 = (bf16[1024,1024]{1,0:T(8,128)(2,1)}, bf16[1024,1024]{1,0:T(8,128)(2,1)S(1)}, u32[]{:S(2)}, u32[]{:S(2)}) collective-permute-start(bf16[1024,1024]{1,0:T(8,128)(2,1)} %pad.12), channel_id=1, source_target_pairs={{0,3},{4,7},{8,11},{12,15}} | collective-permute-start | bytes 6291464 | tf_op jit(solution)/shard_map/ppermute | solution.py:719
  184.5 57.8 %collective-permute-start.4 = (bf16[1024,1024]{1,0:T(8,128)(2,1)}, bf16[1024,1024]{1,0:T(8,128)(2,1)}, u32[]{:S(2)}, u32[]{:S(2)}) collective-permute-start(bf16[1024,1024]{1,0:T(8,128)(2,1)} %slice_bitcast_fusion), channel_id=1, source_target_pairs={{0,2},{4,6},{8,10},{12,14}} | collective-permute-start | bytes 6291464 | tf_op jit(solution)/shard_map/ppermute | solution.py:719
  200.9 50.2 %copy-start.18 = (bf16[512,1024]{1,0:T(8,128)(2,1)S(1)}, bf16[512,1024]{1,0:T(8,128)(2,1)}, u32[]{:S(2)}) copy-start(bf16[512,1024]{1,0:T(8,128)(2,1)} %get-tuple-element.49.refs_1_) | copy-start | bytes 3145732
  252.4 466.6 %all-gather.14.cloned.1.call-start = ((), (), s32[]{:S(2)}) async-start(), calls=%async_computation.3 | async-start | bytes 5242880 | tf_op jit(solution)/shard_map/all_gather | solution.py:792
  481.9 12.6 %copy-start.28 = (f32[128]{0:T(128)S(1)}, f32[128]{0:T(128)}, u32[]{:S(2)}) copy-start(f32[128]{0:T(128)} %copy-done.27) | copy-start | bytes 1540
  605.4 113.7 %all-gather.16.cloned.1.call-start = ((), (), s32[]{:S(2)}) async-start(), calls=%async_computation.4 | async-start | bytes 4456448 | tf_op jit(solution)/shard_map/all_gather | solution.py:780
  605.4 120.7 %collective-permute-start.9 = (f32[3072,1024]{1,0:T(8,128)}, f32[3072,1024]{1,0:T(8,128)}, u32[]{:S(2)}, u32[]{:S(2)}) collective-permute-start(f32[3072,1024]{1,0:T(8,128)} %get-tuple-element.59.refs_3_), channel_id=1, source_target_pairs={{1,0},{5,4},{9,8},{13,12}} | collective-permute-start | bytes 37748744 | tf_op jit(solution)/shard_map/ppermute | solution.py:790
  618.0 106.3 %collective-permute-start.11 = (f32[1024,1024]{1,0:T(8,128)}, f32[1024,1024]{1,0:T(8,128)}, u32[]{:S(2)}, u32[]{:S(2)}) collective-permute-start(f32[1024,1024]{1,0:T(8,128)} %slice.106), channel_id=1, source_target_pairs={{3,0},{7,4},{11,8},{15,12}} | collective-permute-start | bytes 12582920 | tf_op jit(solution)/shard_map/ppermute | solution.py:790
  619.3 106.9 %collective-permute-start.10 = (f32[1024,1024]{1,0:T(8,128)}, f32[1024,1024]{1,0:T(8,128)}, u32[]{:S(2)}, u32[]{:S(2)}) collective-permute-start(f32[1024,1024]{1,0:T(8,128)} %slice.106), channel_id=1, source_target_pairs={{2,0},{6,4},{10,8},{14,12}} | collective-permute-start | bytes 12582920 | tf_op jit(solution)/shard_map/ppermute | solution.py:790
  (43 other events, 180.2 us)
Sparse Core Ops, SparseCore 0:
  139.5 43.8 all-gather.9
  185.6 38.3 all-gather.7
  252.6 54.5 all-gather.11
  605.5 49.8 all-gather.13
  657.5 48.3 all-gather.15

commit v4 on v3

--- a/solution.py
+++ b/solution.py
@@ -21,8 +21,24 @@
     return norm_only(acts).astype(BF)
 
 
+def plain_gain_norm(acts, gain):
+    return (norm_only(acts) * gain.astype(F32)).astype(BF)
+
+
+@jax.custom_vjp
 def gain_norm(acts, gain):
-    return (norm_only(acts) * gain.astype(F32)).astype(BF)
+    return plain_gain_norm(acts, gain)
+
+
+def gain_norm_fwd(acts, gain):
+    return plain_gain_norm(acts, gain), (acts, gain)
+
+
+def gain_norm_bwd(saved, grad):
+    return jax.vjp(plain_gain_norm, *saved)[1](lax.optimization_barrier(grad))
+
+
+gain_norm.defvjp(gain_norm_fwd, gain_norm_bwd)
 
 
 def gelu_bf16(pre_act):
@@ -313,7 +329,15 @@
     )(d_top, acts, w_in, w_out)
 
 
-def wgrad_kernel(n_ref, nt_ref, d_ref, wi_ref, wo_ref, gi_ref, go_ref):
+def wgrad_kernel(acts_ref, d_ref, wi_ref, wo_ref, gi_ref, go_ref, n_ref, nt_ref):
+    @pl.when(pl.program_id(0) == 0)
+    def _():
+        for b in range(n_ref.shape[0] // WG_ROWS):
+            rows = slice(b * WG_ROWS, (b + 1) * WG_ROWS)
+            normed = norm_bf16(acts_ref[rows, :])
+            n_ref[rows, :] = normed
+            nt_ref[:, rows] = normed.T
+
     gi_ref[...] = jnp.zeros_like(gi_ref)
     go_ref[...] = jnp.zeros_like(go_ref)
     for b in range(n_ref.shape[0] // WG_ROWS):
@@ -328,8 +352,8 @@
         go_ref[...] += dot(act, d_ref[rows, :], ((0,), (0,)))
 
 
-def stage_wgrad(normed, normed_t, w_in, w_out, d_out):
-    n_all, hidden = normed.shape
+def stage_wgrad(acts, w_in, w_out, d_out):
+    n_all, hidden = acts.shape
     ffn = w_in.shape[1]
     vmem = pl.BlockSpec(memory_space=pltpu.VMEM)
     cols = pl.BlockSpec((hidden, WG_STEP), lambda i: (0, i))
@@ -337,13 +361,14 @@
     return pl.pallas_call(
         wgrad_kernel,
         grid=(ffn // WG_STEP,),
-        in_specs=[vmem, vmem, vmem, cols, rows],
+        in_specs=[vmem, vmem, cols, rows],
         out_specs=[cols, rows],
+        scratch_shapes=[pltpu.VMEM((n_all, hidden), BF), pltpu.VMEM((hidden, n_all), BF)],
         out_shape=[jax.ShapeDtypeStruct((hidden, ffn), F32), jax.ShapeDtypeStruct((ffn, hidden), F32)],
         compiler_params=pltpu.CompilerParams(vmem_limit_bytes=VMEM_LIMIT),
         cost_estimate=pl.CostEstimate(flops=8 * n_all * hidden * ffn, bytes_accessed=12 * hidden * ffn, transcendentals=n_all * ffn),
         name='stage_wgrad',
-    )(normed, normed_t, d_out, w_in, w_out)
+    )(acts, d_out, w_in, w_out)
 
 
 def scatter_kernel(scale, firsts, starts_ref, rows_ref, perm_ref, *refs):
@@ -782,15 +807,13 @@
         look_ids = jnp.concatenate([tok_all[:, 0:seq_len].reshape(-1), mid_all]) - data * v_own
         look_ids = jnp.where(is_first & (look_ids >= 0) & (look_ids < v_own), look_ids, v_own)
         plan = scatter_plan(look_ids, is_first, v_own)
-        normed = norm_bf16(acts_all)
-        prepared = lax.optimization_barrier((d_hid_q, normed, normed.T, plan))
-        d_hid_q, normed, normed_t, plan = prepared
+        d_hid_q, acts_all, plan = lax.optimization_barrier((d_hid_q, acts_all, plan))
         d_out_all, d_first_all = pipe_bwd(d_hid_q, stage_in, w_in, w_out, n_stages, n_data)
         g_late, d_out_all, d_first_all = lax.optimization_barrier((g_table, d_out_all, d_first_all))
         pieces = [g_table] + [lax.ppermute(g_late[0:VTILE * SHARES[q]], 'pp', [(q, 0)]) for q in range(1, n_stages)]
         d_out_all = d_out_all.reshape(n_all, hidden)
         d_first_all = lax.all_gather(d_first_all.reshape(n_own, hidden), 'dp', axis=0, tiled=True)
-        g_in, g_out = stage_wgrad(normed, normed_t, w_in, w_out, d_out_all)
+        g_in, g_out = stage_wgrad(acts_all, w_in, w_out, d_out_all)
 
         d_first_all, g_in = lax.optimization_barrier((d_first_all, g_in))
         g_shard = scatter_rows(pieces, v_own, d_first_all, d_rows_all, plan, emb_scale)

time: 788 us -> 780 us (0.990)
  other arithmetic: 80.7 us -> 72.3 us
    optimization_barrier x2 -> x0, local copies, waits for them, and re-layouts: 7.93 us -> none  [the longest x1 6.58 us: device_body(): prepared = lax.optimization_barrier((d_hid_q, normed, normed.T, plan))]
  transfers between devices with their start and end apart: 17 -> 17, of which waited for: 7 -> 7; matrix products, arithmetic and copies ran while one was open for 13% -> 12% of each run, Pallas kernels for 42% -> 42%
where the time goes in v4:
time: 780 us; the launch traced here: 769 us
  Pallas kernels  464 us (59%)
  other arithmetic  72.3 us (9%)
  waiting for transfers between devices  72.2 us (9%)
  local copies, waits for them, and re-layouts  53.5 us (7%)
  starting transfers between devices  34.1 us (4%)
  blocking collectives  28.3 us (4%)
  matrix products  25.4 us (3%)
  between operations  19.2 us (2%)
    pallas_call x1, Pallas kernels, head_reduce(): pl.pallas_call(lambda *refs: head_reduce_kernel(weights, n_stages, n_data...  126 us
    pallas_call x1, Pallas kernels, pipe_bwd(): pl.pallas_call(lambda *refs: pipe_bwd_kernel(n_stages, n_data, *refs), in...  95.6 us
    pallas_call x1, Pallas kernels, stage_wgrad(): pl.pallas_call(wgrad_kernel, grid=(ffn // WG_STEP,), in_specs=[vmem, vmem...  94 us
    pallas_call x2, Pallas kernels, head_fwd(): pl.pallas_call(head_fwd_kernel, grid_spec=pltpu.PrefetchScalarGridSpec(nu...  47.6 us
    pallas_call x1, Pallas kernels, scatter_rows(): pl.pallas_call(lambda *refs: scatter_kernel(scale, firsts, *refs), grid_s...  43.3 us
    ppermute x2, waiting for transfers between devices, device_body(): lax.ppermute(piece(q, table), 'pp', [(0, q)])  41.7 us
    pallas_call x1, Pallas kernels, pipe_fwd(): pl.pallas_call(lambda *refs: pipe_fwd_kernel(n_stages, *refs), in_specs=[...  32.8 us
    pallas_call x1, Pallas kernels, head_bwd(): pl.pallas_call(lambda *refs: head_bwd_kernel(weight, *refs), grid_spec=pl...  24.6 us
  transfers between devices with their start and end apart: 17, of which 7 were waited for; matrix products, arithmetic and copies ran while one was open for 12% of the time, Pallas kernels for 42%

profile of v4, /device:TPU:0, one launch (start us, length us, event | category | flops | bytes accessed | tf_op | source)
XLA Modules:
  0.0 769.0 jit_solution(2663649995150345875)
XLA Ops:
  7.2 10.1 %all_gather.24 = s32[64,34]{1,0:T(8,128)S(1)} all-gather(s32[16,34]{1,0:T(8,128)} %bitcast.108), channel_id=1, replica_groups=mesh['dp'=4,'pp'=4] {'dp'}, dimensions={0}, use_global_device_ids=true | all-gather | bytes 10880 | tf_op jit(solution)/shard_map/all_gather | solution.py:728
  18.4 21.3 %gather_fusion = bf16[2176,1024]{1,0:T(8,128)(2,1)} fusion(f32[8032,1024]{1,0:T(8,128)} %bitcast.90, s32[3072]{0:T(1024)S(1)} %pad_clamp_fusion), kind=kCustom, calls=%fused_computation | custom fusion | bytes 8921600 | tf_op jit(solution)/shard_map/jit(_take)/gather | solution.py:731
  57.5 6.2 collective-permute-done
  63.7 11.9 %collective-permute-done.2 = bf16[544,1024]{1,0:T(8,128)(2,1)} collective-permute-done((bf16[544,1024]{1,0:T(8,128)(2,1)S(1)}, bf16[544,1024]{1,0:T(8,128)(2,1)}, u32[]{:S(2)}, u32[]{:S(2)}) %collective-permute-start.2) | collective-permute-done | bytes 1114144 | tf_op jit(solution)/shard_map/ppermute | solution.py:737
  88.6 32.8 %pipe_fwd.1 = (bf16[512,1024]{1,0:T(8,128)(2,1)}, bf16[128,1024]{1,0:T(8,128)(2,1)}) custom-call(bf16[512,1024]{1,0:T(8,128)(2,1)} %bitcast.101, bf16[1024,4096]{1,0:T(8,128)(2,1)} %bitcast.111, bf16[4096,1024]{1,0:T(8,128)(2,1)} %bitcast.114), custom_call_target="tpu_custom_call" | custom-call | flops 34359738368 | bytes 16777216 | tf_op jit(solution)/shard_map/pipe_fwd/pallas_call | solution.py:164
  130.7 4.8 fusion.65
  140.4 11.8 %convert.12 = bf16[8032,1024]{1,0:T(8,128)(2,1)S(1)} convert(f32[8032,1024]{1,0:T(8,128)} %bitcast.91) | non-fusion elementwise | flops 8224768 | bytes 49348608 | tf_op jit(solution)/shard_map/convert.7
  160.1 8.0 %collective-permute-start.3 = (bf16[3072,1024]{1,0:T(8,128)(2,1)}, bf16[3072,1024]{1,0:T(8,128)(2,1)}, u32[]{:S(2)}, u32[]{:S(2)}) collective-permute-start(bf16[3072,1024]{1,0:T(8,128)(2,1)} %slice.111), channel_id=1, source_target_pairs={{0,1},{4,5},{8,9},{12,13}} | collective-permute-start | bytes 18874376 | tf_op jit(solution)/shard_map/ppermute | solution.py:751
  168.1 12.4 %convert.13 = bf16[1,8032,1024]{2,1,0:T(8,128)(2,1)S(1)} convert(f32[1,8032,1024]{2,1,0:T(8,128)} %param.15) | non-fusion elementwise | flops 8224768 | bytes 49348608 | tf_op jit(solution)/shard_map/convert.5
  195.3 5.8 sort.15
  203.1 14.9 %collective-permute-done.5 = bf16[1024,1024]{1,0:T(8,128)(2,1)S(1)} collective-permute-done((bf16[1024,1024]{1,0:T(8,128)(2,1)}, bf16[1024,1024]{1,0:T(8,128)(2,1)S(1)}, u32[]{:S(2)}, u32[]{:S(2)}) %collective-permute-start.5) | collective-permute-done | bytes 2097184 | tf_op jit(solution)/shard_map/ppermute | solution.py:744
  218.0 26.9 %collective-permute-done.4 = bf16[1024,1024]{1,0:T(8,128)(2,1)} collective-permute-done((bf16[1024,1024]{1,0:T(8,128)(2,1)}, bf16[1024,1024]{1,0:T(8,128)(2,1)}, u32[]{:S(2)}, u32[]{:S(2)}) %collective-permute-start.4) | collective-permute-done | bytes 2097184 | tf_op jit(solution)/shard_map/ppermute | solution.py:744
  244.8 8.8 %fusion.2.e_ref.refs_1_.refs_2_ = bf16[3072,1024]{1,0:T(8,128)(2,1)} fusion(bf16[3072,1024]{1,0:T(8,128)(2,1)} %collective-permute-done.3, bf16[8032,1024]{1,0:T(8,128)(2,1)} %copy-done, bf16[1024,1024]{1,0:T(8,128)(2,1)S(1)} %collective-permute-done.5, bf16[1024,1024]{1,0:T(8,128)(2,1)} %collective-permute-done.4, pred[]{:T(512)S(6)} %eq.4), kind=kLoop, calls=%fused_computation.5 | loop fusion | flops 28311552 | bytes 23068672 | tf_op jit(solution)/shard_map/add | solution.py:752
  253.7 23.8 %head_fwd.3 = (f32[2048,3072]{1,0:T(8,128)}, f32[2048,128]{1,0:T(8,128)}, f32[2048,128]{1,0:T(8,128)}) custom-call(s32[2]{0:T(128)} %pad_add_fusion.1.meta.refs_0_, bf16[2048,1024]{1,0:T(8,128)(2,1)} %all-gather.10.cloned.1.call-done.n_ref.refs_1_, bf16[3072,1024]{1,0:T(8,128)(2,1)} %fusion.2.e_ref.refs_1_.refs_2_), custom_call_target="tpu_custom_call" | custom-call | flops 12884901888 | bytes 25165824 | tf_op jit(solution)/shard_map/head_fwd/pallas_call | solution.py:481
  277.5 23.8 %head_fwd.2 = (f32[2048,3072]{1,0:T(8,128)}, f32[2048,128]{1,0:T(8,128)}, f32[2048,128]{1,0:T(8,128)}) custom-call(s32[2]{0:T(128)} %pad_add_fusion.1.meta.refs_0_, bf16[2048,1024]{1,0:T(8,128)(2,1)} %all-gather.8.cloned.1.call-done.n_ref.refs_0_, bf16[3072,1024]{1,0:T(8,128)(2,1)} %fusion.2.e_ref.refs_1_.refs_2_), custom_call_target="tpu_custom_call" | custom-call | flops 12884901888 | bytes 25165824 | tf_op jit(solution)/shard_map/head_fwd/pallas_call | solution.py:481
  306.3 18.2 %all-gather.1 = f32[16,1,8448]{2,1,0:T(1,128)S(1)} all-gather(f32[1,1,8448]{2,1,0:T(1,128)S(1)} %reshape.310), channel_id=2, replica_groups=mesh['dp'=4,'pp'=4] {'dp','pp'}, dimensions={0}, use_global_device_ids=true | all-gather | bytes 574464 | tf_op jit(solution)/shard_map/all_gather | solution.py:787
  328.2 24.6 %head_bwd.1 = f32[2048,1024]{1,0:T(8,128)} custom-call(s32[2]{0:T(128)} %pad_add_fusion.1.meta.refs_0_, bf16[3072,1024]{1,0:T(8,128)(2,1)} %fusion.2.e_ref.refs_1_.refs_2_, f32[2048,3072]{1,0:T(8,128)} %get-tuple-element.45.refs_2_.refs_4_, f32[2048,2]{1,0:T(8,128)} %copy.36.refs_3_.refs_5_, s32[2048,2]{1,0:T(8,128)} %copy.37.refs_4_.refs_6_), custom_call_target="tpu_custom_call" | custom-call | flops 12884901888 | bytes 25165824 | tf_op jit(solution)/shard_map/head_bwd/pallas_call | solution.py:528
  352.8 125.9 %head_reduce.1 = (f32[3072,1024]{1,0:T(8,128)}, f32[128,1024]{1,0:T(8,128)}, f32[128,1024]{1,0:T(8,128)}) custom-call(bf16[2048,1024]{1,0:T(8,128)(2,1)} %all-gather.8.cloned.1.call-done.n_ref.refs_0_, bf16[2048,1024]{1,0:T(8,128)(2,1)} %all-gather.10.cloned.1.call-done.n_ref.refs_1_, bf16[3072,1024]{1,0:T(8,128)(2,1)} %fusion.2.e_ref.refs_1_.refs_2_, ...), custom_call_target="tpu_custom_call" | custom-call | flops 38654705664 | bytes 75497472 | tf_op jit(solution)/shard_map/head_reduce/pallas_call | solution.py:667
  483.0 11.9 %fusion.28 = bf16[128,1024]{1,0:T(8,128)(2,1)S(1)} fusion(bf16[1024,4096]{1,0:T(8,128)(2,1)} %param.23, f32[128,4096]{1,0:T(8,128)S(1)} %copy-done.12, bf16[128,1024]{1,0:T(8,128)(2,1)S(1)} %fusion.48, bf16[4096,1024]{1,0:T(8,128)(2,1)} %param.24), kind=kOutput, calls=%fused_computation.40 | convolution fusion | flops 2158624768 | bytes 19398656 | tf_op jit(solution)/shard_map/transpose(jvp())/dot_general | solution.py:56
  501.1 95.6 %pipe_bwd.1 = (bf16[4,4,128,1024]{3,2,1,0:T(8,128)(2,1)}, bf16[4,128,1024]{2,1,0:T(8,128)(2,1)}) custom-call(bf16[128,1024]{1,0:T(8,128)(2,1)} %fusion.66.refs_0_, bf16[512,1024]{1,0:T(8,128)(2,1)} %get-tuple-element.48.refs_1_, bf16[1024,4096]{1,0:T(8,128)(2,1)} %bitcast.112, bf16[4096,1024]{1,0:T(8,128)(2,1)} %bitcast.115), custom_call_target="tpu_custom_call" | custom-call | flops 51539607552 | bytes 16777216 | tf_op jit(solution)/shard_map/pipe_bwd/pallas_call | solution.py:310
  604.8 4.8 slice.106
  612.2 94.0 %stage_wgrad.1 = (f32[1024,4096]{1,0:T(8,128)}, f32[4096,1024]{1,0:T(8,128)}) custom-call(bf16[2048,1024]{1,0:T(8,128)(2,1)} %all-gather.12.cloned.1.call-done.acts_ref, bf16[2048,1024]{1,0:T(8,128)(2,1)} %bitcast.120, bf16[1024,4096]{1,0:T(8,128)(2,1)} %bitcast.113, bf16[4096,1024]{1,0:T(8,128)(2,1)} %bitcast.116), custom_call_target="tpu_custom_call" | custom-call | flops 68719476736 | bytes 50331648 | tf_op jit(solution)/shard_map/stage_wgrad/pallas_call | solution.py:361
  706.2 9.7 %collective-permute-done.11.refs_6_ = f32[1024,1024]{1,0:T(8,128)} collective-permute-done((f32[1024,1024]{1,0:T(8,128)}, f32[1024,1024]{1,0:T(8,128)}, u32[]{:S(2)}, u32[]{:S(2)}) %collective-permute-start.11) | collective-permute-done | bytes 4194336 | tf_op jit(solution)/shard_map/ppermute | solution.py:813
  717.8 43.3 %scatter_rows.1 = f32[8032,1024]{1,0:T(8,128)} custom-call(s32[34]{0:T(128)} %pad_add_fusion.2.refs_0_, s32[4096]{0:T(1024)} %get-tuple-element.52.refs_1_, s32[4096]{0:T(1024)} %get-tuple-element.53.refs_2_, f32[3072,1024]{1,0:T(8,128)} %get-tuple-element.58.refs_3_, f32[3072,1024]{1,0:T(8,128)} %collective-permute-done.9.refs_4_, ...), custom_call_target="tpu_custom_call" | custom-call | tf_op jit(solution)/shard_map/scatter_rows/pallas_call | solution.py:424
  (220 shorter events, 98.5 us)
Async XLA Ops:
  7.2 246.5 %all-gather.10.cloned.1.call-start = ((), (), s32[]{:S(2)}) async-start(), calls=%async_computation.1 | async-start | bytes 4456448 | tf_op jit(solution)/shard_map/all_gather | solution.py:774
  42.7 12.4 %copy-start.29 = (bf16[1024]{0:T(1024)(128)(2,1)S(1)}, bf16[1024]{0:T(1024)(128)(2,1)}, u32[]{:S(2)}) copy-start(bf16[1024]{0:T(1024)(128)(2,1)} %param.18) | copy-start | bytes 6148
  42.7 13.0 %copy-start.30 = (bf16[1024]{0:T(1024)(128)(2,1)S(1)}, bf16[1024]{0:T(1024)(128)(2,1)}, u32[]{:S(2)}) copy-start(bf16[1024]{0:T(1024)(128)(2,1)} %param.19) | copy-start | bytes 6148
  42.7 13.6 %copy-start.31 = (bf16[1024]{0:T(1024)(128)(2,1)S(1)}, bf16[1024]{0:T(1024)(128)(2,1)}, u32[]{:S(2)}) copy-start(bf16[1024]{0:T(1024)(128)(2,1)} %param.20) | copy-start | bytes 6148
  42.7 14.2 %copy-start.32 = (bf16[1024]{0:T(1024)(128)(2,1)S(1)}, bf16[1024]{0:T(1024)(128)(2,1)}, u32[]{:S(2)}) copy-start(bf16[1024]{0:T(1024)(128)(2,1)} %param.21) | copy-start | bytes 6148
  45.1 18.6 %collective-permute-start = (bf16[544,1024]{1,0:T(8,128)(2,1)}, bf16[544,1024]{1,0:T(8,128)(2,1)S(1)}, u32[]{:S(2)}, u32[]{:S(2)}) collective-permute-start(bf16[544,1024]{1,0:T(8,128)(2,1)} %get-tuple-element.76), channel_id=1, source_target_pairs={{0,4},{4,8},{8,12},{12,0}} | collective-permute-start | bytes 3342344 | tf_op jit(solution)/shard_map/ppermute | solution.py:737
  48.4 27.2 %collective-permute-start.2 = (bf16[544,1024]{1,0:T(8,128)(2,1)S(1)}, bf16[544,1024]{1,0:T(8,128)(2,1)}, u32[]{:S(2)}, u32[]{:S(2)}) collective-permute-start(bf16[544,1024]{1,0:T(8,128)(2,1)S(1)} %get-tuple-element.77), channel_id=1, source_target_pairs={{0,12},{4,0},{8,4},{12,8}} | collective-permute-start | bytes 3342344 | tf_op jit(solution)/shard_map/ppermute | solution.py:737
  51.9 23.8 %collective-permute-start.1 = (bf16[544,1024]{1,0:T(8,128)(2,1)S(1)}, bf16[544,1024]{1,0:T(8,128)(2,1)}, u32[]{:S(2)}, u32[]{:S(2)}) collective-permute-start(bf16[544,1024]{1,0:T(8,128)(2,1)S(1)} %get-tuple-element.78), channel_id=1, source_target_pairs={{0,8},{4,12},{8,0},{12,4}} | collective-permute-start | bytes 3342344 | tf_op jit(solution)/shard_map/ppermute | solution.py:737
  82.5 41.1 %collective-permute-start.7 = (bf16[4,34,1024]{2,1,0:T(8,128)(2,1)}, bf16[4,34,1024]{2,1,0:T(8,128)(2,1)}, u32[]{:S(2)}, u32[]{:S(2)}) collective-permute-start(bf16[4,34,1024]{2,1,0:T(8,128)(2,1)} %slice.92), channel_id=1, source_target_pairs={{0,2},{4,6},{8,10},{12,14}} | collective-permute-start | bytes 835592 | tf_op jit(solution)/shard_map/ppermute | solution.py:705
  84.6 39.1 %collective-permute-start.8 = (bf16[4,34,1024]{2,1,0:T(8,128)(2,1)}, bf16[4,34,1024]{2,1,0:T(8,128)(2,1)}, u32[]{:S(2)}, u32[]{:S(2)}) collective-permute-start(bf16[4,34,1024]{2,1,0:T(8,128)(2,1)} %slice.94), channel_id=1, source_target_pairs={{0,3},{4,7},{8,11},{12,15}} | collective-permute-start | bytes 835592 | tf_op jit(solution)/shard_map/ppermute | solution.py:705
  86.6 37.1 %collective-permute-start.6 = (bf16[4,34,1024]{2,1,0:T(8,128)(2,1)}, bf16[4,34,1024]{2,1,0:T(8,128)(2,1)}, u32[]{:S(2)}, u32[]{:S(2)}) collective-permute-start(bf16[4,34,1024]{2,1,0:T(8,128)(2,1)} %slice.90), channel_id=1, source_target_pairs={{0,1},{4,5},{8,9},{12,13}} | collective-permute-start | bytes 835592 | tf_op jit(solution)/shard_map/ppermute | solution.py:705
  139.6 138.0 %all-gather.8.cloned.1.call-start = ((), (), s32[]{:S(2)}) async-start(), calls=%async_computation | async-start | bytes 4456448 | tf_op jit(solution)/shard_map/all_gather | solution.py:773
  140.3 360.8 %all-gather.12.cloned.1.call-start = ((), (), s32[]{:S(2)}) async-start(), calls=%async_computation.2 | async-start | bytes 5242880 | tf_op jit(solution)/shard_map/all_gather | solution.py:776
  160.1 84.7 %collective-permute-start.3 = (bf16[3072,1024]{1,0:T(8,128)(2,1)}, bf16[3072,1024]{1,0:T(8,128)(2,1)}, u32[]{:S(2)}, u32[]{:S(2)}) collective-permute-start(bf16[3072,1024]{1,0:T(8,128)(2,1)} %slice.111), channel_id=1, source_target_pairs={{0,1},{4,5},{8,9},{12,13}} | collective-permute-start | bytes 18874376 | tf_op jit(solution)/shard_map/ppermute | solution.py:751
  182.2 35.7 %collective-permute-start.5 = (bf16[1024,1024]{1,0:T(8,128)(2,1)}, bf16[1024,1024]{1,0:T(8,128)(2,1)S(1)}, u32[]{:S(2)}, u32[]{:S(2)}) collective-permute-start(bf16[1024,1024]{1,0:T(8,128)(2,1)} %pad.12), channel_id=1, source_target_pairs={{0,3},{4,7},{8,11},{12,15}} | collective-permute-start | bytes 6291464 | tf_op jit(solution)/shard_map/ppermute | solution.py:744
  187.1 57.7 %collective-permute-start.4 = (bf16[1024,1024]{1,0:T(8,128)(2,1)}, bf16[1024,1024]{1,0:T(8,128)(2,1)}, u32[]{:S(2)}, u32[]{:S(2)}) collective-permute-start(bf16[1024,1024]{1,0:T(8,128)(2,1)} %slice_bitcast_fusion), channel_id=1, source_target_pairs={{0,2},{4,6},{8,10},{12,14}} | collective-permute-start | bytes 6291464 | tf_op jit(solution)/shard_map/ppermute | solution.py:744
  253.6 452.5 %all-gather.14.cloned.1.call-start = ((), (), s32[]{:S(2)}) async-start(), calls=%async_computation.3 | async-start | bytes 5242880 | tf_op jit(solution)/shard_map/all_gather | solution.py:815
  483.0 11.9 %copy-start.4 = (f32[128,1024]{1,0:T(8,128)S(1)}, f32[128,1024]{1,0:T(8,128)}, u32[]{:S(2)}) copy-start(f32[128,1024]{1,0:T(8,128)} %copy-done.3) | copy-start | bytes 1572868
  483.0 12.1 %copy-start.40 = (f32[128]{0:T(128)S(1)}, f32[128]{0:T(128)}, u32[]{:S(2)}) copy-start(f32[128]{0:T(128)} %copy-done.39) | copy-start | bytes 1540
  483.0 12.1 %copy-start.24 = (f32[128]{0:T(128)S(1)}, f32[128]{0:T(128)}, u32[]{:S(2)}) copy-start(f32[128]{0:T(128)} %copy-done.23) | copy-start | bytes 1540
  596.8 109.4 %all-gather.16.cloned.1.call-start = ((), (), s32[]{:S(2)}) async-start(), calls=%async_computation.4 | async-start | bytes 4456448 | tf_op jit(solution)/shard_map/all_gather | solution.py:805
  596.8 120.9 %collective-permute-start.9 = (f32[3072,1024]{1,0:T(8,128)}, f32[3072,1024]{1,0:T(8,128)}, u32[]{:S(2)}, u32[]{:S(2)}) collective-permute-start(f32[3072,1024]{1,0:T(8,128)} %get-tuple-element.58.refs_3_), channel_id=1, source_target_pairs={{1,0},{5,4},{9,8},{13,12}} | collective-permute-start | bytes 37748744 | tf_op jit(solution)/shard_map/ppermute | solution.py:813
  609.6 106.3 %collective-permute-start.11 = (f32[1024,1024]{1,0:T(8,128)}, f32[1024,1024]{1,0:T(8,128)}, u32[]{:S(2)}, u32[]{:S(2)}) collective-permute-start(f32[1024,1024]{1,0:T(8,128)} %slice.106), channel_id=1, source_target_pairs={{3,0},{7,4},{11,8},{15,12}} | collective-permute-start | bytes 12582920 | tf_op jit(solution)/shard_map/ppermute | solution.py:813
  610.9 106.9 %collective-permute-start.10 = (f32[1024,1024]{1,0:T(8,128)}, f32[1024,1024]{1,0:T(8,128)}, u32[]{:S(2)}, u32[]{:S(2)}) collective-permute-start(f32[1024,1024]{1,0:T(8,128)} %slice.106), channel_id=1, source_target_pairs={{2,0},{6,4},{10,8},{14,12}} | collective-permute-start | bytes 12582920 | tf_op jit(solution)/shard_map/ppermute | solution.py:813
  (40 other events, 167.9 us)
Sparse Core Ops, SparseCore 0:
  139.7 43.8 all-gather.9
  185.8 38.7 all-gather.7
  253.8 54.6 all-gather.11
  596.9 49.2 all-gather.13
  648.3 48.4 all-gather.15
